TPU v7x, 32 devices: a whole 2x2x4 slice. The times are simulated.
32 devices in a mesh: ctx: 4 (over y, core), exp: 8 (over z, x).
Axes of the slice: x: 2, y: 2, z: 4, core: 2. Of those that a mesh axis runs over, the one named last changes fastest.
Arguments:
- queries: bfloat16 [512, 64, 576], P('ctx', 'exp'), may hold values from -1024 to 1024
- latents: bfloat16 [512, 576], P('ctx'), may hold values from -6.1 to 6.1
- block_starts: int32 [8], replicated, may hold values from 0 to 448, as said below
- w_uv: bfloat16 [64, 512, 128], P('exp'), may hold values from -0.25 to 0.25
- moe_tokens: bfloat16 [1024, 7168], P('exp'), may hold values from -6 to 6
- expert_ids: int32 [1024, 2], P('exp'), may hold values from 0 to 7, as said below
- gate_weights: float32 [1024, 2], P('exp'), may hold values from 0.2 to 1
- w_gate: bfloat16 [8, 7168, 512], P('exp', None, 'ctx'), may hold values from -0.0625 to 0.0625
- w_up: bfloat16 [8, 7168, 512], P('exp', None, 'ctx'), may hold values from -0.0625 to 0.0625
- w_down: bfloat16 [8, 512, 7168], P('exp', 'ctx'), may hold values from -0.25 to 0.25
Outputs:
- attended: bfloat16 [512, 64, 128], P('ctx', 'exp')
- moe_out: bfloat16 [1024, 7168], P('exp', 'ctx')
Inputs may be any that keep to these rules, and one draw needn't show every extreme that they name: Token t has position block_starts[t // 64] + t % 64; block_starts is a permutation of the multiples of 64 below 512. `expert_ids`: each row names 2 different experts. In the rows of one index of exp, one expert, the same for every index, is named by exactly 48 rows, no expert by more, and the other experts' counts differ by at most one.
All inputs are finite; a program needn't handle non-finite values.
Results may differ from a plain program's by a relative error of at most 0.018.
Values may be sent and summed in bfloat16 or wider, within the bound.
No kernel may reach another device: no remote copies, remote signals or barrier semaphores. Data moves between devices by JAX's collectives and lax.ppermute only.
A program may use at most 128 MiB of HBM per device.

v0:
```python
import functools
import math

import jax
import jax.numpy as jnp
from jax import lax
from jax.experimental import pallas as pl
from jax.experimental.pallas import tpu as pltpu
from jax.sharding import PartitionSpec as P


score_scale = (0.1 * math.log(40.0) + 1.0) ** 2 / math.sqrt(192.0)
neg_fill = -1e30
SETS = 2


def swap(x, axis, offset):
    size = lax.axis_size(axis)
    return lax.ppermute(x, axis, [(i, i ^ offset) for i in range(size)])


def set_members(expert_count):
    half = expert_count // 2
    return [
        [k for k in range(expert_count) if (k % half) * SETS // half == s] for s in range(SETS)
    ]


def where_am_i():
    return jnp.stack([lax.axis_index("exp"), lax.axis_index("ctx")]).astype(jnp.int32)


def whole_spec(shape):
    return pl.BlockSpec(shape, lambda i, *_: (0,) * len(shape))


def call(kernel, grid, operands, in_specs, out_shape, out_specs, flops, scalars, vmem=16 << 20, scratch=()):
    scalars = scalars if isinstance(scalars, tuple) else (scalars,)
    shapes = jax.tree.leaves(out_shape)
    moved = sum(math.prod(x.shape) * x.dtype.itemsize for x in list(operands) + shapes)
    return pl.pallas_call(
        kernel,
        out_shape=out_shape,
        grid_spec=pltpu.PrefetchScalarGridSpec(
            num_scalar_prefetch=len(scalars), grid=grid, in_specs=in_specs, out_specs=out_specs,
            scratch_shapes=scratch,
        ),
        cost_estimate=pl.CostEstimate(flops=flops, bytes_accessed=moved, transcendentals=0),
        compiler_params=pltpu.CompilerParams(vmem_limit_bytes=vmem),
    )(*scalars, *operands)


def split_kernel(where_ref, *refs):
    half = len(refs) // 2
    for source, target in zip(refs[:half], refs[half:]):
        target[...] = source[...]


def split_columns(matrix, width, where):
    rows, ctx_size = matrix.shape[0], matrix.shape[1] // width
    count = ctx_size - 1
    operands = [matrix] * count
    specs = [
        pl.BlockSpec((rows, width), lambda i, w, k=k: (0, w[1] ^ k)) for k in range(1, ctx_size)
    ]
    if width % 128:
        specs = [whole_spec((rows, width))] * count
        operands = [
            lax.dynamic_slice_in_dim(matrix, (where[1] ^ k) * width, width, axis=1)
            for k in range(1, ctx_size)
        ]
    out = jax.ShapeDtypeStruct((rows, width), matrix.dtype)
    return call(
        split_kernel, (1,), operands, specs,
        [out] * count, [whole_spec((rows, width))] * count, rows * width, where,
    )


def own_columns(matrix, width, where):
    rows = matrix.shape[0]
    if width % 128:
        return lax.dynamic_slice_in_dim(matrix, where[1] * width, width, axis=1), whole_spec((rows, width))
    return matrix, pl.BlockSpec((rows, width), lambda i, w: (0, w[1]))


def dispatch_kernel(capacity, where_ref, ids_ref, tokens_ref, *out_refs):
    expert_count = len(out_refs)
    ids = ids_ref[...]
    picks, token_count = ids.shape
    experts = lax.broadcasted_iota(jnp.int32, (expert_count, token_count), 0)
    named = jnp.zeros((expert_count, token_count), jnp.float32)
    for k in range(picks):
        named = named + jnp.where(ids[k : k + 1, :] == experts, 1.0, 0.0)
    rows = lax.broadcasted_iota(jnp.int32, (token_count, token_count), 0)
    cols = lax.broadcasted_iota(jnp.int32, (token_count, token_count), 1)
    before = jnp.where(rows < cols, 1.0, 0.0).astype(jnp.bfloat16)
    rank = jnp.dot(named.astype(jnp.bfloat16), before, preferred_element_type=jnp.float32)
    slots = lax.broadcasted_iota(jnp.int32, (expert_count * capacity, token_count), 0)
    chosen = None
    for k in range(picks):
        own = jnp.where(ids[k : k + 1, :] == experts, rank, 0.0)
        place = jnp.sum(own, axis=0, keepdims=True).astype(jnp.int32)
        place = place + (ids[k : k + 1, :] ^ where_ref[0]) * capacity
        hit = jnp.where(place == slots, 1.0, 0.0)
        chosen = hit if chosen is None else chosen + hit
    rows = jnp.dot(
        chosen.astype(jnp.bfloat16), tokens_ref[...], preferred_element_type=jnp.float32
    ).astype(tokens_ref.dtype)
    for k in range(expert_count):
        out_refs[k][...] = rows[k * capacity : (k + 1) * capacity, :]


def dispatch(tokens, ids, capacity, expert_count, width, where):
    operand, spec = own_columns(tokens, width, where)
    block = (capacity, width)
    return call(
        functools.partial(dispatch_kernel, capacity), (1,),
        [ids, operand], [whole_spec(ids.shape), spec],
        [jax.ShapeDtypeStruct(block, tokens.dtype)] * expert_count,
        [whole_spec(block)] * expert_count,
        2 * expert_count * capacity * tokens.shape[0] * width, where,
    )


def pack_kernel(where_ref, *refs):
    rows = refs[0].shape[0]
    for i, source in enumerate(refs[:-1]):
        refs[-1][i * rows : (i + 1) * rows, :] = source[...]


def pack(blocks, where):
    rows, width = blocks[0].shape
    shape = (len(blocks) * rows, width)
    return call(
        pack_kernel, (1,), blocks, [whole_spec((rows, width))] * len(blocks),
        jax.ShapeDtypeStruct(shape, blocks[0].dtype), whole_spec(shape), shape[0] * width, where,
    )


def up_sum(gate_refs, up_refs, pieces):
    acc = None
    for gate_ref, up_ref, piece in zip(gate_refs, up_refs, pieces):
        weights = jnp.concatenate([gate_ref[...], up_ref[...]], axis=1)
        term = jnp.dot(piece[...], weights, preferred_element_type=jnp.float32)
        acc = term if acc is None else acc + term
    return acc


def part_kernel(where_ref, *refs):
    count = len(refs) // 3
    refs[-1][...] = up_sum(refs[:count], refs[count : 2 * count], refs[2 * count : -1])


def mlp_kernel(where_ref, *refs):
    count = len(refs) // 3
    acc = refs[-2][...] + up_sum(refs[:count], refs[count : 2 * count], refs[2 * count : -2])
    hidden_width = acc.shape[1] // 2
    gate_h, up_h = acc[:, :hidden_width], acc[:, hidden_width:]
    refs[-1][...] = (gate_h / (1.0 + jnp.exp(-gate_h)) * up_h).astype(refs[-1].dtype)


def mlp(pieces, offsets, gate_matrix, up_matrix, partial, where):
    rows, width = pieces[0].shape
    count, hidden_width = len(pieces), gate_matrix.shape[1]
    specs = [
        pl.BlockSpec((width, hidden_width), lambda i, w, k=k: (w[1] ^ k, 0)) for k in offsets
    ]
    operands = [gate_matrix] * count + [up_matrix] * count + list(pieces)
    specs = specs + specs + [whole_spec((rows, width))] * count
    if partial is None:
        kernel, out = part_kernel, jax.ShapeDtypeStruct((rows, 2 * hidden_width), jnp.float32)
    else:
        kernel, out = mlp_kernel, jax.ShapeDtypeStruct((rows, hidden_width), pieces[0].dtype)
        operands.append(partial)
        specs.append(whole_spec(partial.shape))
    return call(
        kernel, (1,), operands, specs, out, whole_spec(out.shape),
        4 * count * rows * width * hidden_width, where, vmem=24 << 20,
    )


def tiles(width):
    step = 256 if width % 256 == 0 else width
    return [slice(at, at + step) for at in range(0, width, step)]


def down_kernel(where_ref, hidden_ref, *refs):
    ctx_size = hidden_ref.shape[0]
    parts, out_refs = refs[:ctx_size], refs[ctx_size:]
    rows, width = out_refs[0].shape
    hidden = jnp.concatenate([hidden_ref[where_ref[1] ^ j] for j in range(ctx_size)], axis=1)
    for tile in tiles(width):
        matrix = jnp.concatenate([part[:, tile] for part in parts], axis=0)
        out = jnp.dot(hidden, matrix, preferred_element_type=jnp.float32)
        out = out.astype(out_refs[0].dtype)
        for i, target in enumerate(out_refs):
            target[:, tile] = out[i * rows : (i + 1) * rows, :]


def down(hidden, own, others, block_count, where):
    width = others[0].shape[1]
    operand, spec = own_columns(own, width, where)
    block = (hidden.shape[1] // block_count, width)
    return call(
        down_kernel, (1,), [hidden, operand, *others],
        [whole_spec(hidden.shape), spec] + [whole_spec(others[0].shape)] * len(others),
        [jax.ShapeDtypeStruct(block, hidden.dtype)] * block_count,
        [whole_spec(block)] * block_count,
        2 * math.prod(hidden.shape) * width, where,
    )


def combine_kernel(where_ref, ids_ref, gates_ref, *refs):
    row_refs, out_ref = refs[:-1], refs[-1]
    expert_count, capacity = len(row_refs), row_refs[0].shape[0]
    picks, token_count = ids_ref.shape
    columns = jnp.concatenate(
        [ids_ref[...].astype(jnp.float32), gates_ref[...]]
        + [jnp.zeros((-2 * picks % 8, token_count), jnp.float32)],
        axis=0,
    ).T
    ids, gates = columns[:, :picks].astype(jnp.int32), columns[:, picks : 2 * picks]
    experts = lax.broadcasted_iota(jnp.int32, (token_count, expert_count), 1)
    named = jnp.zeros((token_count, expert_count), jnp.float32)
    for k in range(picks):
        named = named + jnp.where(ids[:, k : k + 1] == experts, 1.0, 0.0)
    rows = lax.broadcasted_iota(jnp.int32, (token_count, token_count), 0)
    cols = lax.broadcasted_iota(jnp.int32, (token_count, token_count), 1)
    before = jnp.where(cols < rows, 1.0, 0.0).astype(jnp.bfloat16)
    rank = jnp.dot(before, named.astype(jnp.bfloat16), preferred_element_type=jnp.float32)
    slots = lax.broadcasted_iota(jnp.int32, (token_count, expert_count * capacity), 1)
    hits = []
    for k in range(picks):
        own = jnp.where(ids[:, k : k + 1] == experts, rank, 0.0)
        place = jnp.sum(own, axis=1, keepdims=True).astype(jnp.int32)
        place = place + (ids[:, k : k + 1] ^ where_ref[0]) * capacity
        hits.append(jnp.where(place == slots, 1.0, 0.0).astype(jnp.bfloat16))
    hits = jnp.concatenate(hits, axis=0)
    for tile in tiles(out_ref.shape[1]):
        arrived = jnp.concatenate([ref[:, tile] for ref in row_refs], axis=0)
        chosen = jnp.dot(hits, arrived, preferred_element_type=jnp.float32)
        total = None
        for k in range(picks):
            term = chosen[k * token_count : (k + 1) * token_count, :] * gates[:, k : k + 1]
            total = term if total is None else total + term
        out_ref[:, tile] = total.astype(out_ref.dtype)


def combine(row_blocks, ids, gates, where):
    capacity, width = row_blocks[0].shape
    picks, token_count = ids.shape
    expert_count = len(row_blocks)
    out = jax.ShapeDtypeStruct((token_count, width), row_blocks[0].dtype)
    return call(
        combine_kernel, (1,), [ids, gates, *row_blocks],
        [whole_spec(ids.shape), whole_spec(gates.shape)]
        + [whole_spec((capacity, width))] * expert_count,
        out, whole_spec(out.shape),
        2 * picks * expert_count * capacity * token_count * width, where,
    )


def block_positions(starts_ref, owner, count, axis):
    shape = (count, 1) if axis == 0 else (1, count)
    index = lax.broadcasted_iota(jnp.int32, shape, axis)
    half = count // 2
    first, second = starts_ref[2 * owner], starts_ref[2 * owner + 1]
    return jnp.where(index < half, first + index, second + index - half)


def attention_kernel(where_ref, starts_ref, queries_ref, uv_ref, *refs):
    keys, out_ref, flipped, joined, late = refs[:-4], refs[-4], refs[-3], refs[-2], refs[-1]
    token_count = queries_ref.shape[2]
    lat_width = uv_ref.shape[1]
    query_positions = block_positions(starts_ref, where_ref[1], token_count, 1)
    for j, block in enumerate(keys):
        at = slice(j * token_count, (j + 1) * token_count)
        flipped[:, at] = block[...]
        joined[at, :] = block[...].T
        key_positions = block_positions(starts_ref, where_ref[1] ^ j, token_count, 0)
        late[at, :] = jnp.where(key_positions <= query_positions, 0.0, neg_fill)

    @pl.loop(0, queries_ref.shape[0])
    def _(head):
        scores = jnp.dot(joined[...], queries_ref[head], preferred_element_type=jnp.float32)
        hidden = late[...] < 0.0
        masked = jnp.where(hidden, neg_fill, scores * score_scale)
        top_score = jnp.max(masked, axis=0, keepdims=True)
        weights = jnp.where(hidden, 0.0, jnp.exp(masked - top_score))
        totals = jnp.sum(weights, axis=0, keepdims=True)
        blended = jnp.dot(
            flipped[:lat_width, :], weights.astype(jnp.bfloat16), preferred_element_type=jnp.float32
        )
        latent_out = (blended / totals).astype(jnp.bfloat16)
        out_ref[head] = lax.dot_general(
            latent_out, uv_ref[head], (((0,), (0,)), ((), ())), preferred_element_type=jnp.float32
        ).astype(out_ref.dtype)


def attention(queries, keys, block_starts, w_uv, where):
    head_count, entry_width, token_count = queries.shape
    key_count = len(keys) * token_count
    shape = (head_count, token_count, w_uv.shape[2])
    return call(
        attention_kernel, (1,), [queries, w_uv, *keys],
        [whole_spec(queries.shape), whole_spec(w_uv.shape)]
        + [whole_spec((entry_width, token_count))] * len(keys),
        jax.ShapeDtypeStruct(shape, queries.dtype), whole_spec(shape),
        4 * head_count * key_count * token_count * entry_width, (where, block_starts),
        vmem=24 << 20,
        scratch=[
            pltpu.VMEM((entry_width, key_count), queries.dtype),
            pltpu.VMEM((key_count, entry_width), queries.dtype),
            pltpu.VMEM((key_count, token_count), jnp.float32),
        ],
    )


def layer(
    queries, latents, block_starts, w_uv, moe_tokens, expert_ids, gate_weights, w_gate, w_up, w_down
):
    token_count, picks = expert_ids.shape
    expert_count = lax.axis_size("exp")
    ctx_size = lax.axis_size("ctx")
    width = moe_tokens.shape[1] // ctx_size
    capacity = 3 * token_count * picks // (2 * expert_count)
    where = where_am_i()
    evens = range(2, ctx_size, 2)

    slices = split_columns(w_down[0], width, where)
    down_parts = [swap(slices[offset - 1], "ctx", offset) for offset in range(1, ctx_size)]

    outgoing = dispatch(moe_tokens, expert_ids.T, capacity, expert_count, width, where)
    sets = set_members(expert_count)
    arrived = [swap(outgoing[k], "exp", k) if k else outgoing[0] for k in range(expert_count)]

    returned = [None] * expert_count
    for members in sets:
        pieces = [None] * ctx_size
        pieces[0] = pack([arrived[k] for k in members], where)
        for offset in evens:
            pieces[offset] = swap(pieces[0], "ctx", offset)
        for offset in range(0, ctx_size, 2):
            pieces[offset + 1] = swap(pieces[offset], "ctx", 1)
        partial = mlp(pieces[:2], [0, 1], w_gate[0], w_up[0], None, where)
        hidden = mlp(pieces[2:], range(2, ctx_size), w_gate[0], w_up[0], partial, where)
        hidden = lax.all_gather(hidden, "ctx", axis=0)
        blocks = down(hidden, w_down[0], down_parts, len(members), where)
        for k, block in zip(members, blocks):
            returned[k] = swap(block, "exp", k) if k else block

    keys = [latents.T] + [None] * (ctx_size - 1)
    for offset in evens:
        keys[offset] = swap(keys[0], "ctx", offset)
    for offset in range(0, ctx_size, 2):
        keys[offset + 1] = swap(keys[offset], "ctx", 1)
    attended = attention(jnp.transpose(queries, (1, 2, 0)), keys, block_starts, w_uv, where)
    attended = jnp.transpose(attended, (1, 0, 2))
    return attended, combine(returned, expert_ids.T, gate_weights.T, where)


def solution(mesh):
    in_specs = (
        P("ctx", "exp", None),
        P("ctx", None),
        P(),
        P("exp", None, None),
        P("exp", None),
        P("exp", None),
        P("exp", None),
        P("exp", None, "ctx"),
        P("exp", None, "ctx"),
        P("exp", "ctx", None),
    )
    out_specs = (P("ctx", "exp", None), P("exp", "ctx"))
    return jax.shard_map(layer, mesh=mesh, in_specs=in_specs, out_specs=out_specs, check_vma=False)
```

profile of v0, /device:TPU:0, one launch (start us, length us, event | category | flops | bytes accessed | tf_op | source)
XLA Modules:
  0.0 136.0 jit_solution(8396100432848841996)
XLA Ops:
  0.7 1.5 %copy-done.3 = bf16[128,7168]{1,0:T(8,128)(2,1)S(1)} copy-done((bf16[128,7168]{1,0:T(8,128)(2,1)S(1)}, bf16[128,7168]{1,0:T(8,128)(2,1)}, u32[]{:S(2)}) %copy-start.3) | copy-done | bytes 1835032
  2.9 1.2 shard_map.114
  4.1 3.1 %collective-permute-start.13 = (bf16[48,1792]{1,0:T(8,128)(2,1)S(1)}, bf16[48,1792]{1,0:T(8,128)(2,1)S(1)}, u32[]{:S(2)}, u32[]{:S(2)}) collective-permute-start(bf16[48,1792]{1,0:T(8,128)(2,1)S(1)} %get-tuple-element.30), channel_id=1, source_target_pairs={{0,2},{1,3},{2,0},{3,1},{4,6},{5,7},{6,4},{7,5},{8,10},{9,11},{10,... | collective-permute-start | bytes 516104 | tf_op jit(solution)/shard_map/ppermute | solution.py:19
  7.2 1.4 %collective-permute-start.14 = (bf16[48,1792]{1,0:T(8,128)(2,1)S(1)}, bf16[48,1792]{1,0:T(8,128)(2,1)S(1)}, u32[]{:S(2)}, u32[]{:S(2)}) collective-permute-start(bf16[48,1792]{1,0:T(8,128)(2,1)S(1)} %get-tuple-element.31), channel_id=1, source_target_pairs={{0,3},{1,2},{2,1},{3,0},{4,7},{5,6},{6,5},{7,4},{8,11},{9,10},{10,... | collective-permute-start | bytes 516104 | tf_op jit(solution)/shard_map/ppermute | solution.py:19
  8.6 3.6 %collective-permute-start.15 = (bf16[48,1792]{1,0:T(8,128)(2,1)S(1)}, bf16[48,1792]{1,0:T(8,128)(2,1)S(1)}, u32[]{:S(2)}, u32[]{:S(2)}) collective-permute-start(bf16[48,1792]{1,0:T(8,128)(2,1)S(1)} %get-tuple-element.32), channel_id=1, source_target_pairs={{0,6},{1,7},{2,4},{3,5},{4,2},{5,3},{6,0},{7,1},{8,14},{9,15},{10,... | collective-permute-start | bytes 516104 | tf_op jit(solution)/shard_map/ppermute | solution.py:19
  12.5 3.9 %collective-permute-done.14.refs_1_ = bf16[48,1792]{1,0:T(8,128)(2,1)S(1)} collective-permute-done((bf16[48,1792]{1,0:T(8,128)(2,1)S(1)}, bf16[48,1792]{1,0:T(8,128)(2,1)S(1)}, u32[]{:S(2)}, u32[]{:S(2)}) %collective-permute-start.14) | collective-permute-done | bytes 172064 | tf_op jit(solution)/shard_map/ppermute | solution.py:19
  16.4 6.2 %collective-permute-done.15.refs_2_ = bf16[48,1792]{1,0:T(8,128)(2,1)S(1)} collective-permute-done((bf16[48,1792]{1,0:T(8,128)(2,1)S(1)}, bf16[48,1792]{1,0:T(8,128)(2,1)S(1)}, u32[]{:S(2)}, u32[]{:S(2)}) %collective-permute-start.15) | collective-permute-done | bytes 172064 | tf_op jit(solution)/shard_map/ppermute | solution.py:19
  22.6 3.4 %collective-permute-done.16.refs_3_ = bf16[48,1792]{1,0:T(8,128)(2,1)S(1)} collective-permute-done((bf16[48,1792]{1,0:T(8,128)(2,1)S(1)}, bf16[48,1792]{1,0:T(8,128)(2,1)S(1)}, u32[]{:S(2)}, u32[]{:S(2)}) %collective-permute-start.16) | collective-permute-done | bytes 172064 | tf_op jit(solution)/shard_map/ppermute | solution.py:19
  26.6 1.6 %collective-permute-start.17 = (bf16[192,1792]{1,0:T(8,128)(2,1)S(1)}, bf16[192,1792]{1,0:T(8,128)(2,1)S(1)}, u32[]{:S(2)}, u32[]{:S(2)}) collective-permute-start(bf16[192,1792]{1,0:T(8,128)(2,1)S(1)} %shard_map.120.refs_4_), channel_id=1, source_target_pairs={{0,16},{8,24},{16,0},{24,8},{1,17},{9,25},{17,1},{25,9},{2,18},{10... | collective-permute-start | bytes 2064392 | tf_op jit(solution)/shard_map/ppermute | solution.py:19
  28.8 2.7 %collective-permute-start.4 = (bf16[48,1792]{1,0:T(8,128)(2,1)S(1)}, bf16[48,1792]{1,0:T(8,128)(2,1)S(1)}, u32[]{:S(2)}, u32[]{:S(2)}) collective-permute-start(bf16[48,1792]{1,0:T(8,128)(2,1)S(1)} %get-tuple-element.23), channel_id=1, source_target_pairs={{0,4},{1,5},{2,6},{3,7},{4,0},{5,1},{6,2},{7,3},{8,12},{9,13},{10,... | collective-permute-start | bytes 516104 | tf_op jit(solution)/shard_map/ppermute | solution.py:19
  31.5 1.1 collective-permute-start.5
  32.5 1.0 collective-permute-done.3.refs_1_
  33.5 8.4 %collective-permute-done.4.refs_2_ = bf16[48,1792]{1,0:T(8,128)(2,1)S(1)} collective-permute-done((bf16[48,1792]{1,0:T(8,128)(2,1)S(1)}, bf16[48,1792]{1,0:T(8,128)(2,1)S(1)}, u32[]{:S(2)}, u32[]{:S(2)}) %collective-permute-start.4) | collective-permute-done | bytes 172064 | tf_op jit(solution)/shard_map/ppermute | solution.py:19
  41.9 3.1 %collective-permute-done.5.refs_3_ = bf16[48,1792]{1,0:T(8,128)(2,1)S(1)} collective-permute-done((bf16[48,1792]{1,0:T(8,128)(2,1)S(1)}, bf16[48,1792]{1,0:T(8,128)(2,1)S(1)}, u32[]{:S(2)}, u32[]{:S(2)}) %collective-permute-start.5) | collective-permute-done | bytes 172064 | tf_op jit(solution)/shard_map/ppermute | solution.py:19
  46.7 15.9 %collective-permute-done.6.refs_4_ = bf16[192,1792]{1,0:T(8,128)(2,1)S(1)} collective-permute-done((bf16[192,1792]{1,0:T(8,128)(2,1)S(1)}, bf16[192,1792]{1,0:T(8,128)(2,1)S(1)}, u32[]{:S(2)}, u32[]{:S(2)}) %collective-permute-start.6) | collective-permute-done | bytes 688160 | tf_op jit(solution)/shard_map/ppermute | solution.py:19
  63.7 5.1 %collective-permute-done.1.refs_2_ = bf16[576,128]{1,0:T(8,128)(2,1)S(1)} collective-permute-done((bf16[576,128]{1,0:T(8,128)(2,1)S(1)}, bf16[576,128]{1,0:T(8,128)(2,1)S(1)}, u32[]{:S(2)}, u32[]{:S(2)}) %collective-permute-start.1) | collective-permute-done | bytes 147488 | tf_op jit(solution)/shard_map/ppermute | solution.py:19
  69.4 1.4 %collective-permute-start.11 = (bf16[128,1792]{1,0:T(8,128)(2,1)S(1)}, bf16[128,1792]{1,0:T(8,128)(2,1)S(1)}, u32[]{:S(2)}, u32[]{:S(2)}) collective-permute-start(bf16[128,1792]{1,0:T(8,128)(2,1)S(1)} %get-tuple-element.27), channel_id=1, source_target_pairs={{0,24},{8,16},{16,8},{24,0},{1,25},{9,17},{17,9},{25,1},{2,26},{10... | collective-permute-start | bytes 1376264 | tf_op jit(solution)/shard_map/ppermute | solution.py:19
  70.7 1.1 shard_map.121.refs_6_
  71.8 1.1 shard_map.122
  72.9 20.6 %all-gather.1 = bf16[768,128]{1,0:T(8,128)(2,1)S(1)} all-gather(bf16[192,128]{1,0:T(8,128)(2,1)S(1)} %shard_map.122), channel_id=3, replica_groups=mesh['ctx'=4,'exp'=8] {'ctx'}, dimensions={0}, use_global_device_ids=true | all-gather | bytes 245760 | tf_op jit(solution)/shard_map/all_gather | solution.py:347
  94.0 1.1 shard_map.123
  96.2 1.1 shard_map.116.refs_6_
  97.3 2.4 %collective-permute-start.24 = (bf16[48,1792]{1,0:T(8,128)(2,1)S(1)}, bf16[48,1792]{1,0:T(8,128)(2,1)S(1)}, u32[]{:S(2)}, u32[]{:S(2)}) collective-permute-start(bf16[48,1792]{1,0:T(8,128)(2,1)S(1)} %get-tuple-element.38), channel_id=1, source_target_pairs={{0,6},{1,7},{2,4},{3,5},{4,2},{5,3},{6,0},{7,1},{8,14},{9,15},{10,... | collective-permute-start | bytes 516104 | tf_op jit(solution)/shard_map/ppermute | solution.py:19
  99.7 1.1 shard_map.117
  100.8 5.7 %all-gather = bf16[768,128]{1,0:T(8,128)(2,1)S(1)} all-gather(bf16[192,128]{1,0:T(8,128)(2,1)S(1)} %shard_map.117), channel_id=2, replica_groups=mesh['ctx'=4,'exp'=8] {'ctx'}, dimensions={0}, use_global_device_ids=true | all-gather | bytes 245760 | tf_op jit(solution)/shard_map/all_gather | solution.py:347
  106.6 1.1 shard_map.119
  107.7 3.4 %collective-permute-start.25 = (bf16[48,1792]{1,0:T(8,128)(2,1)S(1)}, bf16[48,1792]{1,0:T(8,128)(2,1)S(1)}, u32[]{:S(2)}, u32[]{:S(2)}) collective-permute-start(bf16[48,1792]{1,0:T(8,128)(2,1)S(1)} %get-tuple-element.39), channel_id=1, source_target_pairs={{0,7},{1,6},{2,5},{3,4},{4,3},{5,2},{6,1},{7,0},{8,15},{9,14},{10,... | collective-permute-start | bytes 516104 | tf_op jit(solution)/shard_map/ppermute | solution.py:19
  111.2 4.3 %collective-permute-start.23 = (bf16[48,1792]{1,0:T(8,128)(2,1)S(1)}, bf16[48,1792]{1,0:T(8,128)(2,1)S(1)}, u32[]{:S(2)}, u32[]{:S(2)}) collective-permute-start(bf16[48,1792]{1,0:T(8,128)(2,1)S(1)} %get-tuple-element.37), channel_id=1, source_target_pairs={{0,5},{1,4},{2,7},{3,6},{4,1},{5,0},{6,3},{7,2},{8,13},{9,12},{10,... | collective-permute-start | bytes 516104 | tf_op jit(solution)/shard_map/ppermute | solution.py:19
  115.5 9.3 %shard_map.113 = bf16[8,128,128]{2,1,0:T(8,128)(2,1)S(1)} custom-call(s32[2]{0:T(128)S(1)} %pad_add_fusion.where_ref, s32[8]{0:T(128)S(1)} %copy-done.10, bf16[8,576,128]{2,1,0:T(8,128)(2,1)S(1)} %bitcast.39, bf16[8,512,128]{2,1,0:T(8,128)(2,1)S(1)} %copy-done.8, bf16[576,128]{1,0:T(8,128)(2,1)S(1)} %bitcast.42, ...), custom_call_target="tpu_custom_call" | custom-call | flops 1207959552 | bytes 3080192 | tf_op jit(solution)/shard_map/pallas_call | solution.py:41
  125.7 4.6 %collective-permute-done.22.refs_4_ = bf16[48,1792]{1,0:T(8,128)(2,1)S(1)} collective-permute-done((bf16[48,1792]{1,0:T(8,128)(2,1)S(1)}, bf16[48,1792]{1,0:T(8,128)(2,1)S(1)}, u32[]{:S(2)}, u32[]{:S(2)}) %collective-permute-start.22) | collective-permute-done | bytes 172064 | tf_op jit(solution)/shard_map/ppermute | solution.py:19
  130.4 3.1 %collective-permute-done.23.refs_5_ = bf16[48,1792]{1,0:T(8,128)(2,1)S(1)} collective-permute-done((bf16[48,1792]{1,0:T(8,128)(2,1)S(1)}, bf16[48,1792]{1,0:T(8,128)(2,1)S(1)}, u32[]{:S(2)}, u32[]{:S(2)}) %collective-permute-start.23) | collective-permute-done | bytes 172064 | tf_op jit(solution)/shard_map/ppermute | solution.py:19
  133.5 2.5 %shard_map.124 = bf16[128,1792]{1,0:T(8,128)(2,1)} custom-call(s32[2]{0:T(128)S(1)} %pad_add_fusion.where_ref, s32[2,128]{1,0:T(2,128)S(1)} %bitcast.37, f32[2,128]{1,0:T(2,128)S(1)} %bitcast.38, bf16[48,1792]{1,0:T(8,128)(2,1)S(1)} %get-tuple-element.28.refs_0_, bf16[48,1792]{1,0:T(8,128)(2,1)S(1)} %collective-permute-done.12.refs_1_, ...), custom_call_target="tpu_custom_call" | custom-call | flops 352321536 | bytes 1837056 | tf_op jit(solution)/shard_map/pallas_call | solution.py:41
  (58 shorter events, 8.1 us)
Async XLA Ops:
  4.1 58.5 %copy-start.9 = (bf16[128,576]{0,1:T(8,128)(2,1)S(1)}, bf16[128,576]{0,1:T(8,128)(2,1)}, u32[]{:S(2)}) copy-start(bf16[128,576]{0,1:T(8,128)(2,1)} %param.11) | copy-start | bytes 442372
  4.1 59.0 %copy-start.2 = (bf16[1,128,7168]{2,1,0:T(8,128)(2,1)S(1)}, bf16[1,128,7168]{2,1,0:T(8,128)(2,1)}, u32[]{:S(2)}) copy-start(bf16[1,128,7168]{2,1,0:T(8,128)(2,1)} %param.19) | copy-start | bytes 5505028
  4.1 8.3 %collective-permute-start.13 = (bf16[48,1792]{1,0:T(8,128)(2,1)S(1)}, bf16[48,1792]{1,0:T(8,128)(2,1)S(1)}, u32[]{:S(2)}, u32[]{:S(2)}) collective-permute-start(bf16[48,1792]{1,0:T(8,128)(2,1)S(1)} %get-tuple-element.30), channel_id=1, source_target_pairs={{0,2},{1,3},{2,0},{3,1},{4,6},{5,7},{6,4},{7,5},{8,10},{9,11},{10,... | collective-permute-start | bytes 516104 | tf_op jit(solution)/shard_map/ppermute | solution.py:19
  7.2 9.2 %collective-permute-start.14 = (bf16[48,1792]{1,0:T(8,128)(2,1)S(1)}, bf16[48,1792]{1,0:T(8,128)(2,1)S(1)}, u32[]{:S(2)}, u32[]{:S(2)}) collective-permute-start(bf16[48,1792]{1,0:T(8,128)(2,1)S(1)} %get-tuple-element.31), channel_id=1, source_target_pairs={{0,3},{1,2},{2,1},{3,0},{4,7},{5,6},{6,5},{7,4},{8,11},{9,10},{10,... | collective-permute-start | bytes 516104 | tf_op jit(solution)/shard_map/ppermute | solution.py:19
  8.6 14.0 %collective-permute-start.15 = (bf16[48,1792]{1,0:T(8,128)(2,1)S(1)}, bf16[48,1792]{1,0:T(8,128)(2,1)S(1)}, u32[]{:S(2)}, u32[]{:S(2)}) collective-permute-start(bf16[48,1792]{1,0:T(8,128)(2,1)S(1)} %get-tuple-element.32), channel_id=1, source_target_pairs={{0,6},{1,7},{2,4},{3,5},{4,2},{5,3},{6,0},{7,1},{8,14},{9,15},{10,... | collective-permute-start | bytes 516104 | tf_op jit(solution)/shard_map/ppermute | solution.py:19
  12.2 13.8 %collective-permute-start.16 = (bf16[48,1792]{1,0:T(8,128)(2,1)S(1)}, bf16[48,1792]{1,0:T(8,128)(2,1)S(1)}, u32[]{:S(2)}, u32[]{:S(2)}) collective-permute-start(bf16[48,1792]{1,0:T(8,128)(2,1)S(1)} %get-tuple-element.33), channel_id=1, source_target_pairs={{0,7},{1,6},{2,5},{3,4},{4,3},{5,2},{6,1},{7,0},{8,15},{9,14},{10,... | collective-permute-start | bytes 516104 | tf_op jit(solution)/shard_map/ppermute | solution.py:19
  26.6 19.6 %collective-permute-start.17 = (bf16[192,1792]{1,0:T(8,128)(2,1)S(1)}, bf16[192,1792]{1,0:T(8,128)(2,1)S(1)}, u32[]{:S(2)}, u32[]{:S(2)}) collective-permute-start(bf16[192,1792]{1,0:T(8,128)(2,1)S(1)} %shard_map.120.refs_4_), channel_id=1, source_target_pairs={{0,16},{8,24},{16,0},{24,8},{1,17},{9,25},{17,1},{25,9},{2,18},{10... | collective-permute-start | bytes 2064392 | tf_op jit(solution)/shard_map/ppermute | solution.py:19
  28.1 5.4 %collective-permute-start.3 = (bf16[48,1792]{1,0:T(8,128)(2,1)S(1)}, bf16[48,1792]{1,0:T(8,128)(2,1)S(1)}, u32[]{:S(2)}, u32[]{:S(2)}) collective-permute-start(bf16[48,1792]{1,0:T(8,128)(2,1)S(1)} %get-tuple-element.22), channel_id=1, source_target_pairs={{0,1},{1,0},{2,3},{3,2},{4,5},{5,4},{6,7},{7,6},{8,9},{9,8},{10,11... | collective-permute-start | bytes 516104 | tf_op jit(solution)/shard_map/ppermute | solution.py:19
  28.8 13.2 %collective-permute-start.4 = (bf16[48,1792]{1,0:T(8,128)(2,1)S(1)}, bf16[48,1792]{1,0:T(8,128)(2,1)S(1)}, u32[]{:S(2)}, u32[]{:S(2)}) collective-permute-start(bf16[48,1792]{1,0:T(8,128)(2,1)S(1)} %get-tuple-element.23), channel_id=1, source_target_pairs={{0,4},{1,5},{2,6},{3,7},{4,0},{5,1},{6,2},{7,3},{8,12},{9,13},{10,... | collective-permute-start | bytes 516104 | tf_op jit(solution)/shard_map/ppermute | solution.py:19
  31.5 13.6 %collective-permute-start.5 = (bf16[48,1792]{1,0:T(8,128)(2,1)S(1)}, bf16[48,1792]{1,0:T(8,128)(2,1)S(1)}, u32[]{:S(2)}, u32[]{:S(2)}) collective-permute-start(bf16[48,1792]{1,0:T(8,128)(2,1)S(1)} %get-tuple-element.24), channel_id=1, source_target_pairs={{0,5},{1,4},{2,7},{3,6},{4,1},{5,0},{6,3},{7,2},{8,13},{9,12},{10,... | collective-permute-start | bytes 516104 | tf_op jit(solution)/shard_map/ppermute | solution.py:19
  45.6 17.0 %collective-permute-start.6 = (bf16[192,1792]{1,0:T(8,128)(2,1)S(1)}, bf16[192,1792]{1,0:T(8,128)(2,1)S(1)}, u32[]{:S(2)}, u32[]{:S(2)}) collective-permute-start(bf16[192,1792]{1,0:T(8,128)(2,1)S(1)} %shard_map.115.refs_4_), channel_id=1, source_target_pairs={{0,16},{8,24},{16,0},{24,8},{1,17},{9,25},{17,1},{25,9},{2,18},{10... | collective-permute-start | bytes 2064392 | tf_op jit(solution)/shard_map/ppermute | solution.py:19
  46.2 22.7 %collective-permute-start.19 = (bf16[192,1792]{1,0:T(8,128)(2,1)S(1)}, bf16[192,1792]{1,0:T(8,128)(2,1)S(1)}, u32[]{:S(2)}, u32[]{:S(2)}) collective-permute-start(bf16[192,1792]{1,0:T(8,128)(2,1)S(1)} %shard_map.120.refs_4_), channel_id=1, source_target_pairs={{0,8},{8,0},{16,24},{24,16},{1,9},{9,1},{17,25},{25,17},{2,10},{10... | collective-permute-start | bytes 2064392 | tf_op jit(solution)/shard_map/ppermute | solution.py:19
  46.2 23.2 %collective-permute-start.18 = (bf16[192,1792]{1,0:T(8,128)(2,1)S(1)}, bf16[192,1792]{1,0:T(8,128)(2,1)S(1)}, u32[]{:S(2)}, u32[]{:S(2)}) collective-permute-start(bf16[192,1792]{1,0:T(8,128)(2,1)S(1)} %collective-permute-done.17.refs_4_), channel_id=1, source_target_pairs={{0,8},{8,0},{16,24},{24,16},{1,9},{9,1},{17,25},{25,17},{2,10},{10... | collective-permute-start | bytes 2064392 | tf_op jit(solution)/shard_map/ppermute | solution.py:19
  46.7 48.5 %collective-permute-start.8 = (bf16[192,1792]{1,0:T(8,128)(2,1)S(1)}, bf16[192,1792]{1,0:T(8,128)(2,1)S(1)}, u32[]{:S(2)}, u32[]{:S(2)}) collective-permute-start(bf16[192,1792]{1,0:T(8,128)(2,1)S(1)} %shard_map.115.refs_4_), channel_id=1, source_target_pairs={{0,8},{8,0},{16,24},{24,16},{1,9},{9,1},{17,25},{25,17},{2,10},{10... | collective-permute-start | bytes 2064392 | tf_op jit(solution)/shard_map/ppermute | solution.py:19
  62.6 34.7 %collective-permute-start.7 = (bf16[192,1792]{1,0:T(8,128)(2,1)S(1)}, bf16[192,1792]{1,0:T(8,128)(2,1)S(1)}, u32[]{:S(2)}, u32[]{:S(2)}) collective-permute-start(bf16[192,1792]{1,0:T(8,128)(2,1)S(1)} %collective-permute-done.6.refs_4_), channel_id=1, source_target_pairs={{0,8},{8,0},{16,24},{24,16},{1,9},{9,1},{17,25},{25,17},{2,10},{10... | collective-permute-start | bytes 2064392 | tf_op jit(solution)/shard_map/ppermute | solution.py:19
  62.6 6.3 %collective-permute-start.1 = (bf16[576,128]{1,0:T(8,128)(2,1)S(1)}, bf16[576,128]{1,0:T(8,128)(2,1)S(1)}, u32[]{:S(2)}, u32[]{:S(2)}) collective-permute-start(bf16[576,128]{1,0:T(8,128)(2,1)S(1)} %bitcast.40), channel_id=1, source_target_pairs={{0,16},{8,24},{16,0},{24,8},{1,17},{9,25},{17,1},{25,9},{2,18},{10... | collective-permute-start | bytes 442376 | tf_op jit(solution)/shard_map/ppermute | solution.py:19
  68.8 24.7 %collective-permute-start.9 = (bf16[128,1792]{1,0:T(8,128)(2,1)S(1)}, bf16[128,1792]{1,0:T(8,128)(2,1)S(1)}, u32[]{:S(2)}, u32[]{:S(2)}) collective-permute-start(bf16[128,1792]{1,0:T(8,128)(2,1)S(1)} %get-tuple-element.25), channel_id=1, source_target_pairs={{0,8},{8,0},{16,24},{24,16},{1,9},{9,1},{17,25},{25,17},{2,10},{10... | collective-permute-start | bytes 1376264 | tf_op jit(solution)/shard_map/ppermute | solution.py:19
  68.9 25.0 %collective-permute-start.10 = (bf16[128,1792]{1,0:T(8,128)(2,1)S(1)}, bf16[128,1792]{1,0:T(8,128)(2,1)S(1)}, u32[]{:S(2)}, u32[]{:S(2)}) collective-permute-start(bf16[128,1792]{1,0:T(8,128)(2,1)S(1)} %get-tuple-element.26), channel_id=1, source_target_pairs={{0,16},{8,24},{16,0},{24,8},{1,17},{9,25},{17,1},{25,9},{2,18},{10... | collective-permute-start | bytes 1376264 | tf_op jit(solution)/shard_map/ppermute | solution.py:19
  69.4 24.7 %collective-permute-start.11 = (bf16[128,1792]{1,0:T(8,128)(2,1)S(1)}, bf16[128,1792]{1,0:T(8,128)(2,1)S(1)}, u32[]{:S(2)}, u32[]{:S(2)}) collective-permute-start(bf16[128,1792]{1,0:T(8,128)(2,1)S(1)} %get-tuple-element.27), channel_id=1, source_target_pairs={{0,24},{8,16},{16,8},{24,0},{1,25},{9,17},{17,9},{25,1},{2,26},{10... | collective-permute-start | bytes 1376264 | tf_op jit(solution)/shard_map/ppermute | solution.py:19
  93.5 14.2 %collective-permute-start = (bf16[576,128]{1,0:T(8,128)(2,1)S(1)}, bf16[576,128]{1,0:T(8,128)(2,1)S(1)}, u32[]{:S(2)}, u32[]{:S(2)}) collective-permute-start(bf16[576,128]{1,0:T(8,128)(2,1)S(1)} %bitcast.41), channel_id=1, source_target_pairs={{0,8},{8,0},{16,24},{24,16},{1,9},{9,1},{17,25},{25,17},{2,10},{10... | collective-permute-start | bytes 442376 | tf_op jit(solution)/shard_map/ppermute | solution.py:19
  93.9 17.2 %collective-permute-start.2 = (bf16[576,128]{1,0:T(8,128)(2,1)S(1)}, bf16[576,128]{1,0:T(8,128)(2,1)S(1)}, u32[]{:S(2)}, u32[]{:S(2)}) collective-permute-start(bf16[576,128]{1,0:T(8,128)(2,1)S(1)} %collective-permute-done.1.refs_2_), channel_id=1, source_target_pairs={{0,8},{8,0},{16,24},{24,16},{1,9},{9,1},{17,25},{25,17},{2,10},{10... | collective-permute-start | bytes 442376 | tf_op jit(solution)/shard_map/ppermute | solution.py:19
  95.1 16.0 %collective-permute-start.20 = (bf16[48,1792]{1,0:T(8,128)(2,1)S(1)}, bf16[48,1792]{1,0:T(8,128)(2,1)S(1)}, u32[]{:S(2)}, u32[]{:S(2)}) collective-permute-start(bf16[48,1792]{1,0:T(8,128)(2,1)S(1)} %get-tuple-element.34), channel_id=1, source_target_pairs={{0,2},{1,3},{2,0},{3,1},{4,6},{5,7},{6,4},{7,5},{8,10},{9,11},{10,... | collective-permute-start | bytes 516104 | tf_op jit(solution)/shard_map/ppermute | solution.py:19
  95.2 16.0 %collective-permute-start.21 = (bf16[48,1792]{1,0:T(8,128)(2,1)S(1)}, bf16[48,1792]{1,0:T(8,128)(2,1)S(1)}, u32[]{:S(2)}, u32[]{:S(2)}) collective-permute-start(bf16[48,1792]{1,0:T(8,128)(2,1)S(1)} %get-tuple-element.35), channel_id=1, source_target_pairs={{0,3},{1,2},{2,1},{3,0},{4,7},{5,6},{6,5},{7,4},{8,11},{9,10},{10,... | collective-permute-start | bytes 516104 | tf_op jit(solution)/shard_map/ppermute | solution.py:19
  97.3 28.5 %collective-permute-start.24 = (bf16[48,1792]{1,0:T(8,128)(2,1)S(1)}, bf16[48,1792]{1,0:T(8,128)(2,1)S(1)}, u32[]{:S(2)}, u32[]{:S(2)}) collective-permute-start(bf16[48,1792]{1,0:T(8,128)(2,1)S(1)} %get-tuple-element.38), channel_id=1, source_target_pairs={{0,6},{1,7},{2,4},{3,5},{4,2},{5,3},{6,0},{7,1},{8,14},{9,15},{10,... | collective-permute-start | bytes 516104 | tf_op jit(solution)/shard_map/ppermute | solution.py:19
  100.8 14.7 %copy-start.7 = (bf16[128,8,576]{0,2,1:T(8,128)(2,1)S(1)}, bf16[128,8,576]{0,2,1:T(8,128)(2,1)}, u32[]{:S(2)}) copy-start(bf16[128,8,576]{0,2,1:T(8,128)(2,1)} %param.10) | copy-start | bytes 3538948
  100.8 14.7 %copy-start.8 = (bf16[8,512,128]{2,1,0:T(8,128)(2,1)S(1)}, bf16[8,512,128]{2,1,0:T(8,128)(2,1)}, u32[]{:S(2)}) copy-start(bf16[8,512,128]{2,1,0:T(8,128)(2,1)} %uv_ref.1) | copy-start | bytes 3145732
  107.7 18.1 %collective-permute-start.25 = (bf16[48,1792]{1,0:T(8,128)(2,1)S(1)}, bf16[48,1792]{1,0:T(8,128)(2,1)S(1)}, u32[]{:S(2)}, u32[]{:S(2)}) collective-permute-start(bf16[48,1792]{1,0:T(8,128)(2,1)S(1)} %get-tuple-element.39), channel_id=1, source_target_pairs={{0,7},{1,6},{2,5},{3,4},{4,3},{5,2},{6,1},{7,0},{8,15},{9,14},{10,... | collective-permute-start | bytes 516104 | tf_op jit(solution)/shard_map/ppermute | solution.py:19
  111.1 14.7 %collective-permute-start.12 = (bf16[48,1792]{1,0:T(8,128)(2,1)S(1)}, bf16[48,1792]{1,0:T(8,128)(2,1)S(1)}, u32[]{:S(2)}, u32[]{:S(2)}) collective-permute-start(bf16[48,1792]{1,0:T(8,128)(2,1)S(1)} %get-tuple-element.29), channel_id=1, source_target_pairs={{0,1},{1,0},{2,3},{3,2},{4,5},{5,4},{6,7},{7,6},{8,9},{9,8},{10,11... | collective-permute-start | bytes 516104 | tf_op jit(solution)/shard_map/ppermute | solution.py:19
  111.1 19.3 %collective-permute-start.22 = (bf16[48,1792]{1,0:T(8,128)(2,1)S(1)}, bf16[48,1792]{1,0:T(8,128)(2,1)S(1)}, u32[]{:S(2)}, u32[]{:S(2)}) collective-permute-start(bf16[48,1792]{1,0:T(8,128)(2,1)S(1)} %get-tuple-element.36), channel_id=1, source_target_pairs={{0,4},{1,5},{2,6},{3,7},{4,0},{5,1},{6,2},{7,3},{8,12},{9,13},{10,... | collective-permute-start | bytes 516104 | tf_op jit(solution)/shard_map/ppermute | solution.py:19
  111.2 22.3 %collective-permute-start.23 = (bf16[48,1792]{1,0:T(8,128)(2,1)S(1)}, bf16[48,1792]{1,0:T(8,128)(2,1)S(1)}, u32[]{:S(2)}, u32[]{:S(2)}) collective-permute-start(bf16[48,1792]{1,0:T(8,128)(2,1)S(1)} %get-tuple-element.37), channel_id=1, source_target_pairs={{0,5},{1,4},{2,7},{3,6},{4,1},{5,0},{6,3},{7,2},{8,13},{9,12},{10,... | collective-permute-start | bytes 516104 | tf_op jit(solution)/shard_map/ppermute | solution.py:19
  115.5 18.0 %copy-start.5 = (s32[128,2]{0,1:T(2,128)S(1)}, s32[128,2]{0,1:T(2,128)}, u32[]{:S(2)}) copy-start(s32[128,2]{0,1:T(2,128)} %param.15) | copy-start | bytes 3076
  115.5 18.0 %copy-start.6 = (f32[128,2]{0,1:T(2,128)S(1)}, f32[128,2]{0,1:T(2,128)}, u32[]{:S(2)}) copy-start(f32[128,2]{0,1:T(2,128)} %param.16) | copy-start | bytes 3076
  (5 other events, 32.1 us)
where the time goes:
time: 136 us
  waiting for transfers between devices  55.1 us (41%)
  starting transfers between devices  29.3 us (22%)
  blocking collectives  26.3 us (19%)
  Pallas kernels  21.3 us (16%)
  local copies, waits for them, and re-layouts  3.1 us (2%)
    ppermute x26, waiting for transfers between devices, swap(): return lax.ppermute(x, axis, [(i, i ^ offset) for i in range(size)])  55.1 us
    ppermute x26, starting transfers between devices, swap(): return lax.ppermute(x, axis, [(i, i ^ offset) for i in range(size)])  29.3 us
    all_gather x2, blocking collectives, layer(): hidden = lax.all_gather(hidden, 'ctx', axis=0)  26.3 us
    pallas_call x12, Pallas kernels, call(): pl.pallas_call(kernel, out_shape=out_shape, grid_spec=pltpu.PrefetchScala...  21.3 us
    unnamed x23, local copies, waits for them, and re-layouts  3.1 us
  transfers between devices with their start and end apart: 26, of which 11 were waited for; matrix products, arithmetic and copies ran while one was open for 1% of the time, Pallas kernels for 13%

commit v1 on v0

--- a/solution.py
+++ b/solution.py
@@ -12,6 +12,7 @@
 score_scale = (0.1 * math.log(40.0) + 1.0) ** 2 / math.sqrt(192.0)
 neg_fill = -1e30
 SETS = 2
+CHUNKS = (1, 2)
 
 
 def swap(x, axis, offset):
@@ -22,7 +23,8 @@
 def set_members(expert_count):
     half = expert_count // 2
     return [
-        [k for k in range(expert_count) if (k % half) * SETS // half == s] for s in range(SETS)
+        [k for k in range(expert_count) if (k % half) * SETS // half == s]
+        for s in reversed(range(SETS))
     ]
 
 
@@ -122,59 +124,67 @@
     )
 
 
-def pack_kernel(where_ref, *refs):
-    rows = refs[0].shape[0]
-    for i, source in enumerate(refs[:-1]):
-        refs[-1][i * rows : (i + 1) * rows, :] = source[...]
-
-
-def pack(blocks, where):
+def pack_kernel(count, where_ref, *refs):
+    rows, targets = refs[0].shape[0], refs[count:]
+    share = count // len(targets)
+    for i, source in enumerate(refs[:count]):
+        at = i % share * rows
+        targets[i // share][at : at + rows, :] = source[...]
+
+
+def pack(blocks, chunks, where):
     rows, width = blocks[0].shape
-    shape = (len(blocks) * rows, width)
-    return call(
-        pack_kernel, (1,), blocks, [whole_spec((rows, width))] * len(blocks),
-        jax.ShapeDtypeStruct(shape, blocks[0].dtype), whole_spec(shape), shape[0] * width, where,
-    )
-
-
-def up_sum(gate_refs, up_refs, pieces):
+    shape = (len(blocks) // chunks * rows, width)
+    return call(
+        functools.partial(pack_kernel, len(blocks)), (1,), blocks,
+        [whole_spec((rows, width))] * len(blocks),
+        [jax.ShapeDtypeStruct(shape, blocks[0].dtype)] * chunks, [whole_spec(shape)] * chunks,
+        len(blocks) * rows * width, where,
+    )
+
+
+def up_sum(count, refs):
+    gate_refs, up_refs, rows = refs[:count], refs[count : 2 * count], refs[2 * count :]
+    chunks = len(rows) // count
     acc = None
-    for gate_ref, up_ref, piece in zip(gate_refs, up_refs, pieces):
-        weights = jnp.concatenate([gate_ref[...], up_ref[...]], axis=1)
-        term = jnp.dot(piece[...], weights, preferred_element_type=jnp.float32)
+    for j in range(count):
+        weights = jnp.concatenate([gate_refs[j][...], up_refs[j][...]], axis=1)
+        piece = [ref[...] for ref in rows[j * chunks : (j + 1) * chunks]]
+        piece = piece[0] if chunks == 1 else jnp.concatenate(piece, axis=0)
+        term = jnp.dot(piece, weights, preferred_element_type=jnp.float32)
         acc = term if acc is None else acc + term
     return acc
 
 
-def part_kernel(where_ref, *refs):
-    count = len(refs) // 3
-    refs[-1][...] = up_sum(refs[:count], refs[count : 2 * count], refs[2 * count : -1])
-
-
-def mlp_kernel(where_ref, *refs):
-    count = len(refs) // 3
-    acc = refs[-2][...] + up_sum(refs[:count], refs[count : 2 * count], refs[2 * count : -2])
+def part_kernel(count, where_ref, *refs):
+    refs[-1][...] = up_sum(count, refs[:-1])
+
+
+def mlp_kernel(count, where_ref, *refs):
+    acc = refs[-2][...] + up_sum(count, refs[:-2])
     hidden_width = acc.shape[1] // 2
     gate_h, up_h = acc[:, :hidden_width], acc[:, hidden_width:]
     refs[-1][...] = (gate_h / (1.0 + jnp.exp(-gate_h)) * up_h).astype(refs[-1].dtype)
 
 
 def mlp(pieces, offsets, gate_matrix, up_matrix, partial, where):
-    rows, width = pieces[0].shape
+    chunk_rows, width = pieces[0][0].shape
     count, hidden_width = len(pieces), gate_matrix.shape[1]
+    rows = chunk_rows * len(pieces[0])
+    flat = [chunk for piece in pieces for chunk in piece]
     specs = [
         pl.BlockSpec((width, hidden_width), lambda i, w, k=k: (w[1] ^ k, 0)) for k in offsets
     ]
-    operands = [gate_matrix] * count + [up_matrix] * count + list(pieces)
-    specs = specs + specs + [whole_spec((rows, width))] * count
+    operands = [gate_matrix] * count + [up_matrix] * count + flat
+    specs = specs + specs + [whole_spec((chunk_rows, width))] * len(flat)
     if partial is None:
         kernel, out = part_kernel, jax.ShapeDtypeStruct((rows, 2 * hidden_width), jnp.float32)
     else:
-        kernel, out = mlp_kernel, jax.ShapeDtypeStruct((rows, hidden_width), pieces[0].dtype)
+        kernel, out = mlp_kernel, jax.ShapeDtypeStruct((rows, hidden_width), flat[0].dtype)
         operands.append(partial)
         specs.append(whole_spec(partial.shape))
     return call(
-        kernel, (1,), operands, specs, out, whole_spec(out.shape),
+        functools.partial(kernel, count), (1,), operands, specs, out, whole_spec(out.shape),
         4 * count * rows * width * hidden_width, where, vmem=24 << 20,
     )
 
@@ -184,11 +194,10 @@
     return [slice(at, at + step) for at in range(0, width, step)]
 
 
-def down_kernel(where_ref, hidden_ref, *refs):
-    ctx_size = hidden_ref.shape[0]
-    parts, out_refs = refs[:ctx_size], refs[ctx_size:]
+def down_kernel(count, where_ref, *refs):
+    parts, out_refs = refs[count : 2 * count], refs[2 * count :]
     rows, width = out_refs[0].shape
-    hidden = jnp.concatenate([hidden_ref[where_ref[1] ^ j] for j in range(ctx_size)], axis=1)
+    hidden = jnp.concatenate([ref[...] for ref in refs[:count]], axis=1)
     for tile in tiles(width):
         matrix = jnp.concatenate([part[:, tile] for part in parts], axis=0)
         out = jnp.dot(hidden, matrix, preferred_element_type=jnp.float32)
@@ -198,27 +207,39 @@
 
 
 def down(hidden, own, others, block_count, where):
-    width = others[0].shape[1]
+    width, count = others[0].shape[1], len(hidden)
     operand, spec = own_columns(own, width, where)
-    block = (hidden.shape[1] // block_count, width)
-    return call(
-        down_kernel, (1,), [hidden, operand, *others],
-        [whole_spec(hidden.shape), spec] + [whole_spec(others[0].shape)] * len(others),
-        [jax.ShapeDtypeStruct(block, hidden.dtype)] * block_count,
+    block = (hidden[0].shape[0] // block_count, width)
+    return call(
+        functools.partial(down_kernel, count), (1,), [*hidden, operand, *others],
+        [whole_spec(hidden[0].shape)] * count + [spec] + [whole_spec(others[0].shape)] * len(others),
+        [jax.ShapeDtypeStruct(block, hidden[0].dtype)] * block_count,
         [whole_spec(block)] * block_count,
-        2 * math.prod(hidden.shape) * width, where,
-    )
-
-
-def combine_kernel(where_ref, ids_ref, gates_ref, *refs):
-    row_refs, out_ref = refs[:-1], refs[-1]
-    expert_count, capacity = len(row_refs), row_refs[0].shape[0]
+        2 * count * math.prod(hidden[0].shape) * width, where,
+    )
+
+
+def mix(hits, gates, row_refs, tile, picks):
+    token_count = hits.shape[0] // picks
+    arrived = jnp.concatenate([ref[:, tile] for ref in row_refs], axis=0)
+    chosen = jnp.dot(hits, arrived, preferred_element_type=jnp.float32)
+    total = None
+    for k in range(picks):
+        term = chosen[k * token_count : (k + 1) * token_count, :] * gates[:, k : k + 1]
+        total = term if total is None else total + term
+    return total
+
+
+def begin_kernel(members, where_ref, ids_ref, gates_ref, *refs):
+    row_refs, sum_ref, hits_ref, columns_ref = refs[:-3], refs[-3], refs[-2], refs[-1]
+    expert_count, capacity = sum(len(m) for m in members), row_refs[0].shape[0]
     picks, token_count = ids_ref.shape
     columns = jnp.concatenate(
         [ids_ref[...].astype(jnp.float32), gates_ref[...]]
         + [jnp.zeros((-2 * picks % 8, token_count), jnp.float32)],
         axis=0,
     ).T
+    columns_ref[...] = columns
     ids, gates = columns[:, :picks].astype(jnp.int32), columns[:, picks : 2 * picks]
     experts = lax.broadcasted_iota(jnp.int32, (token_count, expert_count), 1)
     named = jnp.zeros((token_count, expert_count), jnp.float32)
@@ -228,35 +249,59 @@
     cols = lax.broadcasted_iota(jnp.int32, (token_count, token_count), 1)
     before = jnp.where(cols < rows, 1.0, 0.0).astype(jnp.bfloat16)
     rank = jnp.dot(before, named.astype(jnp.bfloat16), preferred_element_type=jnp.float32)
-    slots = lax.broadcasted_iota(jnp.int32, (token_count, expert_count * capacity), 1)
-    hits = []
+    places = []
     for k in range(picks):
         own = jnp.where(ids[:, k : k + 1] == experts, rank, 0.0)
-        place = jnp.sum(own, axis=1, keepdims=True).astype(jnp.int32)
-        place = place + (ids[:, k : k + 1] ^ where_ref[0]) * capacity
-        hits.append(jnp.where(place == slots, 1.0, 0.0).astype(jnp.bfloat16))
-    hits = jnp.concatenate(hits, axis=0)
+        rank_k = jnp.sum(own, axis=1, keepdims=True).astype(jnp.int32)
+        places.append((ids[:, k : k + 1] ^ where_ref[0], rank_k))
+
+    def hits_of(group):
+        slots = lax.broadcasted_iota(jnp.int32, (token_count, len(group) * capacity), 1)
+        out = []
+        for block, rank_k in places:
+            place = jnp.full_like(rank_k, -1)
+            for at, k in enumerate(group):
+                place = jnp.where(block == k, at * capacity + rank_k, place)
+            out.append(jnp.where(place == slots, 1.0, 0.0).astype(jnp.bfloat16))
+        return jnp.concatenate(out, axis=0)
+
+    early = [k for group in members[:-1] for k in group]
+    hits_ref[...] = hits_of(members[-1])
+    hits = hits_of(early)
+    for tile in tiles(sum_ref.shape[1]):
+        sum_ref[:, tile] = mix(hits, gates, row_refs, tile, picks)
+
+
+def finish_kernel(picks, where_ref, sum_ref, hits_ref, columns_ref, *refs):
+    row_refs, out_ref = refs[:-1], refs[-1]
+    gates = columns_ref[:, picks : 2 * picks]
     for tile in tiles(out_ref.shape[1]):
-        arrived = jnp.concatenate([ref[:, tile] for ref in row_refs], axis=0)
-        chosen = jnp.dot(hits, arrived, preferred_element_type=jnp.float32)
-        total = None
-        for k in range(picks):
-            term = chosen[k * token_count : (k + 1) * token_count, :] * gates[:, k : k + 1]
-            total = term if total is None else total + term
+        total = sum_ref[:, tile] + mix(hits_ref[...], gates, row_refs, tile, picks)
         out_ref[:, tile] = total.astype(out_ref.dtype)
 
 
-def combine(row_blocks, ids, gates, where):
-    capacity, width = row_blocks[0].shape
+def combine(returned, members, ids, gates, where):
+    capacity, width = returned[0].shape
     picks, token_count = ids.shape
-    expert_count = len(row_blocks)
-    out = jax.ShapeDtypeStruct((token_count, width), row_blocks[0].dtype)
-    return call(
-        combine_kernel, (1,), [ids, gates, *row_blocks],
-        [whole_spec(ids.shape), whole_spec(gates.shape)]
-        + [whole_spec((capacity, width))] * expert_count,
-        out, whole_spec(out.shape),
-        2 * picks * expert_count * capacity * token_count * width, where,
+    early = [returned[k] for group in members[:-1] for k in group]
+    late = [returned[k] for k in members[-1]]
+    block = whole_spec((capacity, width))
+    outs = [
+        jax.ShapeDtypeStruct((token_count, width), jnp.float32),
+        jax.ShapeDtypeStruct((picks * token_count, len(late) * capacity), returned[0].dtype),
+        jax.ShapeDtypeStruct((token_count, 2 * picks + (-2 * picks % 8)), jnp.float32),
+    ]
+    flops = 2 * picks * capacity * token_count * width
+    begun = call(
+        functools.partial(begin_kernel, members), (1,), [ids, gates, *early],
+        [whole_spec(ids.shape), whole_spec(gates.shape)] + [block] * len(early),
+        outs, [whole_spec(out.shape) for out in outs], flops * len(early), where,
+    )
+    out = jax.ShapeDtypeStruct((token_count, width), returned[0].dtype)
+    return call(
+        functools.partial(finish_kernel, picks), (1,), [*begun, *late],
+        [whole_spec(x.shape) for x in outs] + [block] * len(late),
+        out, whole_spec(out.shape), flops * len(late), where,
     )
 
 
@@ -335,16 +380,17 @@
     arrived = [swap(outgoing[k], "exp", k) if k else outgoing[0] for k in range(expert_count)]
 
     returned = [None] * expert_count
-    for members in sets:
+    for s, members in enumerate(sets):
+        chunks = pack([arrived[k] for k in members], CHUNKS[s], where)
         pieces = [None] * ctx_size
-        pieces[0] = pack([arrived[k] for k in members], where)
+        pieces[0] = chunks
         for offset in evens:
-            pieces[offset] = swap(pieces[0], "ctx", offset)
+            pieces[offset] = [swap(chunk, "ctx", offset) for chunk in chunks]
         for offset in range(0, ctx_size, 2):
-            pieces[offset + 1] = swap(pieces[offset], "ctx", 1)
+            pieces[offset + 1] = [swap(chunk, "ctx", 1) for chunk in pieces[offset]]
         partial = mlp(pieces[:2], [0, 1], w_gate[0], w_up[0], None, where)
         hidden = mlp(pieces[2:], range(2, ctx_size), w_gate[0], w_up[0], partial, where)
-        hidden = lax.all_gather(hidden, "ctx", axis=0)
+        hidden = [hidden] + [swap(hidden, "ctx", offset) for offset in range(1, ctx_size)]
         blocks = down(hidden, w_down[0], down_parts, len(members), where)
         for k, block in zip(members, blocks):
             returned[k] = swap(block, "exp", k) if k else block
@@ -356,7 +402,7 @@
         keys[offset + 1] = swap(keys[offset], "ctx", 1)
     attended = attention(jnp.transpose(queries, (1, 2, 0)), keys, block_starts, w_uv, where)
     attended = jnp.transpose(attended, (1, 0, 2))
-    return attended, combine(returned, expert_ids.T, gate_weights.T, where)
+    return attended, combine(returned, sets, expert_ids.T, gate_weights.T, where)
 
 
 def solution(mesh):

time: 136 us -> 134 us (0.985)
  blocking collectives: 26.3 us -> 0 us
  waiting for transfers between devices: 55.1 us -> 70.4 us
  starting transfers between devices: 29.3 us -> 37.7 us
    all_gather x2 -> x0, blocking collectives: 26.3 us -> none  [layer(): hidden = lax.all_gather(hidden, 'ctx', axis=0)]
    ppermute x26 -> x35, waiting for transfers between devices: 55.1 us -> 70.4 us  [swap(): return lax.ppermute(x, axis, [(i, i ^ offset) for i in range(size)])]
    ppermute x26 -> x35, starting transfers between devices: 29.3 us -> 37.7 us  [swap(): return lax.ppermute(x, axis, [(i, i ^ offset) for i in range(size)])]
    pallas_call x12 -> x13, Pallas kernels: 21.3 us -> 22 us  [call(): pl.pallas_call(kernel, out_shape=out_shape, grid_spec=pltpu.PrefetchScala...]
  transfers between devices with their start and end apart: 26 -> 35, of which waited for: 11 -> 19; matrix products, arithmetic and copies ran while one was open for 1% -> 1% of each run, Pallas kernels for 13% -> 14%
where the time goes in v1:
time: 134 us
  waiting for transfers between devices  70.4 us (53%)
  starting transfers between devices  37.7 us (28%)
  Pallas kernels  22 us (16%)
  local copies, waits for them, and re-layouts  3.22 us (2%)
    ppermute x35, waiting for transfers between devices, swap(): return lax.ppermute(x, axis, [(i, i ^ offset) for i in range(size)])  70.4 us
    ppermute x35, starting transfers between devices, swap(): return lax.ppermute(x, axis, [(i, i ^ offset) for i in range(size)])  37.7 us
    pallas_call x13, Pallas kernels, call(): pl.pallas_call(kernel, out_shape=out_shape, grid_spec=pltpu.PrefetchScala...  22 us
    unnamed x23, local copies, waits for them, and re-layouts  3.22 us
  transfers between devices with their start and end apart: 35, of which 19 were waited for; matrix products, arithmetic and copies ran while one was open for 1% of the time, Pallas kernels for 14%

profile of v1, /device:TPU:0, one launch (start us, length us, event | category | flops | bytes accessed | tf_op | source)
XLA Modules:
  0.0 134.3 jit_solution(9324271215897417029)
XLA Ops:
  0.7 1.6 %copy-done.3 = bf16[128,7168]{1,0:T(8,128)(2,1)S(1)} copy-done((bf16[128,7168]{1,0:T(8,128)(2,1)S(1)}, bf16[128,7168]{1,0:T(8,128)(2,1)}, u32[]{:S(2)}) %copy-start.3) | copy-done | bytes 1835032
  4.2 3.1 %collective-permute-start.3 = (bf16[48,1792]{1,0:T(8,128)(2,1)S(1)}, bf16[48,1792]{1,0:T(8,128)(2,1)S(1)}, u32[]{:S(2)}, u32[]{:S(2)}) collective-permute-start(bf16[48,1792]{1,0:T(8,128)(2,1)S(1)} %get-tuple-element.26), channel_id=1, source_target_pairs={{0,2},{1,3},{2,0},{3,1},{4,6},{5,7},{6,4},{7,5},{8,10},{9,11},{10,... | collective-permute-start | bytes 516104 | tf_op jit(solution)/shard_map/ppermute | solution.py:20
  7.3 1.4 %collective-permute-start.4 = (bf16[48,1792]{1,0:T(8,128)(2,1)S(1)}, bf16[48,1792]{1,0:T(8,128)(2,1)S(1)}, u32[]{:S(2)}, u32[]{:S(2)}) collective-permute-start(bf16[48,1792]{1,0:T(8,128)(2,1)S(1)} %get-tuple-element.27), channel_id=1, source_target_pairs={{0,3},{1,2},{2,1},{3,0},{4,7},{5,6},{6,5},{7,4},{8,11},{9,10},{10,... | collective-permute-start | bytes 516104 | tf_op jit(solution)/shard_map/ppermute | solution.py:20
  8.7 3.6 %collective-permute-start.5 = (bf16[48,1792]{1,0:T(8,128)(2,1)S(1)}, bf16[48,1792]{1,0:T(8,128)(2,1)S(1)}, u32[]{:S(2)}, u32[]{:S(2)}) collective-permute-start(bf16[48,1792]{1,0:T(8,128)(2,1)S(1)} %get-tuple-element.28), channel_id=1, source_target_pairs={{0,6},{1,7},{2,4},{3,5},{4,2},{5,3},{6,0},{7,1},{8,14},{9,15},{10,... | collective-permute-start | bytes 516104 | tf_op jit(solution)/shard_map/ppermute | solution.py:20
  12.6 3.9 %collective-permute-done.4.refs_1_ = bf16[48,1792]{1,0:T(8,128)(2,1)S(1)} collective-permute-done((bf16[48,1792]{1,0:T(8,128)(2,1)S(1)}, bf16[48,1792]{1,0:T(8,128)(2,1)S(1)}, u32[]{:S(2)}, u32[]{:S(2)}) %collective-permute-start.4) | collective-permute-done | bytes 172064 | tf_op jit(solution)/shard_map/ppermute | solution.py:20
  16.5 6.2 %collective-permute-done.5.refs_2_ = bf16[48,1792]{1,0:T(8,128)(2,1)S(1)} collective-permute-done((bf16[48,1792]{1,0:T(8,128)(2,1)S(1)}, bf16[48,1792]{1,0:T(8,128)(2,1)S(1)}, u32[]{:S(2)}, u32[]{:S(2)}) %collective-permute-start.5) | collective-permute-done | bytes 172064 | tf_op jit(solution)/shard_map/ppermute | solution.py:20
  22.7 3.4 %collective-permute-done.6.refs_3_ = bf16[48,1792]{1,0:T(8,128)(2,1)S(1)} collective-permute-done((bf16[48,1792]{1,0:T(8,128)(2,1)S(1)}, bf16[48,1792]{1,0:T(8,128)(2,1)S(1)}, u32[]{:S(2)}, u32[]{:S(2)}) %collective-permute-start.6) | collective-permute-done | bytes 172064 | tf_op jit(solution)/shard_map/ppermute | solution.py:20
  26.7 1.6 %collective-permute-start.7 = (bf16[192,1792]{1,0:T(8,128)(2,1)S(1)}, bf16[192,1792]{1,0:T(8,128)(2,1)S(1)}, u32[]{:S(2)}, u32[]{:S(2)}) collective-permute-start(bf16[192,1792]{1,0:T(8,128)(2,1)S(1)} %shard_map.115.refs_4_), channel_id=1, source_target_pairs={{0,16},{8,24},{16,0},{24,8},{1,17},{9,25},{17,1},{25,9},{2,18},{10... | collective-permute-start | bytes 2064392 | tf_op jit(solution)/shard_map/ppermute | solution.py:20
  28.9 2.7 %collective-permute-start.21 = (bf16[48,1792]{1,0:T(8,128)(2,1)S(1)}, bf16[48,1792]{1,0:T(8,128)(2,1)S(1)}, u32[]{:S(2)}, u32[]{:S(2)}) collective-permute-start(bf16[48,1792]{1,0:T(8,128)(2,1)S(1)} %get-tuple-element.42), channel_id=1, source_target_pairs={{0,4},{1,5},{2,6},{3,7},{4,0},{5,1},{6,2},{7,3},{8,12},{9,13},{10,... | collective-permute-start | bytes 516104 | tf_op jit(solution)/shard_map/ppermute | solution.py:20
  33.6 2.8 %collective-permute-start.22 = (bf16[48,1792]{1,0:T(8,128)(2,1)S(1)}, bf16[48,1792]{1,0:T(8,128)(2,1)S(1)}, u32[]{:S(2)}, u32[]{:S(2)}) collective-permute-start(bf16[48,1792]{1,0:T(8,128)(2,1)S(1)} %get-tuple-element.43), channel_id=1, source_target_pairs={{0,5},{1,4},{2,7},{3,6},{4,1},{5,0},{6,3},{7,2},{8,13},{9,12},{10,... | collective-permute-start | bytes 516104 | tf_op jit(solution)/shard_map/ppermute | solution.py:20
  36.4 4.9 %collective-permute-done.21.refs_2_ = bf16[48,1792]{1,0:T(8,128)(2,1)S(1)} collective-permute-done((bf16[48,1792]{1,0:T(8,128)(2,1)S(1)}, bf16[48,1792]{1,0:T(8,128)(2,1)S(1)}, u32[]{:S(2)}, u32[]{:S(2)}) %collective-permute-start.21) | collective-permute-done | bytes 172064 | tf_op jit(solution)/shard_map/ppermute | solution.py:20
  41.3 3.7 %collective-permute-done.7.refs_4_ = bf16[192,1792]{1,0:T(8,128)(2,1)S(1)} collective-permute-done((bf16[192,1792]{1,0:T(8,128)(2,1)S(1)}, bf16[192,1792]{1,0:T(8,128)(2,1)S(1)}, u32[]{:S(2)}, u32[]{:S(2)}) %collective-permute-start.7) | collective-permute-done | bytes 688160 | tf_op jit(solution)/shard_map/ppermute | solution.py:20
  45.2 1.4 %collective-permute-start.1 = (bf16[576,128]{1,0:T(8,128)(2,1)S(1)}, bf16[576,128]{1,0:T(8,128)(2,1)S(1)}, u32[]{:S(2)}, u32[]{:S(2)}) collective-permute-start(bf16[576,128]{1,0:T(8,128)(2,1)S(1)} %bitcast.36), channel_id=1, source_target_pairs={{0,16},{8,24},{16,0},{24,8},{1,17},{9,25},{17,1},{25,9},{2,18},{10... | collective-permute-start | bytes 442376 | tf_op jit(solution)/shard_map/ppermute | solution.py:20
  47.2 8.8 %collective-permute-done.1.refs_2_ = bf16[576,128]{1,0:T(8,128)(2,1)S(1)} collective-permute-done((bf16[576,128]{1,0:T(8,128)(2,1)S(1)}, bf16[576,128]{1,0:T(8,128)(2,1)S(1)}, u32[]{:S(2)}, u32[]{:S(2)}) %collective-permute-start.1) | collective-permute-done | bytes 147488 | tf_op jit(solution)/shard_map/ppermute | solution.py:20
  56.0 1.5 %collective-permute-start.23 = (bf16[96,1792]{1,0:T(8,128)(2,1)S(1)}, bf16[96,1792]{1,0:T(8,128)(2,1)S(1)}, u32[]{:S(2)}, u32[]{:S(2)}) collective-permute-start(bf16[96,1792]{1,0:T(8,128)(2,1)S(1)} %get-tuple-element.44.refs_4_), channel_id=1, source_target_pairs={{0,16},{8,24},{16,0},{24,8},{1,17},{9,25},{17,1},{25,9},{2,18},{10... | collective-permute-start | bytes 1032200 | tf_op jit(solution)/shard_map/ppermute | solution.py:20
  58.1 8.9 %collective-permute-done.23.refs_4_ = bf16[96,1792]{1,0:T(8,128)(2,1)S(1)} collective-permute-done((bf16[96,1792]{1,0:T(8,128)(2,1)S(1)}, bf16[96,1792]{1,0:T(8,128)(2,1)S(1)}, u32[]{:S(2)}, u32[]{:S(2)}) %collective-permute-start.23) | collective-permute-done | bytes 344096 | tf_op jit(solution)/shard_map/ppermute | solution.py:20
  67.0 7.4 %collective-permute-done.24.refs_5_ = bf16[96,1792]{1,0:T(8,128)(2,1)S(1)} collective-permute-done((bf16[96,1792]{1,0:T(8,128)(2,1)S(1)}, bf16[96,1792]{1,0:T(8,128)(2,1)S(1)}, u32[]{:S(2)}, u32[]{:S(2)}) %collective-permute-start.24) | collective-permute-done | bytes 344096 | tf_op jit(solution)/shard_map/ppermute | solution.py:20
  77.1 3.2 %collective-permute-done.15.refs_7_ = bf16[128,1792]{1,0:T(8,128)(2,1)S(1)} collective-permute-done((bf16[128,1792]{1,0:T(8,128)(2,1)S(1)}, bf16[128,1792]{1,0:T(8,128)(2,1)S(1)}, u32[]{:S(2)}, u32[]{:S(2)}) %collective-permute-start.15) | collective-permute-done | bytes 458784 | tf_op jit(solution)/shard_map/ppermute | solution.py:20
  80.4 1.9 %collective-permute-start.12 = (bf16[192,128]{1,0:T(8,128)(2,1)S(1)}, bf16[192,128]{1,0:T(8,128)(2,1)S(1)}, u32[]{:S(2)}, u32[]{:S(2)}) collective-permute-start(bf16[192,128]{1,0:T(8,128)(2,1)S(1)} %shard_map.117.refs_0_), channel_id=1, source_target_pairs={{0,24},{8,16},{16,8},{24,0},{1,25},{9,17},{17,9},{25,1},{2,26},{10... | collective-permute-start | bytes 147464 | tf_op jit(solution)/shard_map/ppermute | solution.py:20
  82.3 1.8 %collective-permute-done.12.refs_3_ = bf16[192,128]{1,0:T(8,128)(2,1)S(1)} collective-permute-done((bf16[192,128]{1,0:T(8,128)(2,1)S(1)}, bf16[192,128]{1,0:T(8,128)(2,1)S(1)}, u32[]{:S(2)}, u32[]{:S(2)}) %collective-permute-start.12) | collective-permute-done | bytes 49184 | tf_op jit(solution)/shard_map/ppermute | solution.py:20
  84.5 3.8 %collective-permute-done.11.refs_2_ = bf16[192,128]{1,0:T(8,128)(2,1)S(1)} collective-permute-done((bf16[192,128]{1,0:T(8,128)(2,1)S(1)}, bf16[192,128]{1,0:T(8,128)(2,1)S(1)}, u32[]{:S(2)}, u32[]{:S(2)}) %collective-permute-start.11) | collective-permute-done | bytes 49184 | tf_op jit(solution)/shard_map/ppermute | solution.py:20
  90.9 2.0 %collective-permute-start.17 = (bf16[48,1792]{1,0:T(8,128)(2,1)S(1)}, bf16[48,1792]{1,0:T(8,128)(2,1)S(1)}, u32[]{:S(2)}, u32[]{:S(2)}) collective-permute-start(bf16[48,1792]{1,0:T(8,128)(2,1)S(1)} %get-tuple-element.34), channel_id=1, source_target_pairs={{0,3},{1,2},{2,1},{3,0},{4,7},{5,6},{6,5},{7,4},{8,11},{9,10},{10,... | collective-permute-start | bytes 516104 | tf_op jit(solution)/shard_map/ppermute | solution.py:20
  96.0 1.4 %collective-permute-start.30 = (bf16[192,128]{1,0:T(8,128)(2,1)S(1)}, bf16[192,128]{1,0:T(8,128)(2,1)S(1)}, u32[]{:S(2)}, u32[]{:S(2)}) collective-permute-start(bf16[192,128]{1,0:T(8,128)(2,1)S(1)} %shard_map.123.refs_0_), channel_id=1, source_target_pairs={{0,16},{8,24},{16,0},{24,8},{1,17},{9,25},{17,1},{25,9},{2,18},{10... | collective-permute-start | bytes 147464 | tf_op jit(solution)/shard_map/ppermute | solution.py:20
  97.4 1.4 %collective-permute-done.31.refs_3_ = bf16[192,128]{1,0:T(8,128)(2,1)S(1)} collective-permute-done((bf16[192,128]{1,0:T(8,128)(2,1)S(1)}, bf16[192,128]{1,0:T(8,128)(2,1)S(1)}, u32[]{:S(2)}, u32[]{:S(2)}) %collective-permute-start.31) | collective-permute-done | bytes 49184 | tf_op jit(solution)/shard_map/ppermute | solution.py:20
  100.3 1.3 collective-permute-start.18
  101.7 3.4 %collective-permute-start.19 = (bf16[48,1792]{1,0:T(8,128)(2,1)S(1)}, bf16[48,1792]{1,0:T(8,128)(2,1)S(1)}, u32[]{:S(2)}, u32[]{:S(2)}) collective-permute-start(bf16[48,1792]{1,0:T(8,128)(2,1)S(1)} %get-tuple-element.36), channel_id=1, source_target_pairs={{0,7},{1,6},{2,5},{3,4},{4,3},{5,2},{6,1},{7,0},{8,15},{9,14},{10,... | collective-permute-start | bytes 516104 | tf_op jit(solution)/shard_map/ppermute | solution.py:20
  106.8 3.8 %collective-permute-start.34 = (bf16[48,1792]{1,0:T(8,128)(2,1)S(1)}, bf16[48,1792]{1,0:T(8,128)(2,1)S(1)}, u32[]{:S(2)}, u32[]{:S(2)}) collective-permute-start(bf16[48,1792]{1,0:T(8,128)(2,1)S(1)} %get-tuple-element.49), channel_id=1, source_target_pairs={{0,5},{1,4},{2,7},{3,6},{4,1},{5,0},{6,3},{7,2},{8,13},{9,12},{10,... | collective-permute-start | bytes 516104 | tf_op jit(solution)/shard_map/ppermute | solution.py:20
  110.7 9.3 %shard_map.113 = bf16[8,128,128]{2,1,0:T(8,128)(2,1)S(1)} custom-call(s32[2]{0:T(128)S(1)} %pad_add_fusion.where_ref, s32[8]{0:T(128)S(1)} %copy-done.10, bf16[8,576,128]{2,1,0:T(8,128)(2,1)S(1)} %bitcast.35, bf16[8,512,128]{2,1,0:T(8,128)(2,1)S(1)} %copy-done.8, bf16[576,128]{1,0:T(8,128)(2,1)S(1)} %bitcast.38, ...), custom_call_target="tpu_custom_call" | custom-call | flops 1207959552 | bytes 3080192 | tf_op jit(solution)/shard_map/pallas_call | solution.py:43
  120.9 1.4 %shard_map.120 = (f32[128,1792]{1,0:T(8,128)S(1)}, bf16[256,192]{1,0:T(8,128)(2,1)S(1)}, f32[128,8]{1,0:T(8,128)S(1)}) custom-call(s32[2]{0:T(128)S(1)} %pad_add_fusion.where_ref, s32[2,128]{1,0:T(2,128)S(1)} %bitcast.33, f32[2,128]{1,0:T(2,128)S(1)} %bitcast.34, bf16[48,1792]{1,0:T(8,128)(2,1)S(1)} %collective-permute-done.16.refs_0_, ...), custom_call_target="tpu_custom_call" | custom-call | flops 176160768 | bytes 1710080 | tf_op jit(solution)/shard_map/pallas_call | solution.py:43
  122.4 7.0 %collective-permute-done.33.refs_2_ = bf16[48,1792]{1,0:T(8,128)(2,1)S(1)} collective-permute-done((bf16[48,1792]{1,0:T(8,128)(2,1)S(1)}, bf16[48,1792]{1,0:T(8,128)(2,1)S(1)}, u32[]{:S(2)}, u32[]{:S(2)}) %collective-permute-start.33) | collective-permute-done | bytes 172064 | tf_op jit(solution)/shard_map/ppermute | solution.py:20
  129.3 3.2 %collective-permute-done.34.refs_3_ = bf16[48,1792]{1,0:T(8,128)(2,1)S(1)} collective-permute-done((bf16[48,1792]{1,0:T(8,128)(2,1)S(1)}, bf16[48,1792]{1,0:T(8,128)(2,1)S(1)}, u32[]{:S(2)}, u32[]{:S(2)}) %collective-permute-start.34) | collective-permute-done | bytes 172064 | tf_op jit(solution)/shard_map/ppermute | solution.py:20
  132.5 1.7 %shard_map.125 = bf16[128,1792]{1,0:T(8,128)(2,1)} custom-call(s32[2]{0:T(128)S(1)} %pad_add_fusion.where_ref, f32[128,1792]{1,0:T(8,128)S(1)} %get-tuple-element.37.sum_ref, bf16[256,192]{1,0:T(8,128)(2,1)S(1)} %get-tuple-element.38.hits_ref, f32[128,8]{1,0:T(8,128)S(1)} %get-tuple-element.39.columns_ref, bf16[48,1792]{1,0:T(8,128)(2,1)S(1)} %get-tuple-element.46.refs_0_, ...), custom_call_target="tpu_custom_call" | custom-call | flops 176160768 | bytes 2166784 | tf_op jit(solution)/shard_map/pallas_call | solution.py:43
  (75 shorter events, 19.8 us)
Async XLA Ops:
  4.2 8.3 %collective-permute-start.3 = (bf16[48,1792]{1,0:T(8,128)(2,1)S(1)}, bf16[48,1792]{1,0:T(8,128)(2,1)S(1)}, u32[]{:S(2)}, u32[]{:S(2)}) collective-permute-start(bf16[48,1792]{1,0:T(8,128)(2,1)S(1)} %get-tuple-element.26), channel_id=1, source_target_pairs={{0,2},{1,3},{2,0},{3,1},{4,6},{5,7},{6,4},{7,5},{8,10},{9,11},{10,... | collective-permute-start | bytes 516104 | tf_op jit(solution)/shard_map/ppermute | solution.py:20
  7.3 9.2 %collective-permute-start.4 = (bf16[48,1792]{1,0:T(8,128)(2,1)S(1)}, bf16[48,1792]{1,0:T(8,128)(2,1)S(1)}, u32[]{:S(2)}, u32[]{:S(2)}) collective-permute-start(bf16[48,1792]{1,0:T(8,128)(2,1)S(1)} %get-tuple-element.27), channel_id=1, source_target_pairs={{0,3},{1,2},{2,1},{3,0},{4,7},{5,6},{6,5},{7,4},{8,11},{9,10},{10,... | collective-permute-start | bytes 516104 | tf_op jit(solution)/shard_map/ppermute | solution.py:20
  8.7 14.0 %collective-permute-start.5 = (bf16[48,1792]{1,0:T(8,128)(2,1)S(1)}, bf16[48,1792]{1,0:T(8,128)(2,1)S(1)}, u32[]{:S(2)}, u32[]{:S(2)}) collective-permute-start(bf16[48,1792]{1,0:T(8,128)(2,1)S(1)} %get-tuple-element.28), channel_id=1, source_target_pairs={{0,6},{1,7},{2,4},{3,5},{4,2},{5,3},{6,0},{7,1},{8,14},{9,15},{10,... | collective-permute-start | bytes 516104 | tf_op jit(solution)/shard_map/ppermute | solution.py:20
  12.3 13.7 %collective-permute-start.6 = (bf16[48,1792]{1,0:T(8,128)(2,1)S(1)}, bf16[48,1792]{1,0:T(8,128)(2,1)S(1)}, u32[]{:S(2)}, u32[]{:S(2)}) collective-permute-start(bf16[48,1792]{1,0:T(8,128)(2,1)S(1)} %get-tuple-element.29), channel_id=1, source_target_pairs={{0,7},{1,6},{2,5},{3,4},{4,3},{5,2},{6,1},{7,0},{8,15},{9,14},{10,... | collective-permute-start | bytes 516104 | tf_op jit(solution)/shard_map/ppermute | solution.py:20
  26.7 18.4 %collective-permute-start.7 = (bf16[192,1792]{1,0:T(8,128)(2,1)S(1)}, bf16[192,1792]{1,0:T(8,128)(2,1)S(1)}, u32[]{:S(2)}, u32[]{:S(2)}) collective-permute-start(bf16[192,1792]{1,0:T(8,128)(2,1)S(1)} %shard_map.115.refs_4_), channel_id=1, source_target_pairs={{0,16},{8,24},{16,0},{24,8},{1,17},{9,25},{17,1},{25,9},{2,18},{10... | collective-permute-start | bytes 2064392 | tf_op jit(solution)/shard_map/ppermute | solution.py:20
  28.2 5.4 %collective-permute-start.20 = (bf16[48,1792]{1,0:T(8,128)(2,1)S(1)}, bf16[48,1792]{1,0:T(8,128)(2,1)S(1)}, u32[]{:S(2)}, u32[]{:S(2)}) collective-permute-start(bf16[48,1792]{1,0:T(8,128)(2,1)S(1)} %get-tuple-element.41), channel_id=1, source_target_pairs={{0,1},{1,0},{2,3},{3,2},{4,5},{5,4},{6,7},{7,6},{8,9},{9,8},{10,11... | collective-permute-start | bytes 516104 | tf_op jit(solution)/shard_map/ppermute | solution.py:20
  28.9 12.4 %collective-permute-start.21 = (bf16[48,1792]{1,0:T(8,128)(2,1)S(1)}, bf16[48,1792]{1,0:T(8,128)(2,1)S(1)}, u32[]{:S(2)}, u32[]{:S(2)}) collective-permute-start(bf16[48,1792]{1,0:T(8,128)(2,1)S(1)} %get-tuple-element.42), channel_id=1, source_target_pairs={{0,4},{1,5},{2,6},{3,7},{4,0},{5,1},{6,2},{7,3},{8,12},{9,13},{10,... | collective-permute-start | bytes 516104 | tf_op jit(solution)/shard_map/ppermute | solution.py:20
  32.2 25.3 %collective-permute-start.13 = (bf16[128,1792]{1,0:T(8,128)(2,1)S(1)}, bf16[128,1792]{1,0:T(8,128)(2,1)S(1)}, u32[]{:S(2)}, u32[]{:S(2)}) collective-permute-start(bf16[128,1792]{1,0:T(8,128)(2,1)S(1)} %get-tuple-element.30), channel_id=1, source_target_pairs={{0,8},{8,0},{16,24},{24,16},{1,9},{9,1},{17,25},{25,17},{2,10},{10... | collective-permute-start | bytes 1376264 | tf_op jit(solution)/shard_map/ppermute | solution.py:20
  32.3 25.8 %collective-permute-start.14 = (bf16[128,1792]{1,0:T(8,128)(2,1)S(1)}, bf16[128,1792]{1,0:T(8,128)(2,1)S(1)}, u32[]{:S(2)}, u32[]{:S(2)}) collective-permute-start(bf16[128,1792]{1,0:T(8,128)(2,1)S(1)} %get-tuple-element.31), channel_id=1, source_target_pairs={{0,16},{8,24},{16,0},{24,8},{1,17},{9,25},{17,1},{25,9},{2,18},{10... | collective-permute-start | bytes 1376264 | tf_op jit(solution)/shard_map/ppermute | solution.py:20
  33.6 11.6 %collective-permute-start.22 = (bf16[48,1792]{1,0:T(8,128)(2,1)S(1)}, bf16[48,1792]{1,0:T(8,128)(2,1)S(1)}, u32[]{:S(2)}, u32[]{:S(2)}) collective-permute-start(bf16[48,1792]{1,0:T(8,128)(2,1)S(1)} %get-tuple-element.43), channel_id=1, source_target_pairs={{0,5},{1,4},{2,7},{3,6},{4,1},{5,0},{6,3},{7,2},{8,13},{9,12},{10,... | collective-permute-start | bytes 516104 | tf_op jit(solution)/shard_map/ppermute | solution.py:20
  41.3 33.0 %collective-permute-start.9 = (bf16[192,1792]{1,0:T(8,128)(2,1)S(1)}, bf16[192,1792]{1,0:T(8,128)(2,1)S(1)}, u32[]{:S(2)}, u32[]{:S(2)}) collective-permute-start(bf16[192,1792]{1,0:T(8,128)(2,1)S(1)} %shard_map.115.refs_4_), channel_id=1, source_target_pairs={{0,8},{8,0},{16,24},{24,16},{1,9},{9,1},{17,25},{25,17},{2,10},{10... | collective-permute-start | bytes 2064392 | tf_op jit(solution)/shard_map/ppermute | solution.py:20
  45.0 29.8 %collective-permute-start.8 = (bf16[192,1792]{1,0:T(8,128)(2,1)S(1)}, bf16[192,1792]{1,0:T(8,128)(2,1)S(1)}, u32[]{:S(2)}, u32[]{:S(2)}) collective-permute-start(bf16[192,1792]{1,0:T(8,128)(2,1)S(1)} %collective-permute-done.7.refs_4_), channel_id=1, source_target_pairs={{0,8},{8,0},{16,24},{24,16},{1,9},{9,1},{17,25},{25,17},{2,10},{10... | collective-permute-start | bytes 2064392 | tf_op jit(solution)/shard_map/ppermute | solution.py:20
  45.2 10.8 %collective-permute-start.1 = (bf16[576,128]{1,0:T(8,128)(2,1)S(1)}, bf16[576,128]{1,0:T(8,128)(2,1)S(1)}, u32[]{:S(2)}, u32[]{:S(2)}) collective-permute-start(bf16[576,128]{1,0:T(8,128)(2,1)S(1)} %bitcast.36), channel_id=1, source_target_pairs={{0,16},{8,24},{16,0},{24,8},{1,17},{9,25},{17,1},{25,9},{2,18},{10... | collective-permute-start | bytes 442376 | tf_op jit(solution)/shard_map/ppermute | solution.py:20
  56.0 10.9 %collective-permute-start.23 = (bf16[96,1792]{1,0:T(8,128)(2,1)S(1)}, bf16[96,1792]{1,0:T(8,128)(2,1)S(1)}, u32[]{:S(2)}, u32[]{:S(2)}) collective-permute-start(bf16[96,1792]{1,0:T(8,128)(2,1)S(1)} %get-tuple-element.44.refs_4_), channel_id=1, source_target_pairs={{0,16},{8,24},{16,0},{24,8},{1,17},{9,25},{17,1},{25,9},{2,18},{10... | collective-permute-start | bytes 1032200 | tf_op jit(solution)/shard_map/ppermute | solution.py:20
  57.5 16.8 %collective-permute-start.24 = (bf16[96,1792]{1,0:T(8,128)(2,1)S(1)}, bf16[96,1792]{1,0:T(8,128)(2,1)S(1)}, u32[]{:S(2)}, u32[]{:S(2)}) collective-permute-start(bf16[96,1792]{1,0:T(8,128)(2,1)S(1)} %get-tuple-element.45.refs_5_), channel_id=1, source_target_pairs={{0,16},{8,24},{16,0},{24,8},{1,17},{9,25},{17,1},{25,9},{2,18},{10... | collective-permute-start | bytes 1032200 | tf_op jit(solution)/shard_map/ppermute | solution.py:20
  58.1 22.3 %collective-permute-start.15 = (bf16[128,1792]{1,0:T(8,128)(2,1)S(1)}, bf16[128,1792]{1,0:T(8,128)(2,1)S(1)}, u32[]{:S(2)}, u32[]{:S(2)}) collective-permute-start(bf16[128,1792]{1,0:T(8,128)(2,1)S(1)} %get-tuple-element.32), channel_id=1, source_target_pairs={{0,24},{8,16},{16,8},{24,0},{1,25},{9,17},{17,9},{25,1},{2,26},{10... | collective-permute-start | bytes 1376264 | tf_op jit(solution)/shard_map/ppermute | solution.py:20
  67.0 23.8 %collective-permute-start.27 = (bf16[96,1792]{1,0:T(8,128)(2,1)S(1)}, bf16[96,1792]{1,0:T(8,128)(2,1)S(1)}, u32[]{:S(2)}, u32[]{:S(2)}) collective-permute-start(bf16[96,1792]{1,0:T(8,128)(2,1)S(1)} %get-tuple-element.44.refs_4_), channel_id=1, source_target_pairs={{0,8},{8,0},{16,24},{24,16},{1,9},{9,1},{17,25},{25,17},{2,10},{10... | collective-permute-start | bytes 1032200 | tf_op jit(solution)/shard_map/ppermute | solution.py:20
  74.3 16.5 %collective-permute-start.28 = (bf16[96,1792]{1,0:T(8,128)(2,1)S(1)}, bf16[96,1792]{1,0:T(8,128)(2,1)S(1)}, u32[]{:S(2)}, u32[]{:S(2)}) collective-permute-start(bf16[96,1792]{1,0:T(8,128)(2,1)S(1)} %get-tuple-element.45.refs_5_), channel_id=1, source_target_pairs={{0,8},{8,0},{16,24},{24,16},{1,9},{9,1},{17,25},{25,17},{2,10},{10... | collective-permute-start | bytes 1032200 | tf_op jit(solution)/shard_map/ppermute | solution.py:20
  74.3 19.6 %collective-permute-start.25 = (bf16[96,1792]{1,0:T(8,128)(2,1)S(1)}, bf16[96,1792]{1,0:T(8,128)(2,1)S(1)}, u32[]{:S(2)}, u32[]{:S(2)}) collective-permute-start(bf16[96,1792]{1,0:T(8,128)(2,1)S(1)} %collective-permute-done.23.refs_4_), channel_id=1, source_target_pairs={{0,8},{8,0},{16,24},{24,16},{1,9},{9,1},{17,25},{25,17},{2,10},{10... | collective-permute-start | bytes 1032200 | tf_op jit(solution)/shard_map/ppermute | solution.py:20
  74.8 19.2 %collective-permute-start.26 = (bf16[96,1792]{1,0:T(8,128)(2,1)S(1)}, bf16[96,1792]{1,0:T(8,128)(2,1)S(1)}, u32[]{:S(2)}, u32[]{:S(2)}) collective-permute-start(bf16[96,1792]{1,0:T(8,128)(2,1)S(1)} %collective-permute-done.24.refs_5_), channel_id=1, source_target_pairs={{0,8},{8,0},{16,24},{24,16},{1,9},{9,1},{17,25},{25,17},{2,10},{10... | collective-permute-start | bytes 1032200 | tf_op jit(solution)/shard_map/ppermute | solution.py:20
  80.4 3.7 %collective-permute-start.12 = (bf16[192,128]{1,0:T(8,128)(2,1)S(1)}, bf16[192,128]{1,0:T(8,128)(2,1)S(1)}, u32[]{:S(2)}, u32[]{:S(2)}) collective-permute-start(bf16[192,128]{1,0:T(8,128)(2,1)S(1)} %shard_map.117.refs_0_), channel_id=1, source_target_pairs={{0,24},{8,16},{16,8},{24,0},{1,25},{9,17},{17,9},{25,1},{2,26},{10... | collective-permute-start | bytes 147464 | tf_op jit(solution)/shard_map/ppermute | solution.py:20
  84.0 4.3 %collective-permute-start.11 = (bf16[192,128]{1,0:T(8,128)(2,1)S(1)}, bf16[192,128]{1,0:T(8,128)(2,1)S(1)}, u32[]{:S(2)}, u32[]{:S(2)}) collective-permute-start(bf16[192,128]{1,0:T(8,128)(2,1)S(1)} %shard_map.117.refs_0_), channel_id=1, source_target_pairs={{0,16},{8,24},{16,0},{24,8},{1,17},{9,25},{17,1},{25,9},{2,18},{10... | collective-permute-start | bytes 147464 | tf_op jit(solution)/shard_map/ppermute | solution.py:20
  89.5 6.5 %collective-permute-start = (bf16[576,128]{1,0:T(8,128)(2,1)S(1)}, bf16[576,128]{1,0:T(8,128)(2,1)S(1)}, u32[]{:S(2)}, u32[]{:S(2)}) collective-permute-start(bf16[576,128]{1,0:T(8,128)(2,1)S(1)} %bitcast.37), channel_id=1, source_target_pairs={{0,8},{8,0},{16,24},{24,16},{1,9},{9,1},{17,25},{25,17},{2,10},{10... | collective-permute-start | bytes 442376 | tf_op jit(solution)/shard_map/ppermute | solution.py:20
  90.8 16.0 %collective-permute-start.16 = (bf16[48,1792]{1,0:T(8,128)(2,1)S(1)}, bf16[48,1792]{1,0:T(8,128)(2,1)S(1)}, u32[]{:S(2)}, u32[]{:S(2)}) collective-permute-start(bf16[48,1792]{1,0:T(8,128)(2,1)S(1)} %get-tuple-element.33), channel_id=1, source_target_pairs={{0,2},{1,3},{2,0},{3,1},{4,6},{5,7},{6,4},{7,5},{8,10},{9,11},{10,... | collective-permute-start | bytes 516104 | tf_op jit(solution)/shard_map/ppermute | solution.py:20
  90.9 15.9 %collective-permute-start.17 = (bf16[48,1792]{1,0:T(8,128)(2,1)S(1)}, bf16[48,1792]{1,0:T(8,128)(2,1)S(1)}, u32[]{:S(2)}, u32[]{:S(2)}) collective-permute-start(bf16[48,1792]{1,0:T(8,128)(2,1)S(1)} %get-tuple-element.34), channel_id=1, source_target_pairs={{0,3},{1,2},{2,1},{3,0},{4,7},{5,6},{6,5},{7,4},{8,11},{9,10},{10,... | collective-permute-start | bytes 516104 | tf_op jit(solution)/shard_map/ppermute | solution.py:20
  94.0 12.2 %collective-permute-start.2 = (bf16[576,128]{1,0:T(8,128)(2,1)S(1)}, bf16[576,128]{1,0:T(8,128)(2,1)S(1)}, u32[]{:S(2)}, u32[]{:S(2)}) collective-permute-start(bf16[576,128]{1,0:T(8,128)(2,1)S(1)} %collective-permute-done.1.refs_2_), channel_id=1, source_target_pairs={{0,8},{8,0},{16,24},{24,16},{1,9},{9,1},{17,25},{25,17},{2,10},{10... | collective-permute-start | bytes 442376 | tf_op jit(solution)/shard_map/ppermute | solution.py:20
  96.0 4.4 %collective-permute-start.30 = (bf16[192,128]{1,0:T(8,128)(2,1)S(1)}, bf16[192,128]{1,0:T(8,128)(2,1)S(1)}, u32[]{:S(2)}, u32[]{:S(2)}) collective-permute-start(bf16[192,128]{1,0:T(8,128)(2,1)S(1)} %shard_map.123.refs_0_), channel_id=1, source_target_pairs={{0,16},{8,24},{16,0},{24,8},{1,17},{9,25},{17,1},{25,9},{2,18},{10... | collective-permute-start | bytes 147464 | tf_op jit(solution)/shard_map/ppermute | solution.py:20
  100.3 20.5 %collective-permute-start.18 = (bf16[48,1792]{1,0:T(8,128)(2,1)S(1)}, bf16[48,1792]{1,0:T(8,128)(2,1)S(1)}, u32[]{:S(2)}, u32[]{:S(2)}) collective-permute-start(bf16[48,1792]{1,0:T(8,128)(2,1)S(1)} %get-tuple-element.35), channel_id=1, source_target_pairs={{0,6},{1,7},{2,4},{3,5},{4,2},{5,3},{6,0},{7,1},{8,14},{9,15},{10,... | collective-permute-start | bytes 516104 | tf_op jit(solution)/shard_map/ppermute | solution.py:20
  101.7 19.2 %collective-permute-start.19 = (bf16[48,1792]{1,0:T(8,128)(2,1)S(1)}, bf16[48,1792]{1,0:T(8,128)(2,1)S(1)}, u32[]{:S(2)}, u32[]{:S(2)}) collective-permute-start(bf16[48,1792]{1,0:T(8,128)(2,1)S(1)} %get-tuple-element.36), channel_id=1, source_target_pairs={{0,7},{1,6},{2,5},{3,4},{4,3},{5,2},{6,1},{7,0},{8,15},{9,14},{10,... | collective-permute-start | bytes 516104 | tf_op jit(solution)/shard_map/ppermute | solution.py:20
  106.2 16.2 %collective-permute-start.32 = (bf16[48,1792]{1,0:T(8,128)(2,1)S(1)}, bf16[48,1792]{1,0:T(8,128)(2,1)S(1)}, u32[]{:S(2)}, u32[]{:S(2)}) collective-permute-start(bf16[48,1792]{1,0:T(8,128)(2,1)S(1)} %get-tuple-element.47), channel_id=1, source_target_pairs={{0,1},{1,0},{2,3},{3,2},{4,5},{5,4},{6,7},{7,6},{8,9},{9,8},{10,11... | collective-permute-start | bytes 516104 | tf_op jit(solution)/shard_map/ppermute | solution.py:20
  106.8 22.6 %collective-permute-start.33 = (bf16[48,1792]{1,0:T(8,128)(2,1)S(1)}, bf16[48,1792]{1,0:T(8,128)(2,1)S(1)}, u32[]{:S(2)}, u32[]{:S(2)}) collective-permute-start(bf16[48,1792]{1,0:T(8,128)(2,1)S(1)} %get-tuple-element.48), channel_id=1, source_target_pairs={{0,4},{1,5},{2,6},{3,7},{4,0},{5,1},{6,2},{7,3},{8,12},{9,13},{10,... | collective-permute-start | bytes 516104 | tf_op jit(solution)/shard_map/ppermute | solution.py:20
  106.8 25.7 %collective-permute-start.34 = (bf16[48,1792]{1,0:T(8,128)(2,1)S(1)}, bf16[48,1792]{1,0:T(8,128)(2,1)S(1)}, u32[]{:S(2)}, u32[]{:S(2)}) collective-permute-start(bf16[48,1792]{1,0:T(8,128)(2,1)S(1)} %get-tuple-element.49), channel_id=1, source_target_pairs={{0,5},{1,4},{2,7},{3,6},{4,1},{5,0},{6,3},{7,2},{8,13},{9,12},{10,... | collective-permute-start | bytes 516104 | tf_op jit(solution)/shard_map/ppermute | solution.py:20
  (14 other events, 208.3 us)

commit v2 on v1

--- a/solution.py
+++ b/solution.py
@@ -11,8 +11,6 @@
 
 score_scale = (0.1 * math.log(40.0) + 1.0) ** 2 / math.sqrt(192.0)
 neg_fill = -1e30
-SETS = 2
-CHUNKS = (1, 2)
 
 
 def swap(x, axis, offset):
@@ -21,11 +19,12 @@
 
 
 def set_members(expert_count):
-    half = expert_count // 2
-    return [
-        [k for k in range(expert_count) if (k % half) * SETS // half == s]
-        for s in reversed(range(SETS))
-    ]
+    cut = expert_count - expert_count // 4
+    return [list(range(cut, expert_count)), list(range(cut))]
+
+
+def is_doubled(ctx_size, width):
+    return ctx_size == 4 and width % 256 == 0
 
 
 def where_am_i():
@@ -85,8 +84,7 @@
     return matrix, pl.BlockSpec((rows, width), lambda i, w: (0, w[1]))
 
 
-def dispatch_kernel(capacity, where_ref, ids_ref, tokens_ref, *out_refs):
-    expert_count = len(out_refs)
+def dispatch_kernel(capacity, expert_count, members, where_ref, ids_ref, *refs):
     ids = ids_ref[...]
     picks, token_count = ids.shape
     experts = lax.broadcasted_iota(jnp.int32, (expert_count, token_count), 0)
@@ -105,53 +103,71 @@
         place = place + (ids[k : k + 1, :] ^ where_ref[0]) * capacity
         hit = jnp.where(place == slots, 1.0, 0.0)
         chosen = hit if chosen is None else chosen + hit
-    rows = jnp.dot(
-        chosen.astype(jnp.bfloat16), tokens_ref[...], preferred_element_type=jnp.float32
-    ).astype(tokens_ref.dtype)
-    for k in range(expert_count):
-        out_refs[k][...] = rows[k * capacity : (k + 1) * capacity, :]
-
-
-def dispatch(tokens, ids, capacity, expert_count, width, where):
+    chosen = chosen.astype(jnp.bfloat16)
+    sources = refs[: 2 if members else 1]
+    targets = refs[len(sources) :]
+    own, half = sources[0], sources[0].shape[1] // 2
+
+    def send(group, columns, outs, at):
+        pick = jnp.concatenate(
+            [chosen[k * capacity : (k + 1) * capacity, :] for k in group], axis=0
+        )
+        rows = jnp.dot(pick, columns, preferred_element_type=jnp.float32).astype(own.dtype)
+        for n, out in enumerate(outs):
+            out[:, at : at + rows.shape[1]] = rows[n * capacity : (n + 1) * capacity, :]
+
+    whole = [k for k in range(expert_count) if k not in members]
+    send(whole, own[...], targets[: len(whole)], 0)
+    if members:
+        late = targets[len(whole) : len(whole) + len(members)]
+        first = targets[len(whole) + len(members) :]
+        send(members, own[:, half:], late, 0)
+        send(members, own[:, :half], first, 0)
+        send(members, sources[1][...], first, half)
+
+
+def dispatch(tokens, ids, capacity, expert_count, width, members, where):
+    token_count = tokens.shape[0]
     operand, spec = own_columns(tokens, width, where)
-    block = (capacity, width)
-    return call(
-        functools.partial(dispatch_kernel, capacity), (1,),
-        [ids, operand], [whole_spec(ids.shape), spec],
-        [jax.ShapeDtypeStruct(block, tokens.dtype)] * expert_count,
-        [whole_spec(block)] * expert_count,
-        2 * expert_count * capacity * tokens.shape[0] * width, where,
-    )
-
-
-def pack_kernel(count, where_ref, *refs):
-    rows, targets = refs[0].shape[0], refs[count:]
-    share = count // len(targets)
-    for i, source in enumerate(refs[:count]):
-        at = i % share * rows
-        targets[i // share][at : at + rows, :] = source[...]
-
-
-def pack(blocks, chunks, where):
+    operands, specs = [operand], [spec]
+    if members:
+        operands.append(tokens)
+        specs.append(pl.BlockSpec((token_count, width // 2), lambda i, w: (0, (w[1] ^ 2) * 2)))
+    widths = [width] * (expert_count - len(members)) + [width // 2] * len(members)
+    widths += [width] * len(members)
+    blocks = [(capacity, w) for w in widths]
+    outs = call(
+        functools.partial(dispatch_kernel, capacity, expert_count, members), (1,),
+        [ids, *operands], [whole_spec(ids.shape), *specs],
+        [jax.ShapeDtypeStruct(block, tokens.dtype) for block in blocks],
+        [whole_spec(block) for block in blocks],
+        2 * expert_count * capacity * token_count * width, where,
+    )
+    order = [k for k in range(expert_count) if k not in members] + members
+    first = dict(zip(members, outs[expert_count:]))
+    return dict(zip(order, outs)), first
+
+
+def pack_kernel(where_ref, *refs):
+    rows = refs[0].shape[0]
+    for i, source in enumerate(refs[:-1]):
+        refs[-1][i * rows : (i + 1) * rows, :] = source[...]
+
+
+def pack(blocks, where):
     rows, width = blocks[0].shape
-    shape = (len(blocks) // chunks * rows, width)
-    return call(
-        functools.partial(pack_kernel, len(blocks)), (1,), blocks,
-        [whole_spec((rows, width))] * len(blocks),
-        [jax.ShapeDtypeStruct(shape, blocks[0].dtype)] * chunks, [whole_spec(shape)] * chunks,
-        len(blocks) * rows * width, where,
+    shape = (len(blocks) * rows, width)
+    return call(
+        pack_kernel, (1,), blocks, [whole_spec((rows, width))] * len(blocks),
+        jax.ShapeDtypeStruct(shape, blocks[0].dtype), whole_spec(shape), shape[0] * width, where,
     )
 
 
 def up_sum(count, refs):
-    gate_refs, up_refs, rows = refs[:count], refs[count : 2 * count], refs[2 * count :]
-    chunks = len(rows) // count
     acc = None
     for j in range(count):
-        weights = jnp.concatenate([gate_refs[j][...], up_refs[j][...]], axis=1)
-        piece = [ref[...] for ref in rows[j * chunks : (j + 1) * chunks]]
-        piece = piece[0] if chunks == 1 else jnp.concatenate(piece, axis=0)
-        term = jnp.dot(piece, weights, preferred_element_type=jnp.float32)
+        weights = jnp.concatenate([refs[j][...], refs[count + j][...]], axis=1)
+        term = jnp.dot(refs[2 * count + j][...], weights, preferred_element_type=jnp.float32)
         acc = term if acc is None else acc + term
     return acc
 
@@ -167,25 +183,30 @@
     refs[-1][...] = (gate_h / (1.0 + jnp.exp(-gate_h)) * up_h).astype(refs[-1].dtype)
 
 
-def mlp(pieces, offsets, gate_matrix, up_matrix, partial, where):
-    chunk_rows, width = pieces[0][0].shape
+def mlp(pieces, width, gate_matrix, up_matrix, partial, where):
     count, hidden_width = len(pieces), gate_matrix.shape[1]
-    rows = chunk_rows * len(pieces[0])
-    flat = [chunk for piece in pieces for chunk in piece]
+    rows = pieces[0][0].shape[0]
+    arrays = [piece[0] for piece in pieces]
     specs = [
-        pl.BlockSpec((width, hidden_width), lambda i, w, k=k: (w[1] ^ k, 0)) for k in offsets
+        pl.BlockSpec((w, hidden_width), lambda i, m, k=k, n=width // w, b=b: ((m[1] ^ k) * n + b, 0))
+        for x, at, k, b, w in pieces
     ]
-    operands = [gate_matrix] * count + [up_matrix] * count + flat
-    specs = specs + specs + [whole_spec((chunk_rows, width))] * len(flat)
+    row_specs = [
+        whole_spec(x.shape) if x.shape[1] == w else pl.BlockSpec((rows, w), lambda i, m, at=at: (0, at))
+        for x, at, k, b, w in pieces
+    ]
+    operands = [gate_matrix] * count + [up_matrix] * count + arrays
+    specs = specs + specs + row_specs
     if partial is None:
         kernel, out = part_kernel, jax.ShapeDtypeStruct((rows, 2 * hidden_width), jnp.float32)
     else:
-        kernel, out = mlp_kernel, jax.ShapeDtypeStruct((rows, hidden_width), flat[0].dtype)
+        kernel, out = mlp_kernel, jax.ShapeDtypeStruct((rows, hidden_width), arrays[0].dtype)
         operands.append(partial)
         specs.append(whole_spec(partial.shape))
+    columns = sum(piece[4] for piece in pieces)
     return call(
         functools.partial(kernel, count), (1,), operands, specs, out, whole_spec(out.shape),
-        4 * count * rows * width * hidden_width, where, vmem=24 << 20,
+        4 * rows * columns * hidden_width, where, vmem=24 << 20,
     )
 
 
@@ -375,21 +396,31 @@
     slices = split_columns(w_down[0], width, where)
     down_parts = [swap(slices[offset - 1], "ctx", offset) for offset in range(1, ctx_size)]
 
-    outgoing = dispatch(moe_tokens, expert_ids.T, capacity, expert_count, width, where)
     sets = set_members(expert_count)
+    doubled = sets[-1] if is_doubled(ctx_size, width) else []
+    outgoing, first = dispatch(
+        moe_tokens, expert_ids.T, capacity, expert_count, width, doubled, where
+    )
     arrived = [swap(outgoing[k], "exp", k) if k else outgoing[0] for k in range(expert_count)]
 
     returned = [None] * expert_count
-    for s, members in enumerate(sets):
-        chunks = pack([arrived[k] for k in members], CHUNKS[s], where)
-        pieces = [None] * ctx_size
-        pieces[0] = chunks
+    for members in sets:
+        own = pack([arrived[k] for k in members], where)
+        beside = swap(own, "ctx", 1)
+        w, b = own.shape[1], width // own.shape[1] - 1
+        early = [(own, 0, 0, b, w), (beside, 0, 1, b, w)]
+        late = []
         for offset in evens:
-            pieces[offset] = [swap(chunk, "ctx", offset) for chunk in chunks]
-        for offset in range(0, ctx_size, 2):
-            pieces[offset + 1] = [swap(chunk, "ctx", 1) for chunk in pieces[offset]]
-        partial = mlp(pieces[:2], [0, 1], w_gate[0], w_up[0], None, where)
-        hidden = mlp(pieces[2:], range(2, ctx_size), w_gate[0], w_up[0], partial, where)
+            crossed = swap(own, "ctx", offset)
+            late += [(crossed, 0, offset, b, w)]
+            late += [(swap(crossed, "ctx", 1), 0, offset + 1, b, w)]
+        if w != width:
+            both = [swap(first[k], "exp", k) if k else first[k] for k in members]
+            both = pack(both, where)
+            other = swap(both, "ctx", 1)
+            early += [(both, 0, 0, 0, w), (both, 1, 2, 0, w), (other, 0, 1, 0, w), (other, 1, 3, 0, w)]
+        partial = mlp(early, width, w_gate[0], w_up[0], None, where)
+        hidden = mlp(late, width, w_gate[0], w_up[0], partial, where)
         hidden = [hidden] + [swap(hidden, "ctx", offset) for offset in range(1, ctx_size)]
         blocks = down(hidden, w_down[0], down_parts, len(members), where)
         for k, block in zip(members, blocks):

time: 134 us -> 130 us (0.970)
  waiting for transfers between devices: 70.4 us -> 36 us
  starting transfers between devices: 37.7 us -> 66.2 us
    ppermute x35 -> x38, waiting for transfers between devices: 70.4 us -> 36 us  [swap(): return lax.ppermute(x, axis, [(i, i ^ offset) for i in range(size)])]
    ppermute x35 -> x38, starting transfers between devices: 37.7 us -> 66.2 us  [swap(): return lax.ppermute(x, axis, [(i, i ^ offset) for i in range(size)])]
    pallas_call x13 -> x14, Pallas kernels: 22 us -> 23.3 us  [call(): pl.pallas_call(kernel, out_shape=out_shape, grid_spec=pltpu.PrefetchScala...]
  transfers between devices with their start and end apart: 35 -> 38, of which waited for: 19 -> 10; matrix products, arithmetic and copies ran while one was open for 1% -> 1% of each run, Pallas kernels for 14% -> 15%
where the time goes in v2:
time: 130 us
  starting transfers between devices  66.2 us (51%)
  waiting for transfers between devices  36 us (28%)
  Pallas kernels  23.3 us (18%)
  local copies, waits for them, and re-layouts  3.1 us (2%)
    ppermute x38, starting transfers between devices, swap(): return lax.ppermute(x, axis, [(i, i ^ offset) for i in range(size)])  66.2 us
    ppermute x38, waiting for transfers between devices, swap(): return lax.ppermute(x, axis, [(i, i ^ offset) for i in range(size)])  36 us
    pallas_call x14, Pallas kernels, call(): pl.pallas_call(kernel, out_shape=out_shape, grid_spec=pltpu.PrefetchScala...  23.3 us
    unnamed x23, local copies, waits for them, and re-layouts  3.1 us
  transfers between devices with their start and end apart: 38, of which 10 were waited for; matrix products, arithmetic and copies ran while one was open for 1% of the time, Pallas kernels for 15%

profile of v2, /device:TPU:0, one launch (start us, length us, event | category | flops | bytes accessed | tf_op | source)
XLA Modules:
  0.0 129.6 jit_solution(7209791842125931700)
XLA Ops:
  0.7 1.5 %copy-done.3 = bf16[128,7168]{1,0:T(8,128)(2,1)S(1)} copy-done((bf16[128,7168]{1,0:T(8,128)(2,1)S(1)}, bf16[128,7168]{1,0:T(8,128)(2,1)}, u32[]{:S(2)}) %copy-start.3) | copy-done | bytes 1835032
  2.9 1.3 %shard_map.114 = (bf16[48,1792]{1,0:T(8,128)(2,1)S(1)}, bf16[48,1792]{1,0:T(8,128)(2,1)S(1)}, bf16[48,896]{1,0:T(8,128)(2,1)S(1)}, bf16[48,896]{1,0:T(8,128)(2,1...) custom-call(s32[2]{0:T(128)S(1)} %pad_add_fusion.where_ref, ...), custom_call_target="tpu_custom_call" | custom-call | flops 176160768 | bytes 5563392 | tf_op jit(solution)/shard_map/pallas_call | solution.py:42
  4.2 3.0 %collective-permute-start.24 = (bf16[48,1792]{1,0:T(8,128)(2,1)S(1)}, bf16[48,1792]{1,0:T(8,128)(2,1)S(1)}, u32[]{:S(2)}, u32[]{:S(2)}) collective-permute-start(bf16[48,1792]{1,0:T(8,128)(2,1)S(1)} %get-tuple-element.47), channel_id=1, source_target_pairs={{0,1},{1,0},{2,3},{3,2},{4,5},{5,4},{6,7},{7,6},{8,9},{9,8},{10,11... | collective-permute-start | bytes 516104 | tf_op jit(solution)/shard_map/ppermute | solution.py:18
  7.2 1.6 %collective-permute-start.25 = (bf16[48,1792]{1,0:T(8,128)(2,1)S(1)}, bf16[48,1792]{1,0:T(8,128)(2,1)S(1)}, u32[]{:S(2)}, u32[]{:S(2)}) collective-permute-start(bf16[48,1792]{1,0:T(8,128)(2,1)S(1)} %get-tuple-element.48), channel_id=1, source_target_pairs={{0,2},{1,3},{2,0},{3,1},{4,6},{5,7},{6,4},{7,5},{8,10},{9,11},{10,... | collective-permute-start | bytes 516104 | tf_op jit(solution)/shard_map/ppermute | solution.py:18
  9.4 1.4 %collective-permute-start.26 = (bf16[48,1792]{1,0:T(8,128)(2,1)S(1)}, bf16[48,1792]{1,0:T(8,128)(2,1)S(1)}, u32[]{:S(2)}, u32[]{:S(2)}) collective-permute-start(bf16[48,1792]{1,0:T(8,128)(2,1)S(1)} %get-tuple-element.49), channel_id=1, source_target_pairs={{0,3},{1,2},{2,1},{3,0},{4,7},{5,6},{6,5},{7,4},{8,11},{9,10},{10,... | collective-permute-start | bytes 516104 | tf_op jit(solution)/shard_map/ppermute | solution.py:18
  10.7 2.6 %collective-permute-start.27 = (bf16[48,1792]{1,0:T(8,128)(2,1)S(1)}, bf16[48,1792]{1,0:T(8,128)(2,1)S(1)}, u32[]{:S(2)}, u32[]{:S(2)}) collective-permute-start(bf16[48,1792]{1,0:T(8,128)(2,1)S(1)} %get-tuple-element.50), channel_id=1, source_target_pairs={{0,4},{1,5},{2,6},{3,7},{4,0},{5,1},{6,2},{7,3},{8,12},{9,13},{10,... | collective-permute-start | bytes 516104 | tf_op jit(solution)/shard_map/ppermute | solution.py:18
  14.0 4.0 %collective-permute-start.3 = (bf16[48,1792]{1,0:T(8,128)(2,1)S(1)}, bf16[48,1792]{1,0:T(8,128)(2,1)S(1)}, u32[]{:S(2)}, u32[]{:S(2)}) collective-permute-start(bf16[48,1792]{1,0:T(8,128)(2,1)S(1)} %get-tuple-element.30), channel_id=1, source_target_pairs={{0,6},{1,7},{2,4},{3,5},{4,2},{5,3},{6,0},{7,1},{8,14},{9,15},{10,... | collective-permute-start | bytes 516104 | tf_op jit(solution)/shard_map/ppermute | solution.py:18
  19.1 3.3 %collective-permute-start.28 = (bf16[48,1792]{1,0:T(8,128)(2,1)S(1)}, bf16[48,1792]{1,0:T(8,128)(2,1)S(1)}, u32[]{:S(2)}, u32[]{:S(2)}) collective-permute-start(bf16[48,1792]{1,0:T(8,128)(2,1)S(1)} %get-tuple-element.51), channel_id=1, source_target_pairs={{0,5},{1,4},{2,7},{3,6},{4,1},{5,0},{6,3},{7,2},{8,13},{9,12},{10,... | collective-permute-start | bytes 516104 | tf_op jit(solution)/shard_map/ppermute | solution.py:18
  23.3 9.8 %collective-permute-start.18 = (bf16[48,896]{1,0:T(8,128)(2,1)S(1)}, bf16[48,896]{1,0:T(8,128)(2,1)S(1)}, u32[]{:S(2)}, u32[]{:S(2)}) collective-permute-start(bf16[48,896]{1,0:T(8,128)(2,1)S(1)} %get-tuple-element.43), channel_id=1, source_target_pairs={{0,3},{1,2},{2,1},{3,0},{4,7},{5,6},{6,5},{7,4},{8,11},{9,10},{10,... | collective-permute-start | bytes 258056 | tf_op jit(solution)/shard_map/ppermute | solution.py:18
  33.1 6.6 %collective-permute-start.19 = (bf16[48,896]{1,0:T(8,128)(2,1)S(1)}, bf16[48,896]{1,0:T(8,128)(2,1)S(1)}, u32[]{:S(2)}, u32[]{:S(2)}) collective-permute-start(bf16[48,896]{1,0:T(8,128)(2,1)S(1)} %get-tuple-element.44), channel_id=1, source_target_pairs={{0,4},{1,5},{2,6},{3,7},{4,0},{5,1},{6,2},{7,3},{8,12},{9,13},{10,... | collective-permute-start | bytes 258056 | tf_op jit(solution)/shard_map/ppermute | solution.py:18
  39.7 7.3 %collective-permute-start.20 = (bf16[48,896]{1,0:T(8,128)(2,1)S(1)}, bf16[48,896]{1,0:T(8,128)(2,1)S(1)}, u32[]{:S(2)}, u32[]{:S(2)}) collective-permute-start(bf16[48,896]{1,0:T(8,128)(2,1)S(1)} %get-tuple-element.45), channel_id=1, source_target_pairs={{0,5},{1,4},{2,7},{3,6},{4,1},{5,0},{6,3},{7,2},{8,13},{9,12},{10,... | collective-permute-start | bytes 258056 | tf_op jit(solution)/shard_map/ppermute | solution.py:18
  47.6 1.6 %collective-permute-start.5 = (bf16[96,1792]{1,0:T(8,128)(2,1)S(1)}, bf16[96,1792]{1,0:T(8,128)(2,1)S(1)}, u32[]{:S(2)}, u32[]{:S(2)}) collective-permute-start(bf16[96,1792]{1,0:T(8,128)(2,1)S(1)} %shard_map.115.refs_4_), channel_id=1, source_target_pairs={{0,16},{8,24},{16,0},{24,8},{1,17},{9,25},{17,1},{25,9},{2,18},{10... | collective-permute-start | bytes 1032200 | tf_op jit(solution)/shard_map/ppermute | solution.py:18
  51.7 1.6 %collective-permute-start.21 = (bf16[288,896]{1,0:T(8,128)(2,1)S(1)}, bf16[288,896]{1,0:T(8,128)(2,1)S(1)}, u32[]{:S(2)}, u32[]{:S(2)}) collective-permute-start(bf16[288,896]{1,0:T(8,128)(2,1)S(1)} %shard_map.121.refs_12_), channel_id=1, source_target_pairs={{0,16},{8,24},{16,0},{24,8},{1,17},{9,25},{17,1},{25,9},{2,18},{10... | collective-permute-start | bytes 1548296 | tf_op jit(solution)/shard_map/ppermute | solution.py:18
  53.8 3.6 %collective-permute-done.5.refs_4_ = bf16[96,1792]{1,0:T(8,128)(2,1)S(1)} collective-permute-done((bf16[96,1792]{1,0:T(8,128)(2,1)S(1)}, bf16[96,1792]{1,0:T(8,128)(2,1)S(1)}, u32[]{:S(2)}, u32[]{:S(2)}) %collective-permute-start.5) | collective-permute-done | bytes 344096 | tf_op jit(solution)/shard_map/ppermute | solution.py:18
  57.4 9.2 %collective-permute-done.21.refs_4_ = bf16[288,896]{1,0:T(8,128)(2,1)S(1)} collective-permute-done((bf16[288,896]{1,0:T(8,128)(2,1)S(1)}, bf16[288,896]{1,0:T(8,128)(2,1)S(1)}, u32[]{:S(2)}, u32[]{:S(2)}) %collective-permute-start.21) | collective-permute-done | bytes 516128 | tf_op jit(solution)/shard_map/ppermute | solution.py:18
  72.3 1.6 %shard_map.123.refs_6_ = f32[288,256]{1,0:T(8,128)S(1)} custom-call(s32[2]{0:T(128)S(1)} %pad_add_fusion.where_ref, bf16[7168,128]{1,0:T(8,128)(2,1)S(1)} %bitcast.14, bf16[7168,128]{1,0:T(8,128)(2,1)S(1)} %bitcast.15, bf16[7168,128]{1,0:T(8,128)(2,1)S(1)} %bitcast.16, bf16[7168,128]{1,0:T(8,128)(2,1)S(1)} %bitcast.17, bf16[7168,128]{1,0:T(8,128)(2,1)S(1)} %bitcast.18, ...), custom_call_target="tpu_custom_call" | custom-call | flops 792723456 | bytes 27475968 | tf_op jit(solution)/shard_map/pallas_call | solution.py:42
  73.9 1.2 collective-permute-start.10
  76.3 4.9 %collective-permute-done.12.refs_6_ = bf16[128,1792]{1,0:T(8,128)(2,1)S(1)} collective-permute-done((bf16[128,1792]{1,0:T(8,128)(2,1)S(1)}, bf16[128,1792]{1,0:T(8,128)(2,1)S(1)}, u32[]{:S(2)}, u32[]{:S(2)}) %collective-permute-start.12) | collective-permute-done | bytes 458784 | tf_op jit(solution)/shard_map/ppermute | solution.py:18
  81.2 8.3 %collective-permute-done.13.refs_7_ = bf16[128,1792]{1,0:T(8,128)(2,1)S(1)} collective-permute-done((bf16[128,1792]{1,0:T(8,128)(2,1)S(1)}, bf16[128,1792]{1,0:T(8,128)(2,1)S(1)}, u32[]{:S(2)}, u32[]{:S(2)}) %collective-permute-start.13) | collective-permute-done | bytes 458784 | tf_op jit(solution)/shard_map/ppermute | solution.py:18
  90.6 2.4 %collective-permute-done.10.refs_3_ = bf16[96,128]{1,0:T(8,128)(2,1)S(1)} collective-permute-done((bf16[96,128]{1,0:T(8,128)(2,1)S(1)}, bf16[96,128]{1,0:T(8,128)(2,1)S(1)}, u32[]{:S(2)}, u32[]{:S(2)}) %collective-permute-start.10) | collective-permute-done | bytes 24608 | tf_op jit(solution)/shard_map/ppermute | solution.py:18
  95.4 2.6 %collective-permute-start.14 = (bf16[48,1792]{1,0:T(8,128)(2,1)S(1)}, bf16[48,1792]{1,0:T(8,128)(2,1)S(1)}, u32[]{:S(2)}, u32[]{:S(2)}) collective-permute-start(bf16[48,1792]{1,0:T(8,128)(2,1)S(1)} %get-tuple-element.35), channel_id=1, source_target_pairs={{0,6},{1,7},{2,4},{3,5},{4,2},{5,3},{6,0},{7,1},{8,14},{9,15},{10,... | collective-permute-start | bytes 516104 | tf_op jit(solution)/shard_map/ppermute | solution.py:18
  98.0 1.6 %collective-permute-start.15 = (bf16[48,1792]{1,0:T(8,128)(2,1)S(1)}, bf16[48,1792]{1,0:T(8,128)(2,1)S(1)}, u32[]{:S(2)}, u32[]{:S(2)}) collective-permute-start(bf16[48,1792]{1,0:T(8,128)(2,1)S(1)} %get-tuple-element.36), channel_id=1, source_target_pairs={{0,7},{1,6},{2,5},{3,4},{4,3},{5,2},{6,1},{7,0},{8,15},{9,14},{10,... | collective-permute-start | bytes 516104 | tf_op jit(solution)/shard_map/ppermute | solution.py:18
  101.1 3.1 %collective-permute-done.32.refs_3_ = bf16[288,128]{1,0:T(8,128)(2,1)S(1)} collective-permute-done((bf16[288,128]{1,0:T(8,128)(2,1)S(1)}, bf16[288,128]{1,0:T(8,128)(2,1)S(1)}, u32[]{:S(2)}, u32[]{:S(2)}) %collective-permute-start.32) | collective-permute-done | bytes 73760 | tf_op jit(solution)/shard_map/ppermute | solution.py:18
  104.3 1.3 shard_map.125
  105.5 1.4 %collective-permute-start.33 = (bf16[48,1792]{1,0:T(8,128)(2,1)S(1)}, bf16[48,1792]{1,0:T(8,128)(2,1)S(1)}, u32[]{:S(2)}, u32[]{:S(2)}) collective-permute-start(bf16[48,1792]{1,0:T(8,128)(2,1)S(1)} %get-tuple-element.53), channel_id=1, source_target_pairs={{0,1},{1,0},{2,3},{3,2},{4,5},{5,4},{6,7},{7,6},{8,9},{9,8},{10,11... | collective-permute-start | bytes 516104 | tf_op jit(solution)/shard_map/ppermute | solution.py:18
  106.9 2.2 %collective-permute-start.35 = (bf16[48,1792]{1,0:T(8,128)(2,1)S(1)}, bf16[48,1792]{1,0:T(8,128)(2,1)S(1)}, u32[]{:S(2)}, u32[]{:S(2)}) collective-permute-start(bf16[48,1792]{1,0:T(8,128)(2,1)S(1)} %get-tuple-element.55), channel_id=1, source_target_pairs={{0,3},{1,2},{2,1},{3,0},{4,7},{5,6},{6,5},{7,4},{8,11},{9,10},{10,... | collective-permute-start | bytes 516104 | tf_op jit(solution)/shard_map/ppermute | solution.py:18
  109.1 1.8 %collective-permute-start.36 = (bf16[48,1792]{1,0:T(8,128)(2,1)S(1)}, bf16[48,1792]{1,0:T(8,128)(2,1)S(1)}, u32[]{:S(2)}, u32[]{:S(2)}) collective-permute-start(bf16[48,1792]{1,0:T(8,128)(2,1)S(1)} %get-tuple-element.56), channel_id=1, source_target_pairs={{0,4},{1,5},{2,6},{3,7},{4,0},{5,1},{6,2},{7,3},{8,12},{9,13},{10,... | collective-permute-start | bytes 516104 | tf_op jit(solution)/shard_map/ppermute | solution.py:18
  110.9 2.9 %collective-permute-start.37 = (bf16[48,1792]{1,0:T(8,128)(2,1)S(1)}, bf16[48,1792]{1,0:T(8,128)(2,1)S(1)}, u32[]{:S(2)}, u32[]{:S(2)}) collective-permute-start(bf16[48,1792]{1,0:T(8,128)(2,1)S(1)} %get-tuple-element.57), channel_id=1, source_target_pairs={{0,5},{1,4},{2,7},{3,6},{4,1},{5,0},{6,3},{7,2},{8,13},{9,12},{10,... | collective-permute-start | bytes 516104 | tf_op jit(solution)/shard_map/ppermute | solution.py:18
  113.9 9.3 %shard_map.113 = bf16[8,128,128]{2,1,0:T(8,128)(2,1)S(1)} custom-call(s32[2]{0:T(128)S(1)} %pad_add_fusion.where_ref, s32[8]{0:T(128)S(1)} %copy-done.10, bf16[8,576,128]{2,1,0:T(8,128)(2,1)S(1)} %bitcast.43, bf16[8,512,128]{2,1,0:T(8,128)(2,1)S(1)} %copy-done.8, bf16[576,128]{1,0:T(8,128)(2,1)S(1)} %bitcast.46, ...), custom_call_target="tpu_custom_call" | custom-call | flops 1207959552 | bytes 3080192 | tf_op jit(solution)/shard_map/pallas_call | solution.py:42
  124.1 1.5 %shard_map.120 = (f32[128,1792]{1,0:T(8,128)S(1)}, bf16[256,288]{1,0:T(8,128)(2,1)S(1)}, f32[128,8]{1,0:T(8,128)S(1)}) custom-call(s32[2]{0:T(128)S(1)} %pad_add_fusion.where_ref, s32[2,128]{1,0:T(2,128)S(1)} %bitcast.41, f32[2,128]{1,0:T(2,128)S(1)} %bitcast.42, bf16[48,1792]{1,0:T(8,128)(2,1)S(1)} %collective-permute-done.14.refs_0_, ...), custom_call_target="tpu_custom_call" | custom-call | flops 88080384 | bytes 1415168 | tf_op jit(solution)/shard_map/pallas_call | solution.py:42
  125.6 2.0 %collective-permute-done.37.refs_5_ = bf16[48,1792]{1,0:T(8,128)(2,1)S(1)} collective-permute-done((bf16[48,1792]{1,0:T(8,128)(2,1)S(1)}, bf16[48,1792]{1,0:T(8,128)(2,1)S(1)}, u32[]{:S(2)}, u32[]{:S(2)}) %collective-permute-start.37) | collective-permute-done | bytes 172064 | tf_op jit(solution)/shard_map/ppermute | solution.py:18
  127.7 2.0 %shard_map.126 = bf16[128,1792]{1,0:T(8,128)(2,1)} custom-call(s32[2]{0:T(128)S(1)} %pad_add_fusion.where_ref, f32[128,1792]{1,0:T(8,128)S(1)} %get-tuple-element.37.sum_ref, bf16[256,288]{1,0:T(8,128)(2,1)S(1)} %get-tuple-element.38.hits_ref, f32[128,8]{1,0:T(8,128)S(1)} %get-tuple-element.39.columns_ref, bf16[48,1792]{1,0:T(8,128)(2,1)S(1)} %get-tuple-element.52.refs_0_, ...), custom_call_target="tpu_custom_call" | custom-call | flops 264241152 | bytes 2560000 | tf_op jit(solution)/shard_map/pallas_call | solution.py:42
  (82 shorter events, 20.4 us)
Async XLA Ops:
  4.2 13.8 %collective-permute-start.24 = (bf16[48,1792]{1,0:T(8,128)(2,1)S(1)}, bf16[48,1792]{1,0:T(8,128)(2,1)S(1)}, u32[]{:S(2)}, u32[]{:S(2)}) collective-permute-start(bf16[48,1792]{1,0:T(8,128)(2,1)S(1)} %get-tuple-element.47), channel_id=1, source_target_pairs={{0,1},{1,0},{2,3},{3,2},{4,5},{5,4},{6,7},{7,6},{8,9},{9,8},{10,11... | collective-permute-start | bytes 516104 | tf_op jit(solution)/shard_map/ppermute | solution.py:18
  7.2 11.8 %collective-permute-start.25 = (bf16[48,1792]{1,0:T(8,128)(2,1)S(1)}, bf16[48,1792]{1,0:T(8,128)(2,1)S(1)}, u32[]{:S(2)}, u32[]{:S(2)}) collective-permute-start(bf16[48,1792]{1,0:T(8,128)(2,1)S(1)} %get-tuple-element.48), channel_id=1, source_target_pairs={{0,2},{1,3},{2,0},{3,1},{4,6},{5,7},{6,4},{7,5},{8,10},{9,11},{10,... | collective-permute-start | bytes 516104 | tf_op jit(solution)/shard_map/ppermute | solution.py:18
  9.4 13.0 %collective-permute-start.26 = (bf16[48,1792]{1,0:T(8,128)(2,1)S(1)}, bf16[48,1792]{1,0:T(8,128)(2,1)S(1)}, u32[]{:S(2)}, u32[]{:S(2)}) collective-permute-start(bf16[48,1792]{1,0:T(8,128)(2,1)S(1)} %get-tuple-element.49), channel_id=1, source_target_pairs={{0,3},{1,2},{2,1},{3,0},{4,7},{5,6},{6,5},{7,4},{8,11},{9,10},{10,... | collective-permute-start | bytes 516104 | tf_op jit(solution)/shard_map/ppermute | solution.py:18
  10.7 12.6 %collective-permute-start.27 = (bf16[48,1792]{1,0:T(8,128)(2,1)S(1)}, bf16[48,1792]{1,0:T(8,128)(2,1)S(1)}, u32[]{:S(2)}, u32[]{:S(2)}) collective-permute-start(bf16[48,1792]{1,0:T(8,128)(2,1)S(1)} %get-tuple-element.50), channel_id=1, source_target_pairs={{0,4},{1,5},{2,6},{3,7},{4,0},{5,1},{6,2},{7,3},{8,12},{9,13},{10,... | collective-permute-start | bytes 516104 | tf_op jit(solution)/shard_map/ppermute | solution.py:18
  14.0 19.0 %collective-permute-start.3 = (bf16[48,1792]{1,0:T(8,128)(2,1)S(1)}, bf16[48,1792]{1,0:T(8,128)(2,1)S(1)}, u32[]{:S(2)}, u32[]{:S(2)}) collective-permute-start(bf16[48,1792]{1,0:T(8,128)(2,1)S(1)} %get-tuple-element.30), channel_id=1, source_target_pairs={{0,6},{1,7},{2,4},{3,5},{4,2},{5,3},{6,0},{7,1},{8,14},{9,15},{10,... | collective-permute-start | bytes 516104 | tf_op jit(solution)/shard_map/ppermute | solution.py:18
  18.0 21.7 %collective-permute-start.4 = (bf16[48,1792]{1,0:T(8,128)(2,1)S(1)}, bf16[48,1792]{1,0:T(8,128)(2,1)S(1)}, u32[]{:S(2)}, u32[]{:S(2)}) collective-permute-start(bf16[48,1792]{1,0:T(8,128)(2,1)S(1)} %get-tuple-element.31), channel_id=1, source_target_pairs={{0,7},{1,6},{2,5},{3,4},{4,3},{5,2},{6,1},{7,0},{8,15},{9,14},{10,... | collective-permute-start | bytes 516104 | tf_op jit(solution)/shard_map/ppermute | solution.py:18
  19.1 28.5 %collective-permute-start.28 = (bf16[48,1792]{1,0:T(8,128)(2,1)S(1)}, bf16[48,1792]{1,0:T(8,128)(2,1)S(1)}, u32[]{:S(2)}, u32[]{:S(2)}) collective-permute-start(bf16[48,1792]{1,0:T(8,128)(2,1)S(1)} %get-tuple-element.51), channel_id=1, source_target_pairs={{0,5},{1,4},{2,7},{3,6},{4,1},{5,0},{6,3},{7,2},{8,13},{9,12},{10,... | collective-permute-start | bytes 516104 | tf_op jit(solution)/shard_map/ppermute | solution.py:18
  22.3 27.5 %collective-permute-start.17 = (bf16[48,896]{1,0:T(8,128)(2,1)S(1)}, bf16[48,896]{1,0:T(8,128)(2,1)S(1)}, u32[]{:S(2)}, u32[]{:S(2)}) collective-permute-start(bf16[48,896]{1,0:T(8,128)(2,1)S(1)} %get-tuple-element.42), channel_id=1, source_target_pairs={{0,2},{1,3},{2,0},{3,1},{4,6},{5,7},{6,4},{7,5},{8,10},{9,11},{10,... | collective-permute-start | bytes 258056 | tf_op jit(solution)/shard_map/ppermute | solution.py:18
  23.3 26.6 %collective-permute-start.18 = (bf16[48,896]{1,0:T(8,128)(2,1)S(1)}, bf16[48,896]{1,0:T(8,128)(2,1)S(1)}, u32[]{:S(2)}, u32[]{:S(2)}) collective-permute-start(bf16[48,896]{1,0:T(8,128)(2,1)S(1)} %get-tuple-element.43), channel_id=1, source_target_pairs={{0,3},{1,2},{2,1},{3,0},{4,7},{5,6},{6,5},{7,4},{8,11},{9,10},{10,... | collective-permute-start | bytes 258056 | tf_op jit(solution)/shard_map/ppermute | solution.py:18
  33.1 16.9 %collective-permute-start.19 = (bf16[48,896]{1,0:T(8,128)(2,1)S(1)}, bf16[48,896]{1,0:T(8,128)(2,1)S(1)}, u32[]{:S(2)}, u32[]{:S(2)}) collective-permute-start(bf16[48,896]{1,0:T(8,128)(2,1)S(1)} %get-tuple-element.44), channel_id=1, source_target_pairs={{0,4},{1,5},{2,6},{3,7},{4,0},{5,1},{6,2},{7,3},{8,12},{9,13},{10,... | collective-permute-start | bytes 258056 | tf_op jit(solution)/shard_map/ppermute | solution.py:18
  39.7 11.4 %collective-permute-start.20 = (bf16[48,896]{1,0:T(8,128)(2,1)S(1)}, bf16[48,896]{1,0:T(8,128)(2,1)S(1)}, u32[]{:S(2)}, u32[]{:S(2)}) collective-permute-start(bf16[48,896]{1,0:T(8,128)(2,1)S(1)} %get-tuple-element.45), channel_id=1, source_target_pairs={{0,5},{1,4},{2,7},{3,6},{4,1},{5,0},{6,3},{7,2},{8,13},{9,12},{10,... | collective-permute-start | bytes 258056 | tf_op jit(solution)/shard_map/ppermute | solution.py:18
  47.6 9.8 %collective-permute-start.5 = (bf16[96,1792]{1,0:T(8,128)(2,1)S(1)}, bf16[96,1792]{1,0:T(8,128)(2,1)S(1)}, u32[]{:S(2)}, u32[]{:S(2)}) collective-permute-start(bf16[96,1792]{1,0:T(8,128)(2,1)S(1)} %shard_map.115.refs_4_), channel_id=1, source_target_pairs={{0,16},{8,24},{16,0},{24,8},{1,17},{9,25},{17,1},{25,9},{2,18},{10... | collective-permute-start | bytes 1032200 | tf_op jit(solution)/shard_map/ppermute | solution.py:18
  49.8 21.4 %collective-permute-start.29 = (bf16[288,1792]{1,0:T(8,128)(2,1)S(1)}, bf16[288,1792]{1,0:T(8,128)(2,1)S(1)}, u32[]{:S(2)}, u32[]{:S(2)}) collective-permute-start(bf16[288,1792]{1,0:T(8,128)(2,1)S(1)} %shard_map.122.refs_14_.refs_15_), channel_id=1, source_target_pairs={{0,8},{8,0},{16,24},{24,16},{1,9},{9,1},{17,25},{25,17},{2,10},{10... | collective-permute-start | bytes 3096584 | tf_op jit(solution)/shard_map/ppermute | solution.py:18
  51.7 14.9 %collective-permute-start.21 = (bf16[288,896]{1,0:T(8,128)(2,1)S(1)}, bf16[288,896]{1,0:T(8,128)(2,1)S(1)}, u32[]{:S(2)}, u32[]{:S(2)}) collective-permute-start(bf16[288,896]{1,0:T(8,128)(2,1)S(1)} %shard_map.121.refs_12_), channel_id=1, source_target_pairs={{0,16},{8,24},{16,0},{24,8},{1,17},{9,25},{17,1},{25,9},{2,18},{10... | collective-permute-start | bytes 1548296 | tf_op jit(solution)/shard_map/ppermute | solution.py:18
  53.3 14.6 %collective-permute-start.23 = (bf16[288,896]{1,0:T(8,128)(2,1)S(1)}, bf16[288,896]{1,0:T(8,128)(2,1)S(1)}, u32[]{:S(2)}, u32[]{:S(2)}) collective-permute-start(bf16[288,896]{1,0:T(8,128)(2,1)S(1)} %shard_map.121.refs_12_), channel_id=1, source_target_pairs={{0,8},{8,0},{16,24},{24,16},{1,9},{9,1},{17,25},{25,17},{2,10},{10... | collective-permute-start | bytes 1548296 | tf_op jit(solution)/shard_map/ppermute | solution.py:18
  53.3 14.0 %collective-permute-start.7 = (bf16[96,1792]{1,0:T(8,128)(2,1)S(1)}, bf16[96,1792]{1,0:T(8,128)(2,1)S(1)}, u32[]{:S(2)}, u32[]{:S(2)}) collective-permute-start(bf16[96,1792]{1,0:T(8,128)(2,1)S(1)} %shard_map.115.refs_4_), channel_id=1, source_target_pairs={{0,8},{8,0},{16,24},{24,16},{1,9},{9,1},{17,25},{25,17},{2,10},{10... | collective-permute-start | bytes 1032200 | tf_op jit(solution)/shard_map/ppermute | solution.py:18
  57.4 11.4 %collective-permute-start.6 = (bf16[96,1792]{1,0:T(8,128)(2,1)S(1)}, bf16[96,1792]{1,0:T(8,128)(2,1)S(1)}, u32[]{:S(2)}, u32[]{:S(2)}) collective-permute-start(bf16[96,1792]{1,0:T(8,128)(2,1)S(1)} %collective-permute-done.5.refs_4_), channel_id=1, source_target_pairs={{0,8},{8,0},{16,24},{24,16},{1,9},{9,1},{17,25},{25,17},{2,10},{10... | collective-permute-start | bytes 1032200 | tf_op jit(solution)/shard_map/ppermute | solution.py:18
  67.3 8.9 %collective-permute-start.11 = (bf16[128,1792]{1,0:T(8,128)(2,1)S(1)}, bf16[128,1792]{1,0:T(8,128)(2,1)S(1)}, u32[]{:S(2)}, u32[]{:S(2)}) collective-permute-start(bf16[128,1792]{1,0:T(8,128)(2,1)S(1)} %get-tuple-element.32), channel_id=1, source_target_pairs={{0,8},{8,0},{16,24},{24,16},{1,9},{9,1},{17,25},{25,17},{2,10},{10... | collective-permute-start | bytes 1376264 | tf_op jit(solution)/shard_map/ppermute | solution.py:18
  67.8 13.4 %collective-permute-start.12 = (bf16[128,1792]{1,0:T(8,128)(2,1)S(1)}, bf16[128,1792]{1,0:T(8,128)(2,1)S(1)}, u32[]{:S(2)}, u32[]{:S(2)}) collective-permute-start(bf16[128,1792]{1,0:T(8,128)(2,1)S(1)} %get-tuple-element.33), channel_id=1, source_target_pairs={{0,16},{8,24},{16,0},{24,8},{1,17},{9,25},{17,1},{25,9},{2,18},{10... | collective-permute-start | bytes 1376264 | tf_op jit(solution)/shard_map/ppermute | solution.py:18
  68.8 20.7 %collective-permute-start.13 = (bf16[128,1792]{1,0:T(8,128)(2,1)S(1)}, bf16[128,1792]{1,0:T(8,128)(2,1)S(1)}, u32[]{:S(2)}, u32[]{:S(2)}) collective-permute-start(bf16[128,1792]{1,0:T(8,128)(2,1)S(1)} %get-tuple-element.34), channel_id=1, source_target_pairs={{0,24},{8,16},{16,8},{24,0},{1,25},{9,17},{17,9},{25,1},{2,26},{10... | collective-permute-start | bytes 1376264 | tf_op jit(solution)/shard_map/ppermute | solution.py:18
  71.3 28.2 %collective-permute-start.1 = (bf16[576,128]{1,0:T(8,128)(2,1)S(1)}, bf16[576,128]{1,0:T(8,128)(2,1)S(1)}, u32[]{:S(2)}, u32[]{:S(2)}) collective-permute-start(bf16[576,128]{1,0:T(8,128)(2,1)S(1)} %bitcast.44), channel_id=1, source_target_pairs={{0,16},{8,24},{16,0},{24,8},{1,17},{9,25},{17,1},{25,9},{2,18},{10... | collective-permute-start | bytes 442376 | tf_op jit(solution)/shard_map/ppermute | solution.py:18
  73.9 19.1 %collective-permute-start.10 = (bf16[96,128]{1,0:T(8,128)(2,1)S(1)}, bf16[96,128]{1,0:T(8,128)(2,1)S(1)}, u32[]{:S(2)}, u32[]{:S(2)}) collective-permute-start(bf16[96,128]{1,0:T(8,128)(2,1)S(1)} %shard_map.117.refs_0_), channel_id=1, source_target_pairs={{0,24},{8,16},{16,8},{24,0},{1,25},{9,17},{17,9},{25,1},{2,26},{10... | collective-permute-start | bytes 73736 | tf_op jit(solution)/shard_map/ppermute | solution.py:18
  76.2 23.5 %collective-permute-start.30 = (bf16[288,128]{1,0:T(8,128)(2,1)S(1)}, bf16[288,128]{1,0:T(8,128)(2,1)S(1)}, u32[]{:S(2)}, u32[]{:S(2)}) collective-permute-start(bf16[288,128]{1,0:T(8,128)(2,1)S(1)} %shard_map.124.refs_0_), channel_id=1, source_target_pairs={{0,8},{8,0},{16,24},{24,16},{1,9},{9,1},{17,25},{25,17},{2,10},{10... | collective-permute-start | bytes 221192 | tf_op jit(solution)/shard_map/ppermute | solution.py:18
  81.2 12.7 %collective-permute-start.8 = (bf16[96,128]{1,0:T(8,128)(2,1)S(1)}, bf16[96,128]{1,0:T(8,128)(2,1)S(1)}, u32[]{:S(2)}, u32[]{:S(2)}) collective-permute-start(bf16[96,128]{1,0:T(8,128)(2,1)S(1)} %shard_map.117.refs_0_), channel_id=1, source_target_pairs={{0,8},{8,0},{16,24},{24,16},{1,9},{9,1},{17,25},{25,17},{2,10},{10... | collective-permute-start | bytes 73736 | tf_op jit(solution)/shard_map/ppermute | solution.py:18
  95.4 13.7 %collective-permute-start.14 = (bf16[48,1792]{1,0:T(8,128)(2,1)S(1)}, bf16[48,1792]{1,0:T(8,128)(2,1)S(1)}, u32[]{:S(2)}, u32[]{:S(2)}) collective-permute-start(bf16[48,1792]{1,0:T(8,128)(2,1)S(1)} %get-tuple-element.35), channel_id=1, source_target_pairs={{0,6},{1,7},{2,4},{3,5},{4,2},{5,3},{6,0},{7,1},{8,14},{9,15},{10,... | collective-permute-start | bytes 516104 | tf_op jit(solution)/shard_map/ppermute | solution.py:18
  98.0 13.0 %collective-permute-start.15 = (bf16[48,1792]{1,0:T(8,128)(2,1)S(1)}, bf16[48,1792]{1,0:T(8,128)(2,1)S(1)}, u32[]{:S(2)}, u32[]{:S(2)}) collective-permute-start(bf16[48,1792]{1,0:T(8,128)(2,1)S(1)} %get-tuple-element.36), channel_id=1, source_target_pairs={{0,7},{1,6},{2,5},{3,4},{4,3},{5,2},{6,1},{7,0},{8,15},{9,14},{10,... | collective-permute-start | bytes 516104 | tf_op jit(solution)/shard_map/ppermute | solution.py:18
  99.5 7.4 %collective-permute-start = (bf16[576,128]{1,0:T(8,128)(2,1)S(1)}, bf16[576,128]{1,0:T(8,128)(2,1)S(1)}, u32[]{:S(2)}, u32[]{:S(2)}) collective-permute-start(bf16[576,128]{1,0:T(8,128)(2,1)S(1)} %bitcast.45), channel_id=1, source_target_pairs={{0,8},{8,0},{16,24},{24,16},{1,9},{9,1},{17,25},{25,17},{2,10},{10... | collective-permute-start | bytes 442376 | tf_op jit(solution)/shard_map/ppermute | solution.py:18
  105.5 20.0 %collective-permute-start.33 = (bf16[48,1792]{1,0:T(8,128)(2,1)S(1)}, bf16[48,1792]{1,0:T(8,128)(2,1)S(1)}, u32[]{:S(2)}, u32[]{:S(2)}) collective-permute-start(bf16[48,1792]{1,0:T(8,128)(2,1)S(1)} %get-tuple-element.53), channel_id=1, source_target_pairs={{0,1},{1,0},{2,3},{3,2},{4,5},{5,4},{6,7},{7,6},{8,9},{9,8},{10,11... | collective-permute-start | bytes 516104 | tf_op jit(solution)/shard_map/ppermute | solution.py:18
  106.9 18.7 %collective-permute-start.34 = (bf16[48,1792]{1,0:T(8,128)(2,1)S(1)}, bf16[48,1792]{1,0:T(8,128)(2,1)S(1)}, u32[]{:S(2)}, u32[]{:S(2)}) collective-permute-start(bf16[48,1792]{1,0:T(8,128)(2,1)S(1)} %get-tuple-element.54), channel_id=1, source_target_pairs={{0,2},{1,3},{2,0},{3,1},{4,6},{5,7},{6,4},{7,5},{8,10},{9,11},{10,... | collective-permute-start | bytes 516104 | tf_op jit(solution)/shard_map/ppermute | solution.py:18
  106.9 18.7 %collective-permute-start.35 = (bf16[48,1792]{1,0:T(8,128)(2,1)S(1)}, bf16[48,1792]{1,0:T(8,128)(2,1)S(1)}, u32[]{:S(2)}, u32[]{:S(2)}) collective-permute-start(bf16[48,1792]{1,0:T(8,128)(2,1)S(1)} %get-tuple-element.55), channel_id=1, source_target_pairs={{0,3},{1,2},{2,1},{3,0},{4,7},{5,6},{6,5},{7,4},{8,11},{9,10},{10,... | collective-permute-start | bytes 516104 | tf_op jit(solution)/shard_map/ppermute | solution.py:18
  109.1 16.5 %collective-permute-start.36 = (bf16[48,1792]{1,0:T(8,128)(2,1)S(1)}, bf16[48,1792]{1,0:T(8,128)(2,1)S(1)}, u32[]{:S(2)}, u32[]{:S(2)}) collective-permute-start(bf16[48,1792]{1,0:T(8,128)(2,1)S(1)} %get-tuple-element.56), channel_id=1, source_target_pairs={{0,4},{1,5},{2,6},{3,7},{4,0},{5,1},{6,2},{7,3},{8,12},{9,13},{10,... | collective-permute-start | bytes 516104 | tf_op jit(solution)/shard_map/ppermute | solution.py:18
  110.9 16.7 %collective-permute-start.37 = (bf16[48,1792]{1,0:T(8,128)(2,1)S(1)}, bf16[48,1792]{1,0:T(8,128)(2,1)S(1)}, u32[]{:S(2)}, u32[]{:S(2)}) collective-permute-start(bf16[48,1792]{1,0:T(8,128)(2,1)S(1)} %get-tuple-element.57), channel_id=1, source_target_pairs={{0,5},{1,4},{2,7},{3,6},{4,1},{5,0},{6,3},{7,2},{8,13},{9,12},{10,... | collective-permute-start | bytes 516104 | tf_op jit(solution)/shard_map/ppermute | solution.py:18
  (17 other events, 147.3 us)

commit v3 on v2

--- a/solution.py
+++ b/solution.py
@@ -19,12 +19,12 @@
 
 
 def set_members(expert_count):
-    cut = expert_count - expert_count // 4
-    return [list(range(cut, expert_count)), list(range(cut))]
+    half, cut = expert_count // 2, expert_count - expert_count // 4
+    return [list(range(cut, expert_count)), list(range(half, cut)), list(range(half))]
 
 
 def is_doubled(ctx_size, width):
-    return ctx_size == 4 and width % 256 == 0
+    return ctx_size == 4 and width % 128 == 0
 
 
 def where_am_i():
@@ -106,46 +106,33 @@
     chosen = chosen.astype(jnp.bfloat16)
     sources = refs[: 2 if members else 1]
     targets = refs[len(sources) :]
-    own, half = sources[0], sources[0].shape[1] // 2
-
-    def send(group, columns, outs, at):
-        pick = jnp.concatenate(
-            [chosen[k * capacity : (k + 1) * capacity, :] for k in group], axis=0
-        )
-        rows = jnp.dot(pick, columns, preferred_element_type=jnp.float32).astype(own.dtype)
-        for n, out in enumerate(outs):
-            out[:, at : at + rows.shape[1]] = rows[n * capacity : (n + 1) * capacity, :]
-
-    whole = [k for k in range(expert_count) if k not in members]
-    send(whole, own[...], targets[: len(whole)], 0)
-    if members:
-        late = targets[len(whole) : len(whole) + len(members)]
-        first = targets[len(whole) + len(members) :]
-        send(members, own[:, half:], late, 0)
-        send(members, own[:, :half], first, 0)
-        send(members, sources[1][...], first, half)
+    width = sources[0].shape[1]
+    for n, source in enumerate(sources):
+        group = members if n else range(expert_count)
+        pick = chosen
+        if n:
+            pick = jnp.concatenate(
+                [chosen[k * capacity : (k + 1) * capacity, :] for k in group], axis=0
+            )
+        rows = jnp.dot(pick, source[...], preferred_element_type=jnp.float32).astype(source.dtype)
+        for at, k in enumerate(group):
+            targets[k][:, n * width : (n + 1) * width] = rows[at * capacity : (at + 1) * capacity, :]
 
 
 def dispatch(tokens, ids, capacity, expert_count, width, members, where):
-    token_count = tokens.shape[0]
     operand, spec = own_columns(tokens, width, where)
     operands, specs = [operand], [spec]
     if members:
         operands.append(tokens)
-        specs.append(pl.BlockSpec((token_count, width // 2), lambda i, w: (0, (w[1] ^ 2) * 2)))
-    widths = [width] * (expert_count - len(members)) + [width // 2] * len(members)
-    widths += [width] * len(members)
-    blocks = [(capacity, w) for w in widths]
-    outs = call(
+        specs.append(pl.BlockSpec((tokens.shape[0], width), lambda i, w: (0, w[1] ^ 2)))
+    blocks = [(capacity, 2 * width if k in members else width) for k in range(expert_count)]
+    return call(
         functools.partial(dispatch_kernel, capacity, expert_count, members), (1,),
         [ids, *operands], [whole_spec(ids.shape), *specs],
         [jax.ShapeDtypeStruct(block, tokens.dtype) for block in blocks],
         [whole_spec(block) for block in blocks],
-        2 * expert_count * capacity * token_count * width, where,
-    )
-    order = [k for k in range(expert_count) if k not in members] + members
-    first = dict(zip(members, outs[expert_count:]))
-    return dict(zip(order, outs)), first
+        2 * expert_count * capacity * tokens.shape[0] * width, where,
+    )
 
 
 def pack_kernel(where_ref, *refs):
@@ -188,12 +175,13 @@
     rows = pieces[0][0].shape[0]
     arrays = [piece[0] for piece in pieces]
     specs = [
-        pl.BlockSpec((w, hidden_width), lambda i, m, k=k, n=width // w, b=b: ((m[1] ^ k) * n + b, 0))
-        for x, at, k, b, w in pieces
+        pl.BlockSpec((width, hidden_width), lambda i, m, k=k: (m[1] ^ k, 0)) for x, at, k in pieces
     ]
     row_specs = [
-        whole_spec(x.shape) if x.shape[1] == w else pl.BlockSpec((rows, w), lambda i, m, at=at: (0, at))
-        for x, at, k, b, w in pieces
+        whole_spec(x.shape)
+        if x.shape[1] == width
+        else pl.BlockSpec((rows, width), lambda i, m, at=at: (0, at))
+        for x, at, k in pieces
     ]
     operands = [gate_matrix] * count + [up_matrix] * count + arrays
     specs = specs + specs + row_specs
@@ -203,7 +191,7 @@
         kernel, out = mlp_kernel, jax.ShapeDtypeStruct((rows, hidden_width), arrays[0].dtype)
         operands.append(partial)
         specs.append(whole_spec(partial.shape))
-    columns = sum(piece[4] for piece in pieces)
+    columns = count * width
     return call(
         functools.partial(kernel, count), (1,), operands, specs, out, whole_spec(out.shape),
         4 * rows * columns * hidden_width, where, vmem=24 << 20,
@@ -346,10 +334,15 @@
         key_positions = block_positions(starts_ref, where_ref[1] ^ j, token_count, 0)
         late[at, :] = jnp.where(key_positions <= query_positions, 0.0, neg_fill)
 
-    @pl.loop(0, queries_ref.shape[0])
-    def _(head):
-        scores = jnp.dot(joined[...], queries_ref[head], preferred_element_type=jnp.float32)
-        hidden = late[...] < 0.0
+    head_count = queries_ref.shape[0]
+    together = 2 if head_count % 2 == 0 else 1
+
+    @pl.loop(0, head_count // together)
+    def _(group):
+        heads = [group * together + n for n in range(together)]
+        rows = jnp.concatenate([queries_ref[head] for head in heads], axis=1)
+        scores = jnp.dot(joined[...], rows, preferred_element_type=jnp.float32)
+        hidden = jnp.concatenate([late[...]] * together, axis=1) < 0.0
         masked = jnp.where(hidden, neg_fill, scores * score_scale)
         top_score = jnp.max(masked, axis=0, keepdims=True)
         weights = jnp.where(hidden, 0.0, jnp.exp(masked - top_score))
@@ -358,9 +351,11 @@
             flipped[:lat_width, :], weights.astype(jnp.bfloat16), preferred_element_type=jnp.float32
         )
         latent_out = (blended / totals).astype(jnp.bfloat16)
-        out_ref[head] = lax.dot_general(
-            latent_out, uv_ref[head], (((0,), (0,)), ((), ())), preferred_element_type=jnp.float32
-        ).astype(out_ref.dtype)
+        for n, head in enumerate(heads):
+            part = latent_out[:, n * token_count : (n + 1) * token_count]
+            out_ref[head] = lax.dot_general(
+                part, uv_ref[head], (((0,), (0,)), ((), ())), preferred_element_type=jnp.float32
+            ).astype(out_ref.dtype)
 
 
 def attention(queries, keys, block_starts, w_uv, where):
@@ -398,7 +393,7 @@
 
     sets = set_members(expert_count)
     doubled = sets[-1] if is_doubled(ctx_size, width) else []
-    outgoing, first = dispatch(
+    outgoing = dispatch(
         moe_tokens, expert_ids.T, capacity, expert_count, width, doubled, where
     )
     arrived = [swap(outgoing[k], "exp", k) if k else outgoing[0] for k in range(expert_count)]
@@ -407,18 +402,14 @@
     for members in sets:
         own = pack([arrived[k] for k in members], where)
         beside = swap(own, "ctx", 1)
-        w, b = own.shape[1], width // own.shape[1] - 1
-        early = [(own, 0, 0, b, w), (beside, 0, 1, b, w)]
-        late = []
-        for offset in evens:
-            crossed = swap(own, "ctx", offset)
-            late += [(crossed, 0, offset, b, w)]
-            late += [(swap(crossed, "ctx", 1), 0, offset + 1, b, w)]
-        if w != width:
-            both = [swap(first[k], "exp", k) if k else first[k] for k in members]
-            both = pack(both, where)
-            other = swap(both, "ctx", 1)
-            early += [(both, 0, 0, 0, w), (both, 1, 2, 0, w), (other, 0, 1, 0, w), (other, 1, 3, 0, w)]
+        if own.shape[1] > width:
+            early, late = [(own, 0, 0), (own, 1, 2)], [(beside, 0, 1), (beside, 1, 3)]
+        else:
+            early, late = [(own, 0, 0), (beside, 0, 1)], []
+            for offset in evens:
+                crossed = swap(own, "ctx", offset)
+                late += [(crossed, 0, offset)]
+                late += [(swap(crossed, "ctx", 1), 0, offset + 1)]
         partial = mlp(early, width, w_gate[0], w_up[0], None, where)
         hidden = mlp(late, width, w_gate[0], w_up[0], partial, where)
         hidden = [hidden] + [swap(hidden, "ctx", offset) for offset in range(1, ctx_size)]
@@ -433,7 +424,7 @@
         keys[offset + 1] = swap(keys[offset], "ctx", 1)
     attended = attention(jnp.transpose(queries, (1, 2, 0)), keys, block_starts, w_uv, where)
     attended = jnp.transpose(attended, (1, 0, 2))
-    return attended, combine(returned, sets, expert_ids.T, gate_weights.T, where)
+    return attended, combine(returned, [sets[0], sets[2], sets[1]], expert_ids.T, gate_weights.T, where)
 
 
 def solution(mesh):

time: 130 us -> 140 us (1.077)
  waiting for transfers between devices: 36 us -> 76.8 us
  starting transfers between devices: 66.2 us -> 36.9 us
    ppermute x38 -> x36, waiting for transfers between devices: 36 us -> 76.8 us  [swap(): return lax.ppermute(x, axis, [(i, i ^ offset) for i in range(size)])]
    ppermute x38 -> x36, starting transfers between devices: 66.2 us -> 36.9 us  [swap(): return lax.ppermute(x, axis, [(i, i ^ offset) for i in range(size)])]
    pallas_call x14 -> x17, Pallas kernels: 23.3 us -> 22.3 us  [call(): pl.pallas_call(kernel, out_shape=out_shape, grid_spec=pltpu.PrefetchScala...]
  transfers between devices with their start and end apart: 38 -> 36, of which waited for: 10 -> 15; matrix products, arithmetic and copies ran while one was open for 1% -> 1% of each run, Pallas kernels for 15% -> 13%
where the time goes in v3:
time: 140 us
  waiting for transfers between devices  76.8 us (55%)
  starting transfers between devices  36.9 us (26%)
  Pallas kernels  22.3 us (16%)
  local copies, waits for them, and re-layouts  3.1 us (2%)
    ppermute x36, waiting for transfers between devices, swap(): return lax.ppermute(x, axis, [(i, i ^ offset) for i in range(size)])  76.8 us
    ppermute x36, starting transfers between devices, swap(): return lax.ppermute(x, axis, [(i, i ^ offset) for i in range(size)])  36.9 us
    pallas_call x17, Pallas kernels, call(): pl.pallas_call(kernel, out_shape=out_shape, grid_spec=pltpu.PrefetchScala...  22.3 us
    unnamed x23, local copies, waits for them, and re-layouts  3.1 us
  transfers between devices with their start and end apart: 36, of which 15 were waited for; matrix products, arithmetic and copies ran while one was open for 1% of the time, Pallas kernels for 13%

profile of v3, /device:TPU:0, one launch (start us, length us, event | category | flops | bytes accessed | tf_op | source)
XLA Modules:
  0.0 140.1 jit_solution(13206398798841809079)
XLA Ops:
  0.7 1.5 %copy-done.3 = bf16[128,7168]{1,0:T(8,128)(2,1)S(1)} copy-done((bf16[128,7168]{1,0:T(8,128)(2,1)S(1)}, bf16[128,7168]{1,0:T(8,128)(2,1)}, u32[]{:S(2)}) %copy-start.3) | copy-done | bytes 1835032
  2.9 1.4 shard_map.114
  4.3 3.0 %collective-permute-start.16 = (bf16[48,3584]{1,0:T(8,128)(2,1)S(1)}, bf16[48,3584]{1,0:T(8,128)(2,1)S(1)}, u32[]{:S(2)}, u32[]{:S(2)}) collective-permute-start(bf16[48,3584]{1,0:T(8,128)(2,1)S(1)} %get-tuple-element.32), channel_id=1, source_target_pairs={{0,1},{1,0},{2,3},{3,2},{4,5},{5,4},{6,7},{7,6},{8,9},{9,8},{10,11... | collective-permute-start | bytes 1032200 | tf_op jit(solution)/shard_map/ppermute | solution.py:18
  7.3 1.6 %collective-permute-start.17 = (bf16[48,3584]{1,0:T(8,128)(2,1)S(1)}, bf16[48,3584]{1,0:T(8,128)(2,1)S(1)}, u32[]{:S(2)}, u32[]{:S(2)}) collective-permute-start(bf16[48,3584]{1,0:T(8,128)(2,1)S(1)} %get-tuple-element.33), channel_id=1, source_target_pairs={{0,2},{1,3},{2,0},{3,1},{4,6},{5,7},{6,4},{7,5},{8,10},{9,11},{10,... | collective-permute-start | bytes 1032200 | tf_op jit(solution)/shard_map/ppermute | solution.py:18
  8.9 6.5 %collective-permute-done.16.refs_1_ = bf16[48,3584]{1,0:T(8,128)(2,1)S(1)} collective-permute-done((bf16[48,3584]{1,0:T(8,128)(2,1)S(1)}, bf16[48,3584]{1,0:T(8,128)(2,1)S(1)}, u32[]{:S(2)}, u32[]{:S(2)}) %collective-permute-start.16) | collective-permute-done | bytes 344096 | tf_op jit(solution)/shard_map/ppermute | solution.py:18
  15.4 2.9 %collective-permute-done.17.refs_2_ = bf16[48,3584]{1,0:T(8,128)(2,1)S(1)} collective-permute-done((bf16[48,3584]{1,0:T(8,128)(2,1)S(1)}, bf16[48,3584]{1,0:T(8,128)(2,1)S(1)}, u32[]{:S(2)}, u32[]{:S(2)}) %collective-permute-start.17) | collective-permute-done | bytes 344096 | tf_op jit(solution)/shard_map/ppermute | solution.py:18
  18.2 5.8 %collective-permute-done.18.refs_3_ = bf16[48,3584]{1,0:T(8,128)(2,1)S(1)} collective-permute-done((bf16[48,3584]{1,0:T(8,128)(2,1)S(1)}, bf16[48,3584]{1,0:T(8,128)(2,1)S(1)}, u32[]{:S(2)}, u32[]{:S(2)}) %collective-permute-start.18) | collective-permute-done | bytes 344096 | tf_op jit(solution)/shard_map/ppermute | solution.py:18
  24.7 3.8 %collective-permute-start.3 = (bf16[48,1792]{1,0:T(8,128)(2,1)S(1)}, bf16[48,1792]{1,0:T(8,128)(2,1)S(1)}, u32[]{:S(2)}, u32[]{:S(2)}) collective-permute-start(bf16[48,1792]{1,0:T(8,128)(2,1)S(1)} %get-tuple-element.24), channel_id=1, source_target_pairs={{0,6},{1,7},{2,4},{3,5},{4,2},{5,3},{6,0},{7,1},{8,14},{9,15},{10,... | collective-permute-start | bytes 516104 | tf_op jit(solution)/shard_map/ppermute | solution.py:18
  30.5 2.0 %collective-permute-start.27 = (bf16[48,1792]{1,0:T(8,128)(2,1)S(1)}, bf16[48,1792]{1,0:T(8,128)(2,1)S(1)}, u32[]{:S(2)}, u32[]{:S(2)}) collective-permute-start(bf16[48,1792]{1,0:T(8,128)(2,1)S(1)} %get-tuple-element.43), channel_id=1, source_target_pairs={{0,5},{1,4},{2,7},{3,6},{4,1},{5,0},{6,3},{7,2},{8,13},{9,12},{10,... | collective-permute-start | bytes 516104 | tf_op jit(solution)/shard_map/ppermute | solution.py:18
  33.6 5.1 %collective-permute-done.4.refs_1_ = bf16[48,1792]{1,0:T(8,128)(2,1)S(1)} collective-permute-done((bf16[48,1792]{1,0:T(8,128)(2,1)S(1)}, bf16[48,1792]{1,0:T(8,128)(2,1)S(1)}, u32[]{:S(2)}, u32[]{:S(2)}) %collective-permute-start.4) | collective-permute-done | bytes 172064 | tf_op jit(solution)/shard_map/ppermute | solution.py:18
  39.3 1.6 %collective-permute-start.5 = (bf16[96,1792]{1,0:T(8,128)(2,1)S(1)}, bf16[96,1792]{1,0:T(8,128)(2,1)S(1)}, u32[]{:S(2)}, u32[]{:S(2)}) collective-permute-start(bf16[96,1792]{1,0:T(8,128)(2,1)S(1)} %shard_map.115.refs_4_), channel_id=1, source_target_pairs={{0,16},{8,24},{16,0},{24,8},{1,17},{9,25},{17,1},{25,9},{2,18},{10... | collective-permute-start | bytes 1032200 | tf_op jit(solution)/shard_map/ppermute | solution.py:18
  40.9 14.5 %collective-permute-done.26.refs_0_ = bf16[48,1792]{1,0:T(8,128)(2,1)S(1)} collective-permute-done((bf16[48,1792]{1,0:T(8,128)(2,1)S(1)}, bf16[48,1792]{1,0:T(8,128)(2,1)S(1)}, u32[]{:S(2)}, u32[]{:S(2)}) %collective-permute-start.26) | collective-permute-done | bytes 172064 | tf_op jit(solution)/shard_map/ppermute | solution.py:18
  55.3 4.1 %collective-permute-done.27.refs_1_ = bf16[48,1792]{1,0:T(8,128)(2,1)S(1)} collective-permute-done((bf16[48,1792]{1,0:T(8,128)(2,1)S(1)}, bf16[48,1792]{1,0:T(8,128)(2,1)S(1)}, u32[]{:S(2)}, u32[]{:S(2)}) %collective-permute-start.27) | collective-permute-done | bytes 172064 | tf_op jit(solution)/shard_map/ppermute | solution.py:18
  60.0 1.6 %collective-permute-start.28 = (bf16[96,1792]{1,0:T(8,128)(2,1)S(1)}, bf16[96,1792]{1,0:T(8,128)(2,1)S(1)}, u32[]{:S(2)}, u32[]{:S(2)}) collective-permute-start(bf16[96,1792]{1,0:T(8,128)(2,1)S(1)} %shard_map.125.refs_4_), channel_id=1, source_target_pairs={{0,16},{8,24},{16,0},{24,8},{1,17},{9,25},{17,1},{25,9},{2,18},{10... | collective-permute-start | bytes 1032200 | tf_op jit(solution)/shard_map/ppermute | solution.py:18
  62.1 10.7 %collective-permute-done.1.refs_2_ = bf16[576,128]{1,0:T(8,128)(2,1)S(1)} collective-permute-done((bf16[576,128]{1,0:T(8,128)(2,1)S(1)}, bf16[576,128]{1,0:T(8,128)(2,1)S(1)}, u32[]{:S(2)}, u32[]{:S(2)}) %collective-permute-start.1) | collective-permute-done | bytes 147488 | tf_op jit(solution)/shard_map/ppermute | solution.py:18
  73.3 1.5 %collective-permute-start.12 = (bf16[128,1792]{1,0:T(8,128)(2,1)S(1)}, bf16[128,1792]{1,0:T(8,128)(2,1)S(1)}, u32[]{:S(2)}, u32[]{:S(2)}) collective-permute-start(bf16[128,1792]{1,0:T(8,128)(2,1)S(1)} %get-tuple-element.27), channel_id=1, source_target_pairs={{0,16},{8,24},{16,0},{24,8},{1,17},{9,25},{17,1},{25,9},{2,18},{10... | collective-permute-start | bytes 1376264 | tf_op jit(solution)/shard_map/ppermute | solution.py:18
  77.5 9.2 %collective-permute-done.12.refs_6_ = bf16[128,1792]{1,0:T(8,128)(2,1)S(1)} collective-permute-done((bf16[128,1792]{1,0:T(8,128)(2,1)S(1)}, bf16[128,1792]{1,0:T(8,128)(2,1)S(1)}, u32[]{:S(2)}, u32[]{:S(2)}) %collective-permute-start.12) | collective-permute-done | bytes 458784 | tf_op jit(solution)/shard_map/ppermute | solution.py:18
  86.7 8.2 %collective-permute-done.13.refs_7_ = bf16[128,1792]{1,0:T(8,128)(2,1)S(1)} collective-permute-done((bf16[128,1792]{1,0:T(8,128)(2,1)S(1)}, bf16[128,1792]{1,0:T(8,128)(2,1)S(1)}, u32[]{:S(2)}, u32[]{:S(2)}) %collective-permute-start.13) | collective-permute-done | bytes 458784 | tf_op jit(solution)/shard_map/ppermute | solution.py:18
  96.9 1.5 %collective-permute-start.9 = (bf16[96,128]{1,0:T(8,128)(2,1)S(1)}, bf16[96,128]{1,0:T(8,128)(2,1)S(1)}, u32[]{:S(2)}, u32[]{:S(2)}) collective-permute-start(bf16[96,128]{1,0:T(8,128)(2,1)S(1)} %shard_map.117.refs_0_), channel_id=1, source_target_pairs={{0,16},{8,24},{16,0},{24,8},{1,17},{9,25},{17,1},{25,9},{2,18},{10... | collective-permute-start | bytes 73736 | tf_op jit(solution)/shard_map/ppermute | solution.py:18
  98.4 2.3 %collective-permute-done.9.refs_2_ = bf16[96,128]{1,0:T(8,128)(2,1)S(1)} collective-permute-done((bf16[96,128]{1,0:T(8,128)(2,1)S(1)}, bf16[96,128]{1,0:T(8,128)(2,1)S(1)}, u32[]{:S(2)}, u32[]{:S(2)}) %collective-permute-start.9) | collective-permute-done | bytes 24608 | tf_op jit(solution)/shard_map/ppermute | solution.py:18
  101.7 2.5 %collective-permute-start.14 = (bf16[48,1792]{1,0:T(8,128)(2,1)S(1)}, bf16[48,1792]{1,0:T(8,128)(2,1)S(1)}, u32[]{:S(2)}, u32[]{:S(2)}) collective-permute-start(bf16[48,1792]{1,0:T(8,128)(2,1)S(1)} %get-tuple-element.29), channel_id=1, source_target_pairs={{0,6},{1,7},{2,4},{3,5},{4,2},{5,3},{6,0},{7,1},{8,14},{9,15},{10,... | collective-permute-start | bytes 516104 | tf_op jit(solution)/shard_map/ppermute | solution.py:18
  107.8 1.6 %collective-permute-start.21 = (bf16[192,128]{1,0:T(8,128)(2,1)S(1)}, bf16[192,128]{1,0:T(8,128)(2,1)S(1)}, u32[]{:S(2)}, u32[]{:S(2)}) collective-permute-start(bf16[192,128]{1,0:T(8,128)(2,1)S(1)} %shard_map.122.refs_0_), channel_id=1, source_target_pairs={{0,16},{8,24},{16,0},{24,8},{1,17},{9,25},{17,1},{25,9},{2,18},{10... | collective-permute-start | bytes 147464 | tf_op jit(solution)/shard_map/ppermute | solution.py:18
  112.1 1.9 %collective-permute-start.32 = (bf16[96,128]{1,0:T(8,128)(2,1)S(1)}, bf16[96,128]{1,0:T(8,128)(2,1)S(1)}, u32[]{:S(2)}, u32[]{:S(2)}) collective-permute-start(bf16[96,128]{1,0:T(8,128)(2,1)S(1)} %shard_map.127.refs_0_), channel_id=1, source_target_pairs={{0,16},{8,24},{16,0},{24,8},{1,17},{9,25},{17,1},{25,9},{2,18},{10... | collective-permute-start | bytes 73736 | tf_op jit(solution)/shard_map/ppermute | solution.py:18
  115.4 1.6 %collective-permute-start.23 = (bf16[48,1792]{1,0:T(8,128)(2,1)S(1)}, bf16[48,1792]{1,0:T(8,128)(2,1)S(1)}, u32[]{:S(2)}, u32[]{:S(2)}) collective-permute-start(bf16[48,1792]{1,0:T(8,128)(2,1)S(1)} %get-tuple-element.36), channel_id=1, source_target_pairs={{0,1},{1,0},{2,3},{3,2},{4,5},{5,4},{6,7},{7,6},{8,9},{9,8},{10,11... | collective-permute-start | bytes 516104 | tf_op jit(solution)/shard_map/ppermute | solution.py:18
  117.3 1.7 %collective-permute-start.25 = (bf16[48,1792]{1,0:T(8,128)(2,1)S(1)}, bf16[48,1792]{1,0:T(8,128)(2,1)S(1)}, u32[]{:S(2)}, u32[]{:S(2)}) collective-permute-start(bf16[48,1792]{1,0:T(8,128)(2,1)S(1)} %get-tuple-element.38), channel_id=1, source_target_pairs={{0,3},{1,2},{2,1},{3,0},{4,7},{5,6},{6,5},{7,4},{8,11},{9,10},{10,... | collective-permute-start | bytes 516104 | tf_op jit(solution)/shard_map/ppermute | solution.py:18
  120.0 2.3 %collective-permute-start.34 = (bf16[48,1792]{1,0:T(8,128)(2,1)S(1)}, bf16[48,1792]{1,0:T(8,128)(2,1)S(1)}, u32[]{:S(2)}, u32[]{:S(2)}) collective-permute-start(bf16[48,1792]{1,0:T(8,128)(2,1)S(1)} %get-tuple-element.44), channel_id=1, source_target_pairs={{0,4},{1,5},{2,6},{3,7},{4,0},{5,1},{6,2},{7,3},{8,12},{9,13},{10,... | collective-permute-start | bytes 516104 | tf_op jit(solution)/shard_map/ppermute | solution.py:18
  122.3 1.6 %collective-permute-start.35 = (bf16[48,1792]{1,0:T(8,128)(2,1)S(1)}, bf16[48,1792]{1,0:T(8,128)(2,1)S(1)}, u32[]{:S(2)}, u32[]{:S(2)}) collective-permute-start(bf16[48,1792]{1,0:T(8,128)(2,1)S(1)} %get-tuple-element.45), channel_id=1, source_target_pairs={{0,5},{1,4},{2,7},{3,6},{4,1},{5,0},{6,3},{7,2},{8,13},{9,12},{10,... | collective-permute-start | bytes 516104 | tf_op jit(solution)/shard_map/ppermute | solution.py:18
  123.9 6.0 %shard_map.113 = bf16[8,128,128]{2,1,0:T(8,128)(2,1)S(1)} custom-call(s32[2]{0:T(128)S(1)} %pad_add_fusion.where_ref, s32[8]{0:T(128)S(1)} %copy-done.10, bf16[8,576,128]{2,1,0:T(8,128)(2,1)S(1)} %bitcast.44, bf16[8,512,128]{2,1,0:T(8,128)(2,1)S(1)} %copy-done.8, bf16[576,128]{1,0:T(8,128)(2,1)S(1)} %bitcast.47, ...), custom_call_target="tpu_custom_call" | custom-call | flops 1207959552 | bytes 3080192 | tf_op jit(solution)/shard_map/pallas_call | solution.py:42
  130.8 1.7 %shard_map.124 = (f32[128,1792]{1,0:T(8,128)S(1)}, bf16[256,96]{1,0:T(8,128)(2,1)S(1)}, f32[128,8]{1,0:T(8,128)S(1)}) custom-call(s32[2]{0:T(128)S(1)} %pad_add_fusion.where_ref, s32[2,128]{1,0:T(2,128)S(1)} %bitcast.42, f32[2,128]{1,0:T(2,128)S(1)} %bitcast.43, bf16[48,1792]{1,0:T(8,128)(2,1)S(1)} %collective-permute-done.14.refs_0_, ...), custom_call_target="tpu_custom_call" | custom-call | flops 264241152 | bytes 2004992 | tf_op jit(solution)/shard_map/pallas_call | solution.py:42
  132.5 2.8 %collective-permute-done.34.refs_0_ = bf16[48,1792]{1,0:T(8,128)(2,1)S(1)} collective-permute-done((bf16[48,1792]{1,0:T(8,128)(2,1)S(1)}, bf16[48,1792]{1,0:T(8,128)(2,1)S(1)}, u32[]{:S(2)}, u32[]{:S(2)}) %collective-permute-start.34) | collective-permute-done | bytes 172064 | tf_op jit(solution)/shard_map/ppermute | solution.py:18
  135.4 3.0 %collective-permute-done.35.refs_1_ = bf16[48,1792]{1,0:T(8,128)(2,1)S(1)} collective-permute-done((bf16[48,1792]{1,0:T(8,128)(2,1)S(1)}, bf16[48,1792]{1,0:T(8,128)(2,1)S(1)}, u32[]{:S(2)}, u32[]{:S(2)}) %collective-permute-start.35) | collective-permute-done | bytes 172064 | tf_op jit(solution)/shard_map/ppermute | solution.py:18
  138.4 1.7 %shard_map.129 = bf16[128,1792]{1,0:T(8,128)(2,1)} custom-call(s32[2]{0:T(128)S(1)} %pad_add_fusion.where_ref, f32[128,1792]{1,0:T(8,128)S(1)} %get-tuple-element.39.sum_ref, bf16[256,96]{1,0:T(8,128)(2,1)S(1)} %get-tuple-element.40.hits_ref, f32[128,8]{1,0:T(8,128)S(1)} %get-tuple-element.41.columns_ref, ...), custom_call_target="tpu_custom_call" | custom-call | flops 88080384 | bytes 1773568 | tf_op jit(solution)/shard_map/pallas_call | solution.py:42
  (81 shorter events, 22.1 us)
Async XLA Ops:
  4.3 11.1 %collective-permute-start.16 = (bf16[48,3584]{1,0:T(8,128)(2,1)S(1)}, bf16[48,3584]{1,0:T(8,128)(2,1)S(1)}, u32[]{:S(2)}, u32[]{:S(2)}) collective-permute-start(bf16[48,3584]{1,0:T(8,128)(2,1)S(1)} %get-tuple-element.32), channel_id=1, source_target_pairs={{0,1},{1,0},{2,3},{3,2},{4,5},{5,4},{6,7},{7,6},{8,9},{9,8},{10,11... | collective-permute-start | bytes 1032200 | tf_op jit(solution)/shard_map/ppermute | solution.py:18
  7.3 10.9 %collective-permute-start.17 = (bf16[48,3584]{1,0:T(8,128)(2,1)S(1)}, bf16[48,3584]{1,0:T(8,128)(2,1)S(1)}, u32[]{:S(2)}, u32[]{:S(2)}) collective-permute-start(bf16[48,3584]{1,0:T(8,128)(2,1)S(1)} %get-tuple-element.33), channel_id=1, source_target_pairs={{0,2},{1,3},{2,0},{3,1},{4,6},{5,7},{6,4},{7,5},{8,10},{9,11},{10,... | collective-permute-start | bytes 1032200 | tf_op jit(solution)/shard_map/ppermute | solution.py:18
  8.9 15.1 %collective-permute-start.18 = (bf16[48,3584]{1,0:T(8,128)(2,1)S(1)}, bf16[48,3584]{1,0:T(8,128)(2,1)S(1)}, u32[]{:S(2)}, u32[]{:S(2)}) collective-permute-start(bf16[48,3584]{1,0:T(8,128)(2,1)S(1)} %get-tuple-element.34), channel_id=1, source_target_pairs={{0,3},{1,2},{2,1},{3,0},{4,7},{5,6},{6,5},{7,4},{8,11},{9,10},{10,... | collective-permute-start | bytes 1032200 | tf_op jit(solution)/shard_map/ppermute | solution.py:18
  24.6 79.6 %collective-permute-start.19 = (bf16[192,3584]{1,0:T(8,128)(2,1)S(1)}, bf16[192,3584]{1,0:T(8,128)(2,1)S(1)}, u32[]{:S(2)}, u32[]{:S(2)}) collective-permute-start(bf16[192,3584]{1,0:T(8,128)(2,1)S(1)} %shard_map.120.refs_4_.refs_5_), channel_id=1, source_target_pairs={{0,8},{8,0},{16,24},{24,16},{1,9},{9,1},{17,25},{25,17},{2,10},{10... | collective-permute-start | bytes 4128776 | tf_op jit(solution)/shard_map/ppermute | solution.py:18
  24.7 8.9 %collective-permute-start.3 = (bf16[48,1792]{1,0:T(8,128)(2,1)S(1)}, bf16[48,1792]{1,0:T(8,128)(2,1)S(1)}, u32[]{:S(2)}, u32[]{:S(2)}) collective-permute-start(bf16[48,1792]{1,0:T(8,128)(2,1)S(1)} %get-tuple-element.24), channel_id=1, source_target_pairs={{0,6},{1,7},{2,4},{3,5},{4,2},{5,3},{6,0},{7,1},{8,14},{9,15},{10,... | collective-permute-start | bytes 516104 | tf_op jit(solution)/shard_map/ppermute | solution.py:18
  28.6 10.2 %collective-permute-start.4 = (bf16[48,1792]{1,0:T(8,128)(2,1)S(1)}, bf16[48,1792]{1,0:T(8,128)(2,1)S(1)}, u32[]{:S(2)}, u32[]{:S(2)}) collective-permute-start(bf16[48,1792]{1,0:T(8,128)(2,1)S(1)} %get-tuple-element.25), channel_id=1, source_target_pairs={{0,7},{1,6},{2,5},{3,4},{4,3},{5,2},{6,1},{7,0},{8,15},{9,14},{10,... | collective-permute-start | bytes 516104 | tf_op jit(solution)/shard_map/ppermute | solution.py:18
  29.7 25.6 %collective-permute-start.26 = (bf16[48,1792]{1,0:T(8,128)(2,1)S(1)}, bf16[48,1792]{1,0:T(8,128)(2,1)S(1)}, u32[]{:S(2)}, u32[]{:S(2)}) collective-permute-start(bf16[48,1792]{1,0:T(8,128)(2,1)S(1)} %get-tuple-element.42), channel_id=1, source_target_pairs={{0,4},{1,5},{2,6},{3,7},{4,0},{5,1},{6,2},{7,3},{8,12},{9,13},{10,... | collective-permute-start | bytes 516104 | tf_op jit(solution)/shard_map/ppermute | solution.py:18
  30.5 28.9 %collective-permute-start.27 = (bf16[48,1792]{1,0:T(8,128)(2,1)S(1)}, bf16[48,1792]{1,0:T(8,128)(2,1)S(1)}, u32[]{:S(2)}, u32[]{:S(2)}) collective-permute-start(bf16[48,1792]{1,0:T(8,128)(2,1)S(1)} %get-tuple-element.43), channel_id=1, source_target_pairs={{0,5},{1,4},{2,7},{3,6},{4,1},{5,0},{6,3},{7,2},{8,13},{9,12},{10,... | collective-permute-start | bytes 516104 | tf_op jit(solution)/shard_map/ppermute | solution.py:18
  33.6 39.6 %collective-permute-start.11 = (bf16[128,1792]{1,0:T(8,128)(2,1)S(1)}, bf16[128,1792]{1,0:T(8,128)(2,1)S(1)}, u32[]{:S(2)}, u32[]{:S(2)}) collective-permute-start(bf16[128,1792]{1,0:T(8,128)(2,1)S(1)} %get-tuple-element.26), channel_id=1, source_target_pairs={{0,8},{8,0},{16,24},{24,16},{1,9},{9,1},{17,25},{25,17},{2,10},{10... | collective-permute-start | bytes 1376264 | tf_op jit(solution)/shard_map/ppermute | solution.py:18
  39.3 33.5 %collective-permute-start.5 = (bf16[96,1792]{1,0:T(8,128)(2,1)S(1)}, bf16[96,1792]{1,0:T(8,128)(2,1)S(1)}, u32[]{:S(2)}, u32[]{:S(2)}) collective-permute-start(bf16[96,1792]{1,0:T(8,128)(2,1)S(1)} %shard_map.115.refs_4_), channel_id=1, source_target_pairs={{0,16},{8,24},{16,0},{24,8},{1,17},{9,25},{17,1},{25,9},{2,18},{10... | collective-permute-start | bytes 1032200 | tf_op jit(solution)/shard_map/ppermute | solution.py:18
  60.0 14.8 %collective-permute-start.28 = (bf16[96,1792]{1,0:T(8,128)(2,1)S(1)}, bf16[96,1792]{1,0:T(8,128)(2,1)S(1)}, u32[]{:S(2)}, u32[]{:S(2)}) collective-permute-start(bf16[96,1792]{1,0:T(8,128)(2,1)S(1)} %shard_map.125.refs_4_), channel_id=1, source_target_pairs={{0,16},{8,24},{16,0},{24,8},{1,17},{9,25},{17,1},{25,9},{2,18},{10... | collective-permute-start | bytes 1032200 | tf_op jit(solution)/shard_map/ppermute | solution.py:18
  61.6 11.2 %collective-permute-start.1 = (bf16[576,128]{1,0:T(8,128)(2,1)S(1)}, bf16[576,128]{1,0:T(8,128)(2,1)S(1)}, u32[]{:S(2)}, u32[]{:S(2)}) collective-permute-start(bf16[576,128]{1,0:T(8,128)(2,1)S(1)} %bitcast.45), channel_id=1, source_target_pairs={{0,16},{8,24},{16,0},{24,8},{1,17},{9,25},{17,1},{25,9},{2,18},{10... | collective-permute-start | bytes 442376 | tf_op jit(solution)/shard_map/ppermute | solution.py:18
  73.3 13.4 %collective-permute-start.12 = (bf16[128,1792]{1,0:T(8,128)(2,1)S(1)}, bf16[128,1792]{1,0:T(8,128)(2,1)S(1)}, u32[]{:S(2)}, u32[]{:S(2)}) collective-permute-start(bf16[128,1792]{1,0:T(8,128)(2,1)S(1)} %get-tuple-element.27), channel_id=1, source_target_pairs={{0,16},{8,24},{16,0},{24,8},{1,17},{9,25},{17,1},{25,9},{2,18},{10... | collective-permute-start | bytes 1376264 | tf_op jit(solution)/shard_map/ppermute | solution.py:18
  74.8 20.1 %collective-permute-start.13 = (bf16[128,1792]{1,0:T(8,128)(2,1)S(1)}, bf16[128,1792]{1,0:T(8,128)(2,1)S(1)}, u32[]{:S(2)}, u32[]{:S(2)}) collective-permute-start(bf16[128,1792]{1,0:T(8,128)(2,1)S(1)} %get-tuple-element.28), channel_id=1, source_target_pairs={{0,24},{8,16},{16,8},{24,0},{1,25},{9,17},{17,9},{25,1},{2,26},{10... | collective-permute-start | bytes 1376264 | tf_op jit(solution)/shard_map/ppermute | solution.py:18
  74.8 33.0 %collective-permute-start.30 = (bf16[96,1792]{1,0:T(8,128)(2,1)S(1)}, bf16[96,1792]{1,0:T(8,128)(2,1)S(1)}, u32[]{:S(2)}, u32[]{:S(2)}) collective-permute-start(bf16[96,1792]{1,0:T(8,128)(2,1)S(1)} %shard_map.125.refs_4_), channel_id=1, source_target_pairs={{0,8},{8,0},{16,24},{24,16},{1,9},{9,1},{17,25},{25,17},{2,10},{10... | collective-permute-start | bytes 1032200 | tf_op jit(solution)/shard_map/ppermute | solution.py:18
  75.4 34.0 %collective-permute-start.29 = (bf16[96,1792]{1,0:T(8,128)(2,1)S(1)}, bf16[96,1792]{1,0:T(8,128)(2,1)S(1)}, u32[]{:S(2)}, u32[]{:S(2)}) collective-permute-start(bf16[96,1792]{1,0:T(8,128)(2,1)S(1)} %collective-permute-done.28.refs_4_), channel_id=1, source_target_pairs={{0,8},{8,0},{16,24},{24,16},{1,9},{9,1},{17,25},{25,17},{2,10},{10... | collective-permute-start | bytes 1032200 | tf_op jit(solution)/shard_map/ppermute | solution.py:18
  86.7 9.0 %collective-permute-start.10 = (bf16[96,128]{1,0:T(8,128)(2,1)S(1)}, bf16[96,128]{1,0:T(8,128)(2,1)S(1)}, u32[]{:S(2)}, u32[]{:S(2)}) collective-permute-start(bf16[96,128]{1,0:T(8,128)(2,1)S(1)} %shard_map.117.refs_0_), channel_id=1, source_target_pairs={{0,24},{8,16},{16,8},{24,0},{1,25},{9,17},{17,9},{25,1},{2,26},{10... | collective-permute-start | bytes 73736 | tf_op jit(solution)/shard_map/ppermute | solution.py:18
  94.9 6.8 %collective-permute-start = (bf16[576,128]{1,0:T(8,128)(2,1)S(1)}, bf16[576,128]{1,0:T(8,128)(2,1)S(1)}, u32[]{:S(2)}, u32[]{:S(2)}) collective-permute-start(bf16[576,128]{1,0:T(8,128)(2,1)S(1)} %bitcast.46), channel_id=1, source_target_pairs={{0,8},{8,0},{16,24},{24,16},{1,9},{9,1},{17,25},{25,17},{2,10},{10... | collective-permute-start | bytes 442376 | tf_op jit(solution)/shard_map/ppermute | solution.py:18
  96.9 3.8 %collective-permute-start.9 = (bf16[96,128]{1,0:T(8,128)(2,1)S(1)}, bf16[96,128]{1,0:T(8,128)(2,1)S(1)}, u32[]{:S(2)}, u32[]{:S(2)}) collective-permute-start(bf16[96,128]{1,0:T(8,128)(2,1)S(1)} %shard_map.117.refs_0_), channel_id=1, source_target_pairs={{0,16},{8,24},{16,0},{24,8},{1,17},{9,25},{17,1},{25,9},{2,18},{10... | collective-permute-start | bytes 73736 | tf_op jit(solution)/shard_map/ppermute | solution.py:18
  100.7 7.0 %collective-permute-start.2 = (bf16[576,128]{1,0:T(8,128)(2,1)S(1)}, bf16[576,128]{1,0:T(8,128)(2,1)S(1)}, u32[]{:S(2)}, u32[]{:S(2)}) collective-permute-start(bf16[576,128]{1,0:T(8,128)(2,1)S(1)} %collective-permute-done.1.refs_2_), channel_id=1, source_target_pairs={{0,8},{8,0},{16,24},{24,16},{1,9},{9,1},{17,25},{25,17},{2,10},{10... | collective-permute-start | bytes 442376 | tf_op jit(solution)/shard_map/ppermute | solution.py:18
  101.7 18.3 %collective-permute-start.14 = (bf16[48,1792]{1,0:T(8,128)(2,1)S(1)}, bf16[48,1792]{1,0:T(8,128)(2,1)S(1)}, u32[]{:S(2)}, u32[]{:S(2)}) collective-permute-start(bf16[48,1792]{1,0:T(8,128)(2,1)S(1)} %get-tuple-element.29), channel_id=1, source_target_pairs={{0,6},{1,7},{2,4},{3,5},{4,2},{5,3},{6,0},{7,1},{8,14},{9,15},{10,... | collective-permute-start | bytes 516104 | tf_op jit(solution)/shard_map/ppermute | solution.py:18
  104.2 18.1 %collective-permute-start.15 = (bf16[48,1792]{1,0:T(8,128)(2,1)S(1)}, bf16[48,1792]{1,0:T(8,128)(2,1)S(1)}, u32[]{:S(2)}, u32[]{:S(2)}) collective-permute-start(bf16[48,1792]{1,0:T(8,128)(2,1)S(1)} %get-tuple-element.30), channel_id=1, source_target_pairs={{0,7},{1,6},{2,5},{3,4},{4,3},{5,2},{6,1},{7,0},{8,15},{9,14},{10,... | collective-permute-start | bytes 516104 | tf_op jit(solution)/shard_map/ppermute | solution.py:18
  107.7 3.9 %collective-permute-start.20 = (bf16[192,128]{1,0:T(8,128)(2,1)S(1)}, bf16[192,128]{1,0:T(8,128)(2,1)S(1)}, u32[]{:S(2)}, u32[]{:S(2)}) collective-permute-start(bf16[192,128]{1,0:T(8,128)(2,1)S(1)} %shard_map.122.refs_0_), channel_id=1, source_target_pairs={{0,8},{8,0},{16,24},{24,16},{1,9},{9,1},{17,25},{25,17},{2,10},{10... | collective-permute-start | bytes 147464 | tf_op jit(solution)/shard_map/ppermute | solution.py:18
  107.8 4.3 %collective-permute-start.21 = (bf16[192,128]{1,0:T(8,128)(2,1)S(1)}, bf16[192,128]{1,0:T(8,128)(2,1)S(1)}, u32[]{:S(2)}, u32[]{:S(2)}) collective-permute-start(bf16[192,128]{1,0:T(8,128)(2,1)S(1)} %shard_map.122.refs_0_), channel_id=1, source_target_pairs={{0,16},{8,24},{16,0},{24,8},{1,17},{9,25},{17,1},{25,9},{2,18},{10... | collective-permute-start | bytes 147464 | tf_op jit(solution)/shard_map/ppermute | solution.py:18
  109.4 4.6 %collective-permute-start.22 = (bf16[192,128]{1,0:T(8,128)(2,1)S(1)}, bf16[192,128]{1,0:T(8,128)(2,1)S(1)}, u32[]{:S(2)}, u32[]{:S(2)}) collective-permute-start(bf16[192,128]{1,0:T(8,128)(2,1)S(1)} %shard_map.122.refs_0_), channel_id=1, source_target_pairs={{0,24},{8,16},{16,8},{24,0},{1,25},{9,17},{17,9},{25,1},{2,26},{10... | collective-permute-start | bytes 147464 | tf_op jit(solution)/shard_map/ppermute | solution.py:18
  111.7 3.7 %collective-permute-start.31 = (bf16[96,128]{1,0:T(8,128)(2,1)S(1)}, bf16[96,128]{1,0:T(8,128)(2,1)S(1)}, u32[]{:S(2)}, u32[]{:S(2)}) collective-permute-start(bf16[96,128]{1,0:T(8,128)(2,1)S(1)} %shard_map.127.refs_0_), channel_id=1, source_target_pairs={{0,8},{8,0},{16,24},{24,16},{1,9},{9,1},{17,25},{25,17},{2,10},{10... | collective-permute-start | bytes 73736 | tf_op jit(solution)/shard_map/ppermute | solution.py:18
  112.1 4.9 %collective-permute-start.32 = (bf16[96,128]{1,0:T(8,128)(2,1)S(1)}, bf16[96,128]{1,0:T(8,128)(2,1)S(1)}, u32[]{:S(2)}, u32[]{:S(2)}) collective-permute-start(bf16[96,128]{1,0:T(8,128)(2,1)S(1)} %shard_map.127.refs_0_), channel_id=1, source_target_pairs={{0,16},{8,24},{16,0},{24,8},{1,17},{9,25},{17,1},{25,9},{2,18},{10... | collective-permute-start | bytes 73736 | tf_op jit(solution)/shard_map/ppermute | solution.py:18
  115.4 15.4 %collective-permute-start.23 = (bf16[48,1792]{1,0:T(8,128)(2,1)S(1)}, bf16[48,1792]{1,0:T(8,128)(2,1)S(1)}, u32[]{:S(2)}, u32[]{:S(2)}) collective-permute-start(bf16[48,1792]{1,0:T(8,128)(2,1)S(1)} %get-tuple-element.36), channel_id=1, source_target_pairs={{0,1},{1,0},{2,3},{3,2},{4,5},{5,4},{6,7},{7,6},{8,9},{9,8},{10,11... | collective-permute-start | bytes 516104 | tf_op jit(solution)/shard_map/ppermute | solution.py:18
  117.0 13.8 %collective-permute-start.24 = (bf16[48,1792]{1,0:T(8,128)(2,1)S(1)}, bf16[48,1792]{1,0:T(8,128)(2,1)S(1)}, u32[]{:S(2)}, u32[]{:S(2)}) collective-permute-start(bf16[48,1792]{1,0:T(8,128)(2,1)S(1)} %get-tuple-element.37), channel_id=1, source_target_pairs={{0,2},{1,3},{2,0},{3,1},{4,6},{5,7},{6,4},{7,5},{8,10},{9,11},{10,... | collective-permute-start | bytes 516104 | tf_op jit(solution)/shard_map/ppermute | solution.py:18
  117.3 13.5 %collective-permute-start.25 = (bf16[48,1792]{1,0:T(8,128)(2,1)S(1)}, bf16[48,1792]{1,0:T(8,128)(2,1)S(1)}, u32[]{:S(2)}, u32[]{:S(2)}) collective-permute-start(bf16[48,1792]{1,0:T(8,128)(2,1)S(1)} %get-tuple-element.38), channel_id=1, source_target_pairs={{0,3},{1,2},{2,1},{3,0},{4,7},{5,6},{6,5},{7,4},{8,11},{9,10},{10,... | collective-permute-start | bytes 516104 | tf_op jit(solution)/shard_map/ppermute | solution.py:18
  120.0 15.4 %collective-permute-start.34 = (bf16[48,1792]{1,0:T(8,128)(2,1)S(1)}, bf16[48,1792]{1,0:T(8,128)(2,1)S(1)}, u32[]{:S(2)}, u32[]{:S(2)}) collective-permute-start(bf16[48,1792]{1,0:T(8,128)(2,1)S(1)} %get-tuple-element.44), channel_id=1, source_target_pairs={{0,4},{1,5},{2,6},{3,7},{4,0},{5,1},{6,2},{7,3},{8,12},{9,13},{10,... | collective-permute-start | bytes 516104 | tf_op jit(solution)/shard_map/ppermute | solution.py:18
  122.3 16.1 %collective-permute-start.35 = (bf16[48,1792]{1,0:T(8,128)(2,1)S(1)}, bf16[48,1792]{1,0:T(8,128)(2,1)S(1)}, u32[]{:S(2)}, u32[]{:S(2)}) collective-permute-start(bf16[48,1792]{1,0:T(8,128)(2,1)S(1)} %get-tuple-element.45), channel_id=1, source_target_pairs={{0,5},{1,4},{2,7},{3,6},{4,1},{5,0},{6,3},{7,2},{8,13},{9,12},{10,... | collective-permute-start | bytes 516104 | tf_op jit(solution)/shard_map/ppermute | solution.py:18
  (15 other events, 194.1 us)
